TPU v7x, 32 devices: a whole 2x2x4 slice. The times are simulated.
32 devices in a mesh: section: 2 (over core), blk: 4 (over z), shard: 4 (over y, x).
Axes of the slice: x: 2, y: 2, z: 4, core: 2. Of those that a mesh axis runs over, the one named last changes fastest.
Arguments:
- ids: int32 [2, 4, 1024], P(None, 'shard', 'blk'), may hold values from 0 to 31999
- targets: int32 [2, 4, 1024, 2], P(None, 'shard', 'blk'), may hold values from 0 to 31999
- segments: int32 [2, 4, 1024], P(None, 'shard'), may hold values from 0 to 3, never falling along the last dimension, each value on 1 to 512 neighbouring positions
- table: float32 [32000, 768], P(('section', 'blk', 'shard')), may hold values from -0.4375 to 0.4375
- table_m: float32 [32000, 768], P(('section', 'blk', 'shard')), may hold values from -9.536743e-06 to 9.536743e-06
- table_v: float32 [32000, 768], P(('section', 'blk', 'shard')), may hold values from 2e-12 to 2e-11
- blocks: float32 [2, 1728, 64, 64], P('section', ('blk', 'shard')), may hold values from -1.1547005 to 1.1547005
- left_stats: float32 [2, 1728, 64, 64], P('section', ('blk', 'shard')), may hold values from -1.6e-07 to 2e-06, as said below
- right_stats: float32 [2, 1728, 64, 64], P('section', ('blk', 'shard')), may hold values from -1.6e-07 to 2e-06, as said below
- left_root: float32 [2, 1728, 64, 64], P('section', ('blk', 'shard')), may hold values from -24 to 180, as said below
- right_root: float32 [2, 1728, 64, 64], P('section', ('blk', 'shard')), may hold values from -24 to 180, as said below
- gains: float32 [5, 768], replicated, may hold values from 0.5 to 1.5
- gains_m: float32 [5, 768], replicated, may hold values from -0.00061035156 to 0.00061035156
- gains_v: float32 [5, 768], replicated, may hold values from 1e-10 to 1e-09
Outputs:
- loss: float32 [], replicated
- clip_norm: float32 [], replicated
- table_new: float32 [32000, 768], P(('section', 'blk', 'shard'))
- table_m_new: float32 [32000, 768], P(('section', 'blk', 'shard'))
- table_v_new: float32 [32000, 768], P(('section', 'blk', 'shard'))
- table_low: bfloat16 [32000, 768], P(('section', 'blk', 'shard'))
- blocks_new: float32 [2, 1728, 64, 64], P('section', ('blk', 'shard'))
- blocks_low: bfloat16 [2, 1728, 64, 64], P('section', ('blk', 'shard'))
- left_new: float32 [2, 1728, 64, 64], P('section', ('blk', 'shard'))
- right_new: float32 [2, 1728, 64, 64], P('section', ('blk', 'shard'))
- gains_new: float32 [5, 768], replicated
- gains_m_new: float32 [5, 768], replicated
- gains_v_new: float32 [5, 768], replicated
Inputs may be any that keep to these rules, and one draw needn't show every extreme that they name: `left_stats`: symmetric. `right_stats`: symmetric. `left_root`: symmetric. `right_root`: symmetric.
All inputs are finite; a program needn't handle non-finite values.
Results may differ from a plain program's by a relative error of at most 0.014.
Values may be sent and summed in bfloat16 or wider, within the bound.
A program may use at most 448 MiB of HBM per device.

v0:
```python
import jax
import jax.numpy as jnp
from jax import lax
from jax.sharding import PartitionSpec as P

D = 768
HEADS = 12
HEAD_DIM = 64
FF = 2048
BS = 64


norm_eps = 1e-05
rope_base = 10000.0
clip_bound = 0.08
shampoo_rate = 0.1
adam_rate = 0.02
beta_first = 0.9
beta_second = 0.95
adam_eps = 1e-08
weight_decay = 0.1
stat_decay = 0.5
second_weight = 0.3
highest = lax.Precision.HIGHEST


def shifted(block, axis, distance):
    devices = range(lax.axis_size(axis))
    route = [(i - distance, i) for i in devices if i - distance in devices]
    return lax.ppermute(block, axis, route)


def shifted_2(value, axis, steps):
    count = lax.axis_size(axis)
    pairs = [(source, (source + steps) % count) for source in range(count)]
    return lax.ppermute(value, axis, pairs)


def merged(value, axis, join):
    pieces = jax.tree.map(lambda part: lax.all_gather(part, axis), value)
    head = jax.tree.map(lambda part: part[0], pieces)
    tail = jax.tree.map(lambda part: part[1:], pieces)
    running, _ = lax.scan(lambda running, piece: (join(running, piece), None), head, tail)
    return running


def matrix_layout():
    return ((D, 3 * D), (D, D), (D, 2 * FF), (FF, D))


def assemble(pieces):
    matrices = []
    offset = 0
    for row_count, col_count in matrix_layout():
        row_blocks = row_count // BS
        col_blocks = col_count // BS
        chosen = pieces[offset : offset + row_blocks * col_blocks].reshape(
            row_blocks, col_blocks, BS, BS
        )
        matrices.append(chosen.transpose(0, 2, 1, 3).reshape(row_count, col_count))
        offset += row_blocks * col_blocks
    return matrices


def disassemble(matrices):
    block_list = []
    for matrix, shape_pair in zip(matrices, matrix_layout()):
        row_blocks = shape_pair[0] // BS
        col_blocks = shape_pair[1] // BS
        block_list.append(
            matrix.reshape(row_blocks, BS, col_blocks, BS)
            .transpose(0, 2, 1, 3)
            .reshape(row_blocks * col_blocks, BS, BS)
        )
    return jnp.concatenate(block_list, axis=0)


def rms_scale(states, gain_row):
    return (
        states * lax.rsqrt(jnp.mean(states * states, axis=-1, keepdims=True) + norm_eps) * gain_row
    )


def rms_back(states, gain_row, grad_out):
    inverse = lax.rsqrt(jnp.mean(states * states, axis=-1, keepdims=True) + norm_eps)
    weighted = grad_out * gain_row
    grad_in = inverse * weighted - states * inverse * inverse * inverse * jnp.mean(
        weighted * states, axis=-1, keepdims=True
    )
    return (grad_in, jnp.sum(grad_out * states * inverse, axis=0))


def rope_tables(positions):
    half_dim = HEAD_DIM // 2
    frequency = rope_base ** (-jnp.arange(half_dim, dtype=jnp.float32) * 2.0 / HEAD_DIM)
    angles = positions.astype(jnp.float32)[:, None] * frequency[None, :]
    cosine = jnp.concatenate([jnp.cos(angles), jnp.cos(angles)], axis=-1)[:, None, :]
    sine_table = jnp.concatenate([jnp.sin(angles), jnp.sin(angles)], axis=-1)[:, None, :]
    return (cosine, sine_table)


def rotate(values, cosine, sine_table):
    half_dim = HEAD_DIM // 2
    turned = jnp.concatenate([-values[..., half_dim:], values[..., :half_dim]], axis=-1)
    return values * cosine + turned * sine_table


def rotate_back(grads_in, cosine, sine_table):
    half_dim = HEAD_DIM // 2
    scaled = grads_in * sine_table
    turned = jnp.concatenate([scaled[..., half_dim:], -scaled[..., :half_dim]], axis=-1)
    return grads_in * cosine + turned


def to_first(values):
    return shifted(values.astype(jnp.bfloat16), "section", -1).astype(values.dtype)


def to_last(values):
    return shifted(values, "section", 1)


def layer_forward(
    states, weights, gain_first, gain_second, seg_rows, pos_rows, query_start, tok_rows
):
    w_qkv, w_out, w_gate_up, w_down = weights
    scale_factor = HEAD_DIM ** (-0.5)
    normed = rms_scale(states, gain_first).astype(jnp.bfloat16)
    projected = jnp.dot(normed, w_qkv, preferred_element_type=jnp.float32)
    query_pos = lax.dynamic_slice_in_dim(pos_rows, query_start, tok_rows)
    query_seg = lax.dynamic_slice_in_dim(seg_rows, query_start, tok_rows)
    cosine, sine_table = rope_tables(query_pos)
    queries = rotate(
        projected[:, :D].reshape(tok_rows, HEADS, HEAD_DIM), cosine, sine_table
    ).astype(jnp.bfloat16)
    key_heads = rotate(
        projected[:, D : 2 * D].reshape(tok_rows, HEADS, HEAD_DIM), cosine, sine_table
    ).astype(jnp.bfloat16)
    values = projected[:, 2 * D :].astype(jnp.bfloat16)
    initial = (
        jnp.zeros((HEADS, tok_rows), jnp.float32),
        jnp.zeros((tok_rows, HEADS, HEAD_DIM), jnp.float32),
    )
    key_piece = lax.all_gather(key_heads.reshape(tok_rows, D), "blk", axis=0, tiled=True)
    value_piece = lax.all_gather(values, "blk", axis=0, tiled=True)
    key_count = key_piece.shape[0]
    allowed = (pos_rows[None, :] <= query_pos[:, None]) & (seg_rows[None, :] == query_seg[:, None])

    def add_compute(running):
        scores = (
            jnp.einsum(
                "qhe,khe->hqk",
                queries,
                key_piece.reshape(key_count, HEADS, HEAD_DIM),
                preferred_element_type=jnp.float32,
            )
            * scale_factor
        )
        exp_scores = jnp.where(allowed[None], jnp.exp(scores), 0.0)
        added = jnp.einsum(
            "hqk,khe->qhe",
            exp_scores.astype(jnp.bfloat16),
            value_piece.reshape(key_count, HEADS, HEAD_DIM),
            preferred_element_type=jnp.float32,
        )
        return (jnp.sum(exp_scores, axis=-1), added)

    totals, weighted = lax.cond(jnp.any(allowed), add_compute, lambda running: running, initial)
    attended = (weighted / totals.T[:, :, None]).astype(jnp.bfloat16).reshape(tok_rows, D)
    mid_state = states + jnp.dot(attended, w_out, preferred_element_type=jnp.float32)
    normed_mid = rms_scale(mid_state, gain_second).astype(jnp.bfloat16)
    gate_up = jnp.dot(normed_mid, w_gate_up, preferred_element_type=jnp.float32)
    gate_part = gate_up[:, :FF]
    up_part = gate_up[:, FF:]
    hidden = (jax.nn.silu(gate_part) * up_part).astype(jnp.bfloat16)
    output = mid_state + jnp.dot(hidden, w_down, preferred_element_type=jnp.float32)
    layer_cache = (
        states,
        normed,
        queries,
        key_heads,
        values,
        totals,
        weighted,
        attended,
        mid_state,
        normed_mid,
        gate_part,
        up_part,
        hidden,
        query_pos,
        query_seg,
        cosine,
        sine_table,
        seg_rows,
    )
    return (output, layer_cache)


def layer_backward(
    layer_cache,
    grad_out,
    weights,
    gain_first,
    gain_second,
    pos_rows,
    cycle_index,
    cycle_size,
    tok_rows,
):
    (
        states,
        normed,
        queries,
        key_heads,
        values,
        totals,
        weighted,
        attended,
        mid_state,
        normed_mid,
        gate_part,
        up_part,
        hidden,
        query_pos,
        query_seg,
        cosine,
        sine_table,
        seg_rows,
    ) = layer_cache
    w_qkv, w_out, w_gate_up, w_down = weights
    scale_factor = HEAD_DIM ** (-0.5)
    grad_low = grad_out.astype(jnp.bfloat16)
    grad_w_down = jnp.einsum("rf,rd->fd", hidden, grad_low, preferred_element_type=jnp.float32)
    grad_hidden = jnp.einsum("rd,fd->rf", grad_low, w_down, preferred_element_type=jnp.float32)
    gate_sig = jax.nn.sigmoid(gate_part)
    grad_gate = grad_hidden * up_part * gate_sig * (1.0 + gate_part * (1.0 - gate_sig))
    grad_up = grad_hidden * gate_part * gate_sig
    grad_gate_up = jnp.concatenate([grad_gate, grad_up], axis=-1).astype(jnp.bfloat16)
    grad_w_gate_up = jnp.einsum(
        "rd,rf->df", normed_mid, grad_gate_up, preferred_element_type=jnp.float32
    )
    grad_normed_mid = jnp.einsum(
        "rf,df->rd", grad_gate_up, w_gate_up, preferred_element_type=jnp.float32
    )
    grad_mid_norm, grad_gain_second = rms_back(mid_state, gain_second, grad_normed_mid)
    grad_mid = grad_out + grad_mid_norm
    grad_att = grad_mid.astype(jnp.bfloat16)
    grad_w_out = jnp.einsum("rd,re->de", attended, grad_att, preferred_element_type=jnp.float32)
    grad_attended = jnp.einsum(
        "re,de->rd", grad_att, w_out, preferred_element_type=jnp.float32
    ).reshape(tok_rows, HEADS, HEAD_DIM)
    inverse = 1.0 / totals.T
    grad_weighted = (grad_attended * inverse[:, :, None]).astype(jnp.bfloat16)
    grad_totals = (-jnp.sum(grad_attended * weighted, axis=-1) * inverse * inverse).T

    def visit_block(step_index, key_piece, value_piece, grad_keys, grad_values, grad_queries):
        owner_index = (cycle_index + step_index) % cycle_size
        key_pos = lax.dynamic_slice_in_dim(pos_rows, owner_index * tok_rows, tok_rows)
        key_seg = lax.dynamic_slice_in_dim(seg_rows, owner_index * tok_rows, tok_rows)
        allowed = (key_pos[None, :] <= query_pos[:, None]) & (
            key_seg[None, :] == query_seg[:, None]
        )

        def visit_compute(grad_triple):
            key_low = key_piece.reshape(tok_rows, HEADS, HEAD_DIM)
            value_low = value_piece.reshape(tok_rows, HEADS, HEAD_DIM)
            scores = (
                jnp.einsum("qhe,khe->hqk", queries, key_low, preferred_element_type=jnp.float32)
                * scale_factor
            )
            exp_scores = jnp.where(allowed[None], jnp.exp(scores), 0.0)
            grad_probs = jnp.einsum(
                "qhe,khe->hqk", grad_weighted, value_low, preferred_element_type=jnp.float32
            )
            grad_scores = (exp_scores * (grad_probs + grad_totals[:, :, None])).astype(jnp.bfloat16)
            new_queries = (
                grad_triple[0]
                + jnp.einsum(
                    "hqk,khe->qhe", grad_scores, key_low, preferred_element_type=jnp.float32
                )
                * scale_factor
            )
            new_keys = grad_triple[1] + (
                jnp.einsum("hqk,qhe->khe", grad_scores, queries, preferred_element_type=jnp.float32)
                * scale_factor
            ).reshape(tok_rows, D)
            new_values = grad_triple[2] + jnp.einsum(
                "hqk,qhe->khe",
                exp_scores.astype(jnp.bfloat16),
                grad_weighted,
                preferred_element_type=jnp.float32,
            ).reshape(tok_rows, D)
            return (new_queries, new_keys, new_values)

        return lax.cond(
            jnp.any(allowed),
            visit_compute,
            lambda grad_triple: grad_triple,
            (grad_queries, grad_keys, grad_values),
        )

    def cycle_step(step_index, cycle_state):
        key_piece, value_piece, grad_keys, grad_values, grad_queries = cycle_state
        grad_queries, grad_keys, grad_values = visit_block(
            step_index, key_piece, value_piece, grad_keys, grad_values, grad_queries
        )
        key_piece, value_piece = shifted_2((key_piece, value_piece), "blk", -1)
        grad_keys, grad_values = (
            shifted_2(grad_keys.astype(jnp.bfloat16), "blk", -1).astype(grad_keys.dtype),
            shifted_2(grad_values.astype(jnp.bfloat16), "blk", -1).astype(grad_values.dtype),
        )
        return (key_piece, value_piece, grad_keys, grad_values, grad_queries)

    zeros_flat = jnp.zeros((tok_rows, D), jnp.float32)
    cycle_state = (
        key_heads.reshape(tok_rows, D),
        values,
        zeros_flat,
        zeros_flat,
        jnp.zeros((tok_rows, HEADS, HEAD_DIM), jnp.float32),
    )
    key_piece, value_piece, grad_keys, grad_values, grad_queries = lax.fori_loop(
        0, cycle_size - 1, cycle_step, cycle_state
    )
    grad_queries, grad_keys, grad_values = visit_block(
        cycle_size - 1, key_piece, value_piece, grad_keys, grad_values, grad_queries
    )
    grad_keys, grad_values = (
        shifted_2(grad_keys.astype(jnp.bfloat16), "blk", -1).astype(grad_keys.dtype),
        shifted_2(grad_values.astype(jnp.bfloat16), "blk", -1).astype(grad_values.dtype),
    )
    grad_query_pre = rotate_back(grad_queries, cosine, sine_table).reshape(tok_rows, D)
    grad_key_pre = rotate_back(
        grad_keys.reshape(tok_rows, HEADS, HEAD_DIM), cosine, sine_table
    ).reshape(tok_rows, D)
    grad_projected = jnp.concatenate([grad_query_pre, grad_key_pre, grad_values], axis=-1).astype(
        jnp.bfloat16
    )
    grad_w_qkv = jnp.einsum("rd,rf->df", normed, grad_projected, preferred_element_type=jnp.float32)
    grad_normed = jnp.einsum("rf,df->rd", grad_projected, w_qkv, preferred_element_type=jnp.float32)
    grad_state_norm, grad_gain_first = rms_back(states, gain_first, grad_normed)
    return (
        grad_mid + grad_state_norm,
        (grad_w_qkv, grad_w_out, grad_w_gate_up, grad_w_down),
        grad_gain_first,
        grad_gain_second,
    )


def adam_step(weight, first, second, grad_in, decay):
    first_new = beta_first * first + (1.0 - beta_first) * grad_in
    second_new = beta_second * second + (1.0 - beta_second) * grad_in * grad_in
    weight_new = weight - adam_rate * (
        first_new / (jnp.sqrt(second_new) + adam_eps) + decay * weight
    )
    return (weight_new, first_new, second_new)


def on_device(
    ids,
    targets,
    segments,
    table,
    table_m,
    table_v,
    blocks,
    left_stats,
    right_stats,
    left_root,
    right_root,
    gains,
    gains_m,
    gains_v,
):
    cycle_size = lax.axis_size("blk")
    section_index = lax.axis_index("section")
    cycle_index = lax.axis_index("blk")
    last_section = lax.axis_size("section") - 1
    micro_count = ids.shape[0]
    tok_rows = ids.shape[2]
    seq_len = segments.shape[2]
    table_half, block_all = (
        lax.all_gather(table.astype(jnp.bfloat16), ("blk", "shard"), axis=0, tiled=True),
        lax.all_gather(blocks[0].astype(jnp.bfloat16), ("blk", "shard"), axis=0, tiled=True),
    )
    weights = assemble(block_all)
    gain_first = lax.dynamic_index_in_dim(gains, 2 * section_index, 0, keepdims=False)
    gain_second = lax.dynamic_index_in_dim(gains, 2 * section_index + 1, 0, keepdims=False)
    final_gain = gains[gains.shape[0] - 1]
    token_ids = ids[:, 0, :]
    token_targets = targets[:, 0, :, :]
    seq_segments = segments[:, 0, :]
    pos_rows = jnp.arange(seq_len, dtype=jnp.int32)
    half_vocab = table_half.shape[0]
    local_ids = token_ids - section_index * half_vocab
    inside = (local_ids >= 0) & (local_ids < half_vocab)
    safe_ids = jnp.clip(local_ids, 0, half_vocab - 1)
    looked = jnp.where(
        inside[..., None], jnp.take(table_half, safe_ids, axis=0).astype(jnp.float32), 0.0
    )
    embedded = looked + to_first(looked)
    zeros_rows = jnp.zeros((tok_rows, D), jnp.float32)
    received = zeros_rows
    caches = []
    outputs = []
    for period in range(micro_count + 1):
        first_in = embedded[period] if period < micro_count else zeros_rows
        layer_in = jnp.where(section_index == 0, first_in, received)
        batch_index = jnp.clip(period - section_index, 0, micro_count - 1)
        segment_now = lax.dynamic_index_in_dim(seq_segments, batch_index, 0, keepdims=False)
        layer_out, layer_cache = layer_forward(
            layer_in,
            weights,
            gain_first,
            gain_second,
            segment_now,
            pos_rows,
            cycle_index * tok_rows,
            tok_rows,
        )
        caches.append(layer_cache)
        outputs.append(layer_out)
        if period < micro_count:
            received = to_last(layer_out)
    total_rows = micro_count * tok_rows
    stacked = jnp.stack(outputs[1:], axis=0)
    final_states = jnp.where(section_index == last_section, stacked, to_first(stacked)).reshape(
        total_rows, D
    )
    normed_final = rms_scale(final_states, final_gain).astype(jnp.bfloat16)
    block_rows = min(512, total_rows)
    block_total = total_rows // block_rows
    normed_blocks = normed_final.reshape(block_total, block_rows, D)
    target_blocks = (token_targets - section_index * half_vocab).reshape(block_total, block_rows, 2)
    columns = jnp.arange(half_vocab, dtype=jnp.int32)
    inv_count = 1.0 / (micro_count * lax.axis_size("shard") * seq_len)

    def vocab_logits(rows_in):
        return jnp.einsum("rd,vd->rv", rows_in, table_half, preferred_element_type=jnp.float32)

    def row_stats(logits, targets_local):
        row_top = jnp.max(logits, axis=-1)
        row_total = jnp.sum(jnp.exp(logits - row_top[:, None]), axis=-1)
        valid = (targets_local >= 0) & (targets_local < half_vocab)
        picked = jnp.take_along_axis(logits, jnp.clip(targets_local, 0, half_vocab - 1), axis=1)
        return (row_top, row_total, jnp.where(valid, picked, 0.0))

    def head_step(table_grad, logits, rows_in, targets_local, log_total):
        softmax_rows = jnp.exp(logits - log_total[:, None])
        target_hits = (columns[None, :] == targets_local[:, 0:1]).astype(
            jnp.float32
        ) + second_weight * (columns[None, :] == targets_local[:, 1:2]).astype(jnp.float32)
        grad_logits = (((1.0 + second_weight) * softmax_rows - target_hits) * inv_count).astype(
            jnp.bfloat16
        )
        grad_rows = jnp.einsum(
            "rv,vd->rd", grad_logits, table_half, preferred_element_type=jnp.float32
        )
        return (
            table_grad
            + jnp.einsum("rv,rd->vd", grad_logits, rows_in, preferred_element_type=jnp.float32),
            grad_rows,
        )

    table_zero = jnp.zeros((half_vocab, D), jnp.float32)

    def first_pass(pair_in):
        logits = vocab_logits(pair_in[0])
        return (logits,) + row_stats(logits, pair_in[1])

    kept_logits, row_top, row_total, row_picks = lax.map(first_pass, (normed_blocks, target_blocks))

    def combine(first_set, second_set):
        larger = jnp.maximum(first_set[0], second_set[0])
        summed = first_set[1] * jnp.exp(first_set[0] - larger) + second_set[1] * jnp.exp(
            second_set[0] - larger
        )
        return (larger, summed)

    row_top, row_total = merged((row_top, row_total), "section", combine)
    log_total = row_top + jnp.log(row_total)

    def back_pass(table_grad, quad_in):
        return head_step(table_grad, quad_in[0], quad_in[1], quad_in[2], quad_in[3])

    table_grad, grad_rows = lax.scan(
        back_pass, table_zero, (kept_logits, normed_blocks, target_blocks, log_total)
    )
    spread_part = jnp.where(
        section_index == last_section, (1.0 + second_weight) * jnp.sum(log_total), 0.0
    )
    loss_part = (
        spread_part - jnp.sum(row_picks[..., 0]) - second_weight * jnp.sum(row_picks[..., 1])
    )
    grad_flat = grad_rows.reshape(total_rows, D)
    grad_final = grad_flat + to_last(grad_flat)
    grad_state_flat, grad_gain_final = rms_back(final_states, final_gain, grad_final)
    grad_states = grad_state_flat.reshape(micro_count, tok_rows, D)
    received = zeros_rows
    grad_inputs = []
    weight_grads = None
    gain_grad_first = jnp.zeros((D,), jnp.float32)
    gain_grad_second = jnp.zeros((D,), jnp.float32)
    for period in range(micro_count + 1):
        own_grad = grad_states[micro_count - 1 - period] if period < micro_count else zeros_rows
        incoming = jnp.where(section_index == last_section, own_grad, received)
        grad_in, grads_now, grad_gain_a, grad_gain_b = layer_backward(
            caches[micro_count - period],
            incoming,
            weights,
            gain_first,
            gain_second,
            pos_rows,
            cycle_index,
            cycle_size,
            tok_rows,
        )
        weight_grads = (
            grads_now if weight_grads is None else jax.tree.map(jnp.add, weight_grads, grads_now)
        )
        gain_grad_first = gain_grad_first + grad_gain_a
        gain_grad_second = gain_grad_second + grad_gain_b
        if period >= 1:
            grad_inputs.append(grad_in)
        if period < micro_count:
            received = to_first(grad_in)
    grad_first = jnp.stack(grad_inputs[::-1], axis=0)
    grad_embed = jnp.where(section_index == 0, grad_first, to_last(grad_first))
    table_grad = table_grad.at[safe_ids].add(jnp.where(inside[..., None], grad_embed, 0.0))
    block_grads = disassemble(list(weight_grads))
    table_own, block_own = (
        lax.psum_scatter(table_grad, ("blk", "shard"), scatter_dimension=0, tiled=True),
        lax.psum_scatter(block_grads, ("blk", "shard"), scatter_dimension=0, tiled=True),
    )
    row_index = jnp.arange(gains.shape[0], dtype=jnp.int32)[:, None]
    gains_part = jnp.where(row_index == 2 * section_index, gain_grad_first[None, :], 0.0)
    gains_part = gains_part + jnp.where(
        row_index == 2 * section_index + 1, gain_grad_second[None, :], 0.0
    )
    gains_part = gains_part + jnp.where(
        (row_index == gains.shape[0] - 1) & (section_index == last_section),
        grad_gain_final[None, :],
        0.0,
    )
    square_sum = jnp.sum(table_own * table_own) + jnp.sum(block_own * block_own)
    square_total, gain_grad, loss_total = lax.psum(
        (square_sum, gains_part, loss_part), ("section", "blk", "shard")
    )
    clip_norm = jnp.sqrt(square_total + jnp.sum(gain_grad * gain_grad))
    factor = clip_bound / jnp.maximum(clip_norm, clip_bound)
    loss = loss_total * inv_count
    grad_blocks = block_own * factor
    left_new = stat_decay * left_stats[0] + (1.0 - stat_decay) * jnp.einsum(
        "bij,bkj->bik", grad_blocks, grad_blocks, precision=highest
    )
    right_new = stat_decay * right_stats[0] + (1.0 - stat_decay) * jnp.einsum(
        "bji,bjk->bik", grad_blocks, grad_blocks, precision=highest
    )
    direction = jnp.einsum(
        "bij,bjk->bik",
        left_root[0],
        jnp.einsum("bij,bjk->bik", grad_blocks, right_root[0], precision=highest),
        precision=highest,
    )
    blocks_new = blocks[0] - shampoo_rate * direction
    table_new, table_m_new, table_v_new = adam_step(
        table, table_m, table_v, table_own * factor, weight_decay
    )
    gains_new, gains_m_new, gains_v_new = adam_step(
        gains, gains_m, gains_v, gain_grad * factor, 0.0
    )
    return (
        loss,
        clip_norm,
        table_new,
        table_m_new,
        table_v_new,
        table_new.astype(jnp.bfloat16),
        blocks_new[None],
        blocks_new[None].astype(jnp.bfloat16),
        left_new[None],
        right_new[None],
        gains_new,
        gains_m_new,
        gains_v_new,
    )


def solution(mesh):
    placed = (
        P(None, "shard", "blk"),
        P(None, "shard", "blk", None),
        P(None, "shard", None),
        P(("section", "blk", "shard"), None),
        P(("section", "blk", "shard"), None),
        P(("section", "blk", "shard"), None),
        P("section", ("blk", "shard"), None, None),
        P("section", ("blk", "shard"), None, None),
        P("section", ("blk", "shard"), None, None),
        P("section", ("blk", "shard"), None, None),
        P("section", ("blk", "shard"), None, None),
        P(),
        P(),
        P(),
    )
    return jax.shard_map(
        on_device,
        mesh=mesh,
        in_specs=placed,
        out_specs=(
            P(),
            P(),
            P(("section", "blk", "shard"), None),
            P(("section", "blk", "shard"), None),
            P(("section", "blk", "shard"), None),
            P(("section", "blk", "shard"), None),
            P("section", ("blk", "shard"), None, None),
            P("section", ("blk", "shard"), None, None),
            P("section", ("blk", "shard"), None, None),
            P("section", ("blk", "shard"), None, None),
            P(),
            P(),
            P(),
        ),
        check_vma=False,
    )
```

profile of v0, /device:TPU:0, one launch (start us, length us, event | category | flops | bytes accessed | tf_op | source)
XLA Modules:
  0.0 3473.6 jit_solution(5586249890609389496)
XLA Ops:
  21.3 257.6 %all-gather.13.cloned.1.call-done = bf16[16000,768]{1,0:T(8,128)(2,1)} async-done(((bf16[1000,768]{1,0:T(8,128)(2,1)}), bf16[16000,768]{1,0:T(8,128)(2,1)}) %all-gather.13.cloned.1.call-update) | async-done | bytes 24576016 | tf_op jit(solution)/shard_map/all_gather | solution.py:384
  278.9 13.5 gather_fusion
  298.8 281.9 %all-gather.15.cloned.1.call-done = bf16[1728,64,64]{2,1,0:T(8,128)(2,1)} async-done(((bf16[108,64,64]{2,1,0:T(8,128)(2,1)}), bf16[1728,64,64]{2,1,0:T(8,128)(2,1)}) %all-gather.15.cloned.1.call-update) | async-done | bytes 14155792 | tf_op jit(solution)/shard_map/all_gather | solution.py:385
  650.5 17.1 reshape.800
  699.3 23.2 conditional.9
  761.1 27.7 all-gather.21.cloned.1.call-done
  788.8 37.3 %all-gather.23.cloned.1.call-done = bf16[1024,768]{1,0:T(8,128)(2,1)} async-done(((bf16[256,768]{1,0:T(8,128)(2,1)}), bf16[1024,768]{1,0:T(8,128)(2,1)}) %all-gather.23.cloned.1.call-update) | async-done | bytes 1572880 | tf_op jit(solution)/shard_map/all_gather | solution.py:145
  826.2 23.2 conditional.10
  882.1 33.0 all-gather.25.cloned.1.call-done
  915.1 37.5 %all-gather.27.cloned.1.call-done = bf16[1024,768]{1,0:T(8,128)(2,1)} async-done(((bf16[256,768]{1,0:T(8,128)(2,1)}), bf16[1024,768]{1,0:T(8,128)(2,1)}) %all-gather.27.cloned.1.call-update) | async-done | bytes 1572880 | tf_op jit(solution)/shard_map/all_gather | solution.py:145
  952.6 19.3 conditional.11
  991.0 26.1 fusion.237
  1017.1 16.2 exponential_reduce_fusion
  1037.8 14.5 multiply_convert_fusion.6
  1052.3 22.3 fusion.248
  1121.6 127.4 %while.89 = (s32[]{:T(128)}, bf16[256,768]{0,1:T(8,128)(2,1)S(1)}, bf16[256,768]{0,1:T(8,128)(2,1)S(1)}, f32[256,768]{0,1:T(8,128)}, f32[256,768]{0,1:T(8,128)},...) while((s32[]{:T(128)}, bf16[256,768]{0,1:T(8,128)(2,1)S(1)}, ...), condition=%wide.region_33.34_spmd.clone, body=%wide.region_29.33_spmd.clone.sunk | while | flops 512032800 | bytes 42603240 | solution.py:323
  1301.4 136.5 %while.90 = (s32[]{:T(128)}, bf16[256,768]{0,1:T(8,128)(2,1)S(1)}, bf16[256,768]{0,1:T(8,128)(2,1)S(1)}, f32[256,768]{0,1:T(8,128)}, f32[256,768]{0,1:T(8,128)},...) while((s32[]{:T(128)}, bf16[256,768]{0,1:T(8,128)(2,1)S(1)}, ...), condition=%wide.region_44.45_spmd.clone, body=%wide.region_40.44_spmd.clone.sunk | while | flops 512032800 | bytes 41030348 | solution.py:323
  1486.9 137.6 %while.91 = (s32[]{:T(128)}, bf16[256,768]{0,1:T(8,128)(2,1)S(1)}, bf16[256,768]{0,1:T(8,128)(2,1)S(1)}, f32[256,768]{0,1:T(8,128)}, f32[256,768]{0,1:T(8,128)},...) while((s32[]{:T(128)}, bf16[256,768]{0,1:T(8,128)(2,1)S(1)}, ...), condition=%wide.region_55.56_spmd.clone, body=%wide.region_51.55_spmd.clone.sunk | while | flops 512032800 | bytes 41030348 | solution.py:323
  1661.8 14.9 add_add_fusion
  1676.7 20.4 reshape.820
  1697.1 31.1 copy.432
  1728.3 25.6 reshape.821
  1780.2 12.7 copy.434
  1817.3 12.5 reshape.816
  1829.7 12.9 copy.430
  1854.7 34.4 concatenate.102
  1899.2 27.9 fusion.247
  1927.8 36.7 %scatter_fusion = f32[16000,768]{1,0:T(8,128)} fusion(f32[16000,768]{1,0:T(8,128)} %fusion.247, s32[512]{0:T(512)S(1)} %bitcast.567, f32[512,768]{1,0:T(8,128)S(1)} %bitcast.511), kind=kCustom, calls=%fused_computation.2 | custom fusion | flops 393216 | bytes 4720640 | tf_op jit(solution)/shard_map/scatter-add | solution.py:530
  1981.0 15.4 gather_fusion.1
  2000.1 650.8 %all-reduce.5.cloned.1.call-done = f32[1728,64,64]{0,2,1:T(8,128)} async-done(((f32[1728,64,64]{0,2,1:T(8,128)}), f32[1728,64,64]{0,2,1:T(8,128)}) %all-reduce.5.cloned.1.call-update) | async-done | bytes 28311568
  2654.4 684.3 %reduce-scatter.5.cloned.1.call-done = f32[1000,768]{1,0:T(8,128)} async-done(((f32[16000,768]{1,0:T(8,128)}), f32[1000,768]{1,0:T(8,128)}) %reduce-scatter.5.cloned.1.call-update) | async-done | bytes 3072016
  3347.3 39.9 %all-reduce.2 = (f32[]{:T(128)}, f32[]{:T(128)}, f32[5,768]{1,0:T(8,128)S(1)}) all-reduce(f32[]{:T(128)S(6)} %sub.181, f32[]{:T(128)S(6)} %add.756, f32[5,768]{1,0:T(8,128)S(1)} %select_add_fusion), channel_id=1, replica_groups=mesh['section'=2,'blk'=4,'shard'=4] {'section','blk','shard'}, use_global_device_ids=true, to_apply=%region_24.25 | all-reduce | flops 3842 | bytes 30736 | tf_op jit(solution)/shard_map/psum | solution.py:547
  (866 shorter events, 1048.8 us)
Async XLA Ops:
  7.2 271.7 %all-gather.13.cloned.1.call-start = ((), (), s32[]{:S(2)}) async-start(), calls=%async_computation.1 | async-start | bytes 26112000 | tf_op jit(solution)/shard_map/all_gather | solution.py:384
  10.4 570.3 %all-gather.15.cloned.1.call-start = ((), (), s32[]{:S(2)}) async-start(), calls=%async_computation.2 | async-start | bytes 30081024 | tf_op jit(solution)/shard_map/all_gather | solution.py:385
  20.6 678.7 %all-gather.17.cloned.1.call-start = ((), (), s32[]{:S(2)}) async-start(), calls=%async_computation.3 | async-start | bytes 1966080 | tf_op jit(solution)/shard_map/all_gather | solution.py:144
  293.6 308.3 %collective-permute-start.12 = (bf16[2,256,768]{2,1,0:T(8,128)(2,1)}, bf16[2,256,768]{2,1,0:T(8,128)(2,1)}, u32[]{:S(2)}, u32[]{:S(2)}) collective-permute-start(bf16[2,256,768]{2,1,0:T(8,128)(2,1)} %fusion.104), channel_id=1, source_target_pairs={{16,0},{17,1},{18,2},{19,3},{20,4},{21,5},{22,6},{23,7},{24,8},{25... | collective-permute-start | bytes 2359304 | tf_op jit(solution)/shard_map/ppermute | solution.py:30
  619.2 80.1 %all-gather.19.cloned.1.call-start = ((), (), s32[]{:S(2)}) async-start(), calls=%async_computation.4 | async-start | bytes 1966080 | tf_op jit(solution)/shard_map/all_gather | solution.py:145
  621.2 167.6 %all-gather.21.cloned.1.call-start = ((), (), s32[]{:S(2)}) async-start(), calls=%async_computation.5 | async-start | bytes 1966080 | tf_op jit(solution)/shard_map/all_gather | solution.py:144
  752.8 73.4 %all-gather.23.cloned.1.call-start = ((), (), s32[]{:S(2)}) async-start(), calls=%async_computation.6 | async-start | bytes 1966080 | tf_op jit(solution)/shard_map/all_gather | solution.py:145
  754.8 160.3 %all-gather.25.cloned.1.call-start = ((), (), s32[]{:S(2)}) async-start(), calls=%async_computation.7 | async-start | bytes 1966080 | tf_op jit(solution)/shard_map/all_gather | solution.py:144
  878.4 74.1 %all-gather.27.cloned.1.call-start = ((), (), s32[]{:S(2)}) async-start(), calls=%async_computation.8 | async-start | bytes 1966080 | tf_op jit(solution)/shard_map/all_gather | solution.py:145
  879.3 1771.6 %all-reduce.5.cloned.1.call-start = ((), (), s32[]{:S(2)}) async-start(), calls=%async_computation.9 | async-start | bytes 58720256
  1135.1 31.2 collective-permute-start.1
  1176.1 26.5 collective-permute-start
  1176.5 31.0 collective-permute-start.1
  1218.4 26.3 collective-permute-start
  1218.5 30.5 collective-permute-start.1
  1316.3 26.5 collective-permute-start.4
  1316.4 34.4 collective-permute-start.5
  1361.2 26.5 collective-permute-start.4
  1361.2 33.6 collective-permute-start.5
  1405.2 26.5 collective-permute-start.4
  1405.2 32.7 collective-permute-start.5
  1439.6 27.0 collective-permute-start.21
  1501.8 26.4 collective-permute-start.8
  1501.9 34.8 %collective-permute-start.9 = (bf16[256,768]{0,1:T(8,128)(2,1)S(1)}, bf16[256,768]{0,1:T(8,128)(2,1)S(1)}, u32[]{:S(2)}, u32[]{:S(2)}) collective-permute-start(bf16[256,768]{0,1:T(8,128)(2,1)S(1)} %copy.553), channel_id=1, source_target_pairs={{0,12},{4,0},{8,4},{12,8},{1,13},{5,1},{9,5},{13,9},{2,14},{6,2},{... | collective-permute-start | bytes 1179656 | tf_op jit(solution)/shard_map/while/body/eval_jaxpr/ppermute | solution.py:36
  1547.0 26.5 collective-permute-start.8
  1547.1 34.0 collective-permute-start.9
  1591.3 26.5 collective-permute-start.8
  1591.4 33.1 collective-permute-start.9
  1626.6 180.7 %collective-permute-start.24 = (bf16[256,768]{0,1:T(8,128)(2,1)}, bf16[256,768]{0,1:T(8,128)(2,1)}, u32[]{:S(2)}, u32[]{:S(2)}) collective-permute-start(bf16[256,768]{0,1:T(8,128)(2,1)} %convert_element_type.468), channel_id=1, source_target_pairs={{0,12},{4,0},{8,4},{12,8},{1,13},{5,1},{9,5},{13,9},{2,14},{6,2},{... | collective-permute-start | bytes 1179656 | tf_op jit(solution)/shard_map/ppermute | solution.py:36
  1639.9 164.5 %collective-permute-start.23 = (bf16[256,768]{0,1:T(8,128)(2,1)}, bf16[256,768]{0,1:T(8,128)(2,1)}, u32[]{:S(2)}, u32[]{:S(2)}) collective-permute-start(bf16[256,768]{0,1:T(8,128)(2,1)} %convert_element_type.466), channel_id=1, source_target_pairs={{0,12},{4,0},{8,4},{12,8},{1,13},{5,1},{9,5},{13,9},{2,14},{6,2},{... | collective-permute-start | bytes 1179656 | tf_op jit(solution)/shard_map/ppermute | solution.py:36
  1889.1 1449.5 %reduce-scatter.5.cloned.1.call-start = ((), (), s32[]{:S(2)}) async-start(), calls=%async_computation.10 | async-start | bytes 52224000
  1896.7 30.4 collective-permute-start.25
  (215 other events, 5748.9 us)
Sparse Core Ops, SparseCore 0:
  11.4 267.5 all-gather.12
  282.3 298.3 all-gather.14
  619.3 35.1 all-gather.16
  656.0 35.8 all-gather.18
  752.9 35.8 all-gather.20
  790.2 35.8 all-gather.22
  878.6 36.4 all-gather.24
  916.6 35.8 all-gather.26
  1889.2 761.6 all-reduce.4
  2657.1 681.5 reduce-scatter.4
where the time goes:
time: 3480 us; the launch traced here: 3470 us
  waiting for transfers between devices  2290 us (66%)
  local copies, waits for them, and re-layouts  490 us (14%)
  matrix products  291 us (8%)
  other arithmetic  224 us (6%)
  starting transfers between devices  94.1 us (3%)
  blocking collectives  43.8 us (1%)
    unnamed x12, waiting for transfers between devices  1340 us
    all_gather x1, waiting for transfers between devices, on_device(): lax.all_gather(blocks[0].astype(jnp.bfloat16), ('blk', 'shard'), axis=0,...  282 us
    ppermute x42, waiting for transfers between devices, shifted_2(): return lax.ppermute(value, axis, pairs)  277 us
    all_gather x1, waiting for transfers between devices, on_device(): lax.all_gather(table.astype(jnp.bfloat16), ('blk', 'shard'), axis=0, tile...  258 us
    reshape x5, local copies, waits for them, and re-layouts, disassemble(): matrix.reshape(row_blocks, BS, col_blocks, BS).transpose(0, 2, 1, 3)  80.7 us
    ppermute x42, starting transfers between devices, shifted_2(): return lax.ppermute(value, axis, pairs)  77.8 us
    all_gather x3, waiting for transfers between devices, layer_forward(): value_piece = lax.all_gather(values, 'blk', axis=0, tiled=True)  74.8 us
  transfers between devices with their start and end apart: 60, of which 49 were waited for; matrix products, arithmetic and copies ran while one was open for 14% of the time, Pallas kernels for 0%

commit v1 on v0

v1 whole, which is shorter than its diff:
```python
import functools

import jax
import jax.numpy as jnp
from jax import lax
from jax.experimental import pallas as pl
from jax.experimental.pallas import tpu as pltpu
from jax.sharding import PartitionSpec as P

D = 768
HEADS = 12
HEAD_DIM = 64
FF = 2048
BS = 64
QUAD = 256

norm_eps = 1e-05
rope_base = 10000.0
clip_bound = 0.08
shampoo_rate = 0.1
adam_rate = 0.02
beta_first = 0.9
beta_second = 0.95
adam_eps = 1e-08
weight_decay = 0.1
stat_decay = 0.5
second_weight = 0.3
highest = lax.Precision.HIGHEST
MESH = pl.DeviceIdType.MESH
ORDER = ("blk", "shard", "section")
VMEM_MAX = 62 * 1024 * 1024
f32 = jnp.float32
bf16 = jnp.bfloat16


def remote(src,dst,ssem,rsem,dev):
    return pltpu.make_async_remote_copy(src_ref=src,dst_ref=dst,send_sem=ssem,recv_sem=rsem,device_id=dev,device_id_type=MESH)

def split_rows(R, step, frac):
    a=int(round(R*frac/step))*step
    return min(max(a,0),R)

def ag_kernel(B,H,parts,by_section,x_ref,o_ref,ssem,rsem,lsem):
    s=lax.axis_index("section"); b=lax.axis_index("blk"); h=lax.axis_index("shard")
    x1=h^1; y1=h^2; xy=h^3
    part=(1-s,b,h)
    xn=(s,b,x1); yn=(s,b,y1); lf=(s,b-1,h); rt=(s,b+1,h)
    has_l=b>0; has_r=b<B-1
    bar=pltpu.get_barrier_semaphore()
    for t in (part,xn,yn):
        pl.semaphore_signal(bar,inc=1,device_id=t,device_id_type=MESH)
    @pl.when(has_l)
    def _(): pl.semaphore_signal(bar,inc=1,device_id=lf,device_id_type=MESH)
    @pl.when(has_r)
    def _(): pl.semaphore_signal(bar,inc=1,device_id=rt,device_id_type=MESH)
    def slot(bb,hh,ss):
        return (ss*B+bb)*H+hh if by_section else (bb*H+hh)*2+ss
    def dst(p,bb,hh,ss): return o_ref.at[slot(bb,hh,ss),pl.ds(parts[p][0],parts[p][1])]
    def rs(p,bb,hh,ss): return rsem.at[p,slot(bb,hh,ss)]
    local=pltpu.make_async_copy(x_ref,o_ref.at[slot(b,h,s)],lsem.at[0])
    local.start()
    pl.semaphore_wait(bar,3+has_l.astype(jnp.int32)+has_r.astype(jnp.int32))
    pend=[]
    def send(p,bb,hh,ss,dev,cond=None,own=False,kind=0):
        i=len(pend)
        src=x_ref.at[pl.ds(parts[p][0],parts[p][1])] if own else dst(p,bb,hh,ss)
        cp=remote(src,dst(p,bb,hh,ss),ssem.at[i],rs(p,bb,hh,ss),dev)
        pend.append((cond,cp))
        if cond is None: cp.start()
        else:
            @pl.when(cond)
            def _(): cp.start()
    def wait(p,bb,hh,ss):
        remote(dst(p,bb,hh,ss),dst(p,bb,hh,ss),ssem.at[0],rs(p,bb,hh,ss),part).wait_recv()
    def andc(a,c):
        return c if a is None else jnp.logical_and(a,c)
    def on_arrive(cond,fn):
        if cond is None: fn()
        else: pl.when(cond)(fn)
    def group(cond,waits,sends):
        i0=len(pend)
        cps=[]
        for k,(p,bb,hh,dev,c,own) in enumerate(sends):
            src=x_ref.at[pl.ds(parts[p][0],parts[p][1])] if own else dst(p,bb,hh,s)
            cp=remote(src,dst(p,bb,hh,s),ssem.at[i0+k],rs(p,bb,hh,s),dev)
            cps.append((c,cp))
        def run():
            for (p,bb,hh) in waits: wait(p,bb,hh,s)
            for c,cp in cps:
                if c is None: cp.start()
                else: pl.when(c)(cp.start)
        on_arrive(cond,run)
        for c,cp in cps:
            cc=cond if c is None else (c if cond is None else jnp.logical_and(cond,c))
            pend.append((cc,cp))
    two=len(parts)>1
    group(None,[],[(0,b,h,rt,has_r,True),(0,b,h,lf,has_l,True),(0,b,h,xn,None,True),(0,b,h,yn,None,True)])
    if two:
        group(None,[],[(1,b,h,yn,None,True),(1,b,h,rt,has_r,True),(1,b,h,lf,has_l,True),(1,b,h,xn,None,True)])
    group(None,[],[(p,b,h,part,None,True) for p in range(len(parts))])
    if two:
        group(None,[(1,b,y1)],[(1,b,y1,rt,has_r,False),(1,b,y1,lf,has_l,False),(1,b,y1,xn,None,False),(1,b,y1,part,None,False)])
    group(None,[(0,b,x1)],[(0,b,x1,yn,None,False),(0,b,x1,part,None,False)])
    for d in range(1,B):
        cl=b>=d; cr=b+d<B
        group(cl,[(0,b-d,h)],[(0,b-d,h,rt,has_r,False),(0,b-d,h,xn,None,False),(0,b-d,h,yn,None,False),(0,b-d,h,part,None,False)])
        group(cr,[(0,b+d,h)],[(0,b+d,h,lf,has_l,False),(0,b+d,h,xn,None,False),(0,b+d,h,yn,None,False),(0,b+d,h,part,None,False)])
        if two:
            for hh in (h,y1):
                group(cl,[(1,b-d,hh)],[(1,b-d,hh,rt,has_r,False),(1,b-d,hh,xn,None,False),(1,b-d,hh,part,None,False)])
                group(cr,[(1,b+d,hh)],[(1,b+d,hh,lf,has_l,False),(1,b+d,hh,xn,None,False),(1,b+d,hh,part,None,False)])
        group(cl,[(0,b-d,x1)],[(0,b-d,x1,yn,None,False),(0,b-d,x1,part,None,False)])
        group(cr,[(0,b+d,x1)],[(0,b+d,x1,yn,None,False),(0,b+d,x1,part,None,False)])
    for d in range(B):
        for sg in ((1,-1) if d else (1,)):
            c=None if d==0 else (b+d<B if sg>0 else b>=d)
            bb=b+sg*d
            w=[(0,bb,y1),(0,bb,xy)]
            if two: w+= [(1,bb,x1),(1,bb,xy)]
            for e in w:
                group(c,[e],[(e[0],bb,e[2],part,None,False)])
    for bb in range(B):
        for hh in range(H):
            for p in range(len(parts)): wait(p,bb,hh,1-s)
    local.wait()
    for c,cp in pend:
        if c is None: cp.wait_send()
        else: pl.when(c)(cp.wait_send)

def all_gather32(x,B,H,cid,by_section=False,frac=0.636,vmem_out=False):
    R,C=x.shape
    step=16 if x.dtype==jnp.bfloat16 else 8
    a=split_rows(R,step,frac) if R>=4*step else R
    parts=[(0,a)]+([(a,R-a)] if a<R else [])
    n=2*B*H
    nsend=4+4+2+4+2+(B-1)*(8+4*4*1+4)+ (2*B-1)*4+16
    return pl.pallas_call(functools.partial(ag_kernel,B,H,parts,by_section),
        out_shape=jax.ShapeDtypeStruct((n,R,C),x.dtype),
        in_specs=[pl.BlockSpec(memory_space=pltpu.VMEM)],
        out_specs=pl.BlockSpec(memory_space=pl.ANY),
        scratch_shapes=[pltpu.SemaphoreType.DMA((nsend,)),pltpu.SemaphoreType.DMA((len(parts),n)),pltpu.SemaphoreType.DMA((1,))],
        compiler_params=pltpu.CompilerParams(collective_id=cid,has_side_effects=True),name=f"gather_{R}")(x)

def rs_kernel(B,H,parts,by_section,ranges,*refs):
    n_in=len(ranges)
    p_refs=refs[:n_in]; o_ref=refs[n_in]
    q,r1,ya,xa,za,xb,zb,yb,lsem,psem_s,psem_r,ssem,ya_s,xa_s,za_s,xb_s,zb_s,yb_s=refs[n_in+1:]
    s=lax.axis_index("section"); b=lax.axis_index("blk"); h=lax.axis_index("shard")
    x=h&1; y=h>>1
    part=(1-s,b,h); xn=(s,b,h^1); yn=(s,b,h^2); lf=(s,b-1,h); rt=(s,b+1,h)
    has_l=b>0; has_r=b<B-1
    bar=pltpu.get_barrier_semaphore()
    for t in (part,xn,yn):
        pl.semaphore_signal(bar,inc=1,device_id=t,device_id_type=MESH)
    @pl.when(has_l)
    def _(): pl.semaphore_signal(bar,inc=1,device_id=lf,device_id_type=MESH)
    @pl.when(has_r)
    def _(): pl.semaphore_signal(bar,inc=1,device_id=rt,device_id_type=MESH)
    (a0,an),(b0,bn)=parts
    def slot(bb,hh,ss):
        return (ss*B+bb)*H+hh if by_section else (bb*H+hh)*2+ss
    hs=[h^3,h^2,h^1,h]
    order=[(d,sg,k) for k in range(4) for d in range(B-1,-1,-1) for sg in ((1,-1) if d else (1,))]
    N=B*H
    def src(bb,hh,ss):
        return p_refs[0].at[slot(bb,hh,ss)]
    seq=[(bb,k) for k in range(4) for bb in range(B)]
    loads=[]
    for i,(bb,k) in enumerate(seq):
        hh=hs[k]
        cp=pltpu.make_async_copy(src(bb,hh,s),q.at[bb*H+hh],lsem.at[i]); cp.start()
        loads.append(cp)
    pl.semaphore_wait(bar,3+has_l.astype(jnp.int32)+has_r.astype(jnp.int32))
    psend=[]
    for i,(bb,k) in enumerate(seq):
        hh=hs[k]
        cp=remote(src(bb,hh,1-s),r1.at[bb*H+hh],psem_s.at[i],psem_r.at[i],part); cp.start()
        psend.append(cp)
    pend=[]; late=[]
    def flush():
        while late:
            c,cp=late.pop(0)
            if c is None: cp.start()
            else: pl.when(c)(cp.start)
    def queue(c,srcr,dstr,sem,dev):
        cp=remote(srcr,dstr,ssem.at[len(pend)],sem,dev)
        pend.append((c,cp)); late.append((c,cp))
    def add(dst,a,n):
        step=next(k for k in (128,112,96,80,64,48,32,16) if n%k==0)
        @pl.loop(0,n//step)
        def _(i):
            r=pl.ds(pl.multiple_of(i*step,step),step)
            dst[r,:]=dst[r,:]+a[r,:]
    A=pl.ds(a0,an); Bp=pl.ds(b0,bn)
    def got(dst,sem):
        remote(dst,dst,ssem.at[0],sem,part).wait_recv()
    R=an+bn
    for i,(bb,k) in enumerate(seq):
        hh=hs[k]
        loads[i].wait(); got(r1.at[bb*H+hh],psem_r.at[i])
        add(q.at[bb*H+hh],r1.at[bb*H+hh],R)
        flush()
        if k in (0,1):
            xx=(x^1) if k==0 else x
            queue(None,q.at[bb*H+hh,A],ya.at[bb*2+xx],ya_s.at[bb*2+xx],yn)
        if k in (0,2):
            yy=(y^1) if k==0 else y
            queue(None,q.at[bb*H+hh,Bp],xb.at[bb*2+yy],xb_s.at[bb*2+yy],xn)
    flush()
    for bb in range(B):
        for kk in range(2):
            xx=(x^1) if kk==0 else x
            hA=(h^1) if kk==0 else h
            yy=(y^1) if kk==0 else y
            hB=(h^2) if kk==0 else h
            if kk==0:
                got(ya.at[bb*2+xx],ya_s.at[bb*2+xx])
                add(q.at[bb*H+hA,A],ya.at[bb*2+xx],an)
                flush()
                queue(None,q.at[bb*H+hA,A],xa.at[bb],xa_s.at[bb],xn)
            got(xb.at[bb*2+yy],xb_s.at[bb*2+yy])
            add(q.at[bb*H+hB,Bp],xb.at[bb*2+yy],bn)
            flush()
    for bb in range(B):
        got(ya.at[bb*2+x],ya_s.at[bb*2+x])
        add(q.at[bb*H+h,A],ya.at[bb*2+x],an)
    def line_step(qref_of,zref_of,zsem_of,nn,d,sg,pre=None):
        t=b+sg*d
        c=(t<B) if sg>0 else (t>=0)
        hin=has_l if sg>0 else has_r
        dn=0 if sg>0 else 1
        dev=rt if sg>0 else lf
        def run():
            if pre is not None: pre(t)
            @pl.when(hin)
            def _():
                got(zref_of(dn,t),zsem_of(dn,t))
                add(qref_of(t),zref_of(dn,t),nn)
        pl.when(c)(run)
        flush()
        queue(c,qref_of(t),zref_of(dn,t),zsem_of(dn,t),dev)
    def final(qref_of,zref_of,zsem_of,nn):
        for dn,hin in ((0,has_l),(1,has_r)):
            @pl.when(hin)
            def _():
                got(zref_of(dn,b),zsem_of(dn,b))
                add(qref_of(b),zref_of(dn,b),nn)
    def pre_a(t):
        got(xa.at[t],xa_s.at[t])
        add(q.at[t*H+h,A],xa.at[t],an)
    fB=[]
    for yy,hh in ((y^1,h^2),(y,h)):
        fB.append((lambda t,hh=hh: q.at[t*H+hh,Bp], lambda dn,t,yy=yy: zb.at[(dn*B+t)*2+yy], lambda dn,t,yy=yy: zb_s.at[(dn*B+t)*2+yy], bn))
    fA=(lambda t: q.at[t*H+h,A], lambda dn,t: za.at[dn*B+t], lambda dn,t: za_s.at[dn*B+t], an)
    for d in range(B-1,0,-1):
        for sg in (1,-1):
            line_step(*fB[0],d,sg)
            line_step(*fB[1],d,sg)
            line_step(*fA,d,sg,pre_a)
    flush()
    pre_a(b)
    final(*fB[0])
    queue(None,q.at[b*H+(h^2),Bp],yb,yb_s.at[0],yn)
    final(*fA)
    flush()
    final(*fB[1])
    got(yb,yb_s.at[0])
    add(q.at[b*H+h,Bp],yb,bn)
    o_ref[...]=q[b*H+h]
    for cp in psend: cp.wait_send()
    for c,cp in pend:
        if c is None: cp.wait_send()
        else: pl.when(c)(cp.wait_send)

def reduce_scatter32(p,B,H,cid,by_section=False,frac=0.636):
    n,R,C=p.shape
    a=split_rows(R,16,frac)
    parts=((0,a),(a,R-a))
    V=lambda *s: pltpu.VMEM(s,p.dtype)
    D=lambda *s: pltpu.SemaphoreType.DMA(s)
    N=B*H
    an,bn=a,R-a
    nsend=8*B+B+6*(B-1)+8
    return pl.pallas_call(functools.partial(rs_kernel,B,H,parts,by_section,((0,n),)),
        out_shape=jax.ShapeDtypeStruct((R,C),p.dtype),
        in_specs=[pl.BlockSpec(memory_space=pl.ANY)],
        out_specs=pl.BlockSpec(memory_space=pltpu.VMEM),
        scratch_shapes=[V(N,R,C),V(N,R,C),V(2*B,an,C),V(B,an,C),V(2*B,an,C),V(2*B,bn,C),V(4*B,bn,C),V(bn,C),
           D(N),D(N),D(N),D(nsend),D(2*B),D(B),D(2*B),D(2*B),D(4*B),D(1)],
        compiler_params=pltpu.CompilerParams(collective_id=cid,has_side_effects=True,vmem_limit_bytes=63*1024*1024),name=f"scatter_{R}")(p)


def gather_all(value, cid, by_section=False):
    blk, shard = lax.axis_size("blk"), lax.axis_size("shard")
    if blk * shard <= 16 and shard == 4:
        return all_gather32(value, blk, shard, cid, by_section)
    names = ("section", "blk", "shard") if by_section else ORDER
    return lax.all_gather(value, names)


def scatter_all(value, cid, by_section=False):
    blk, shard = lax.axis_size("blk"), lax.axis_size("shard")
    if blk * shard <= 16 and shard == 4:
        return reduce_scatter32(value, blk, shard, cid, by_section)
    names = ("section", "blk", "shard") if by_section else ORDER
    return lax.psum_scatter(value, names, scatter_dimension=0)


def lookup_kernel(ids_ref, tab_ref, o_ref):
    rows = lax.broadcasted_iota(jnp.int32, (tab_ref.shape[0], ids_ref.shape[-1]), 0)
    hot = jnp.where(rows == ids_ref[0], 1.0, 0.0).astype(bf16)
    o_ref[0] = lax.dot_general(
        hot, tab_ref[...], (((0,), (0,)), ((), ())), preferred_element_type=f32
    ).astype(bf16)


def lookup(local_ids, table_low):
    count, tokens = local_ids.shape
    vocab = table_low.shape[0]
    return pl.pallas_call(
        lookup_kernel,
        grid=(count,),
        out_shape=jax.ShapeDtypeStruct((count, tokens, D), bf16),
        in_specs=[
            pl.BlockSpec((1, 1, tokens), lambda i: (i, 0, 0)),
            pl.BlockSpec((vocab, D), lambda i: (0, 0)),
        ],
        out_specs=pl.BlockSpec((1, tokens, D), lambda i: (i, 0, 0)),
        name="lookup",
    )(local_ids[:, None, :], table_low)


def spread_kernel(ids_ref, g_ref, base_ref, o_ref):
    rows = lax.broadcasted_iota(jnp.int32, (o_ref.shape[0], ids_ref.shape[-1]), 0)
    hot = jnp.where(rows == ids_ref[0], 1.0, 0.0).astype(bf16)

    @pl.when(pl.program_id(0) == 0)
    def _():
        o_ref[...] = base_ref[...]

    o_ref[...] += jnp.dot(hot, g_ref[0], preferred_element_type=f32)


def spread(local_ids, grads, base):
    count, tokens = local_ids.shape
    vocab = base.shape[0]
    return pl.pallas_call(
        spread_kernel,
        grid=(count,),
        out_shape=jax.ShapeDtypeStruct((vocab, D), f32),
        in_specs=[
            pl.BlockSpec((1, 1, tokens), lambda i: (i, 0, 0)),
            pl.BlockSpec((1, tokens, D), lambda i: (i, 0, 0)),
            pl.BlockSpec((vocab, D), lambda i: (0, 0)),
        ],
        out_specs=pl.BlockSpec((vocab, D), lambda i: (0, 0)),
        name="spread",
    )(local_ids[:, None, :], grads, base)


def stats_kernel(vocab, nf_ref, tab_ref, top_ref, sum_ref):
    logits = lax.dot_general(
        tab_ref[...], nf_ref[0], (((1,), (1,)), ((), ())), preferred_element_type=f32
    )
    rows = lax.broadcasted_iota(jnp.int32, logits.shape, 0)
    logits = jnp.where(rows < vocab, logits, -1e30)
    top = jnp.max(logits, axis=0, keepdims=True)
    top_ref[0] = top
    sum_ref[0] = jnp.sum(jnp.exp(logits - top), axis=0, keepdims=True)


def vocab_stats(normed, table_low, vocab):
    count, tokens, _ = normed.shape
    padded = table_low.shape[0]
    row = jax.ShapeDtypeStruct((count, 1, tokens), f32)
    return pl.pallas_call(
        functools.partial(stats_kernel, vocab),
        grid=(count,),
        out_shape=(row, row),
        in_specs=[
            pl.BlockSpec((1, tokens, D), lambda i: (i, 0, 0)),
            pl.BlockSpec((padded, D), lambda i: (0, 0)),
        ],
        out_specs=(
            pl.BlockSpec((1, 1, tokens), lambda i: (i, 0, 0)),
            pl.BlockSpec((1, 1, tokens), lambda i: (i, 0, 0)),
        ),
        name="vocab_stats",
    )(normed, table_low)


def vocab_kernel(vocab, scale, nf_ref, tab_ref, lse_ref, t0_ref, t1_ref, g_ref, acc_ref, pick_ref):
    logits = lax.dot_general(
        tab_ref[...], nf_ref[0], (((1,), (1,)), ((), ())), preferred_element_type=f32
    )
    rows = lax.broadcasted_iota(jnp.int32, logits.shape, 0)
    hits = jnp.where(rows == t0_ref[0], 1.0, 0.0) + jnp.where(rows == t1_ref[0], second_weight, 0.0)
    soft = jnp.exp(logits - lse_ref[0]) * (1.0 + second_weight)
    grad = jnp.where(rows < vocab, (soft - hits) * scale, 0.0).astype(bf16)

    @pl.when(pl.program_id(0) == 0)
    def _():
        acc_ref[...] = jnp.zeros_like(acc_ref)
        pick_ref[...] = jnp.zeros_like(pick_ref)

    pick_ref[...] += jnp.sum(hits * logits, axis=0, keepdims=True)
    g_ref[0] = lax.dot_general(
        grad, tab_ref[...], (((0,), (0,)), ((), ())), preferred_element_type=f32
    ).astype(bf16)
    acc_ref[...] += jnp.dot(grad, nf_ref[0], preferred_element_type=f32)


def vocab_grads(normed, table_low, log_total, first, second, vocab, scale):
    count, tokens, _ = normed.shape
    padded = table_low.shape[0]
    row = pl.BlockSpec((1, 1, tokens), lambda i: (i, 0, 0))
    return pl.pallas_call(
        functools.partial(vocab_kernel, vocab, scale),
        grid=(count,),
        out_shape=(
            jax.ShapeDtypeStruct((count, tokens, D), bf16),
            jax.ShapeDtypeStruct((padded, D), f32),
            jax.ShapeDtypeStruct((1, tokens), f32),
        ),
        in_specs=[
            pl.BlockSpec((1, tokens, D), lambda i: (i, 0, 0)),
            pl.BlockSpec((padded, D), lambda i: (0, 0)),
            row,
            row,
            row,
        ],
        out_specs=(
            pl.BlockSpec((1, tokens, D), lambda i: (i, 0, 0)),
            pl.BlockSpec((padded, D), lambda i: (0, 0)),
            pl.BlockSpec((1, tokens), lambda i: (0, 0)),
        ),
        name="vocab_grads",
    )(normed, table_low, log_total[:, None, :], first[:, None, :], second[:, None, :])


def place_of(index, shard):
    return (index % 2, index // (2 * shard), (index // 2) % shard)


def my_place():
    shard = lax.axis_size("shard")
    return (lax.axis_index("blk") * shard + lax.axis_index("shard")) * 2 + lax.axis_index("section")


def meet(reach, block, blocks, mine, shard, sign):
    barrier = pltpu.get_barrier_semaphore()
    above = [block + d < blocks for d in range(1, reach + 1)]
    below = [block >= d for d in range(1, reach + 1)]
    sources, targets = (below, above) if sign > 0 else (above, below)
    for d in range(1, reach + 1):

        @pl.when(sources[d - 1])
        def _():
            pl.semaphore_signal(
                barrier, inc=1, device_id=place_of(mine - sign * d, shard), device_id_type=MESH
            )

    @pl.when(targets[0])
    def _():
        pl.semaphore_wait(barrier, sum(held.astype(jnp.int32) for held in targets))


def half_masks(tokens):
    lane = lax.broadcasted_iota(jnp.int32, (tokens, 2 * HEAD_DIM), 1)
    return lane < HEAD_DIM


def allowed_mask(d, seg_ref, tokens):
    own = jnp.transpose(jnp.broadcast_to(seg_ref[0], (128, tokens)))[:, :1]
    allowed = own == seg_ref[d]
    if d == 0:
        row = lax.broadcasted_iota(jnp.int32, (tokens, tokens), 0)
        col = lax.broadcasted_iota(jnp.int32, (tokens, tokens), 1)
        allowed = allowed & (col <= row)
    return allowed


def attend_kernel(reach, blocks, q_ref, k_ref, v_ref, seg_ref, tot_ref, acc_ref, kr_ref, vr_ref,
                  send_sem, recv_sem):
    shard = lax.axis_size("shard")
    mine = (lax.axis_index("blk") * shard + lax.axis_index("shard")) * 2 + lax.axis_index("section")
    block = mine % blocks
    tokens = q_ref.shape[0]
    meet(reach, block, blocks, mine, shard, 1)

    def copies(d):
        target = place_of(mine + d, shard)
        return [
            pltpu.make_async_remote_copy(
                src_ref=source,
                dst_ref=target_ref.at[d - 1],
                send_sem=send_sem.at[d - 1, i],
                recv_sem=recv_sem.at[d - 1, i],
                device_id=target,
                device_id_type=MESH,
            )
            for i, (source, target_ref) in enumerate(((k_ref, kr_ref), (v_ref, vr_ref)))
        ]

    for d in range(reach, 0, -1):

        @pl.when(block + d < blocks)
        def _():
            for copy in copies(d):
                copy.start()

    scale = HEAD_DIM ** (-0.5)
    left = half_masks(tokens)
    zero = jnp.zeros((tokens, 2 * HEAD_DIM), bf16)

    def visit(d, keys, values):
        allowed = allowed_mask(d, seg_ref, tokens)

        @pl.loop(0, HEADS // 2)
        def _(pair):
            lanes = pl.ds(pl.multiple_of(pair * 128, 128), 128)
            q_pair, k_pair, v_pair = q_ref[:, lanes], keys[:, lanes], values[:, lanes]
            totals, sums = [], []
            for side in (left, ~left):
                scores = lax.dot_general(
                    jnp.where(side, q_pair, zero),
                    k_pair,
                    (((1,), (1,)), ((), ())),
                    preferred_element_type=f32,
                )
                expo = jnp.where(allowed, jnp.exp(scores * scale), 0.0)
                totals.append(jnp.sum(expo, axis=1, keepdims=True))
                sums.append(jnp.dot(expo.astype(bf16), v_pair, preferred_element_type=f32))
            total = jnp.where(left, totals[0], totals[1])
            added = jnp.where(left, sums[0], sums[1])
            if d == 0:
                tot_ref[:, lanes] = total
                acc_ref[:, lanes] = added
            else:
                tot_ref[:, lanes] += total
                acc_ref[:, lanes] += added

    visit(0, k_ref, v_ref)
    for d in range(1, reach + 1):

        @pl.when(block >= d)
        def _():
            for copy in copies(d):
                copy.wait_recv()
            visit(d, kr_ref.at[d - 1], vr_ref.at[d - 1])

    for d in range(1, reach + 1):

        @pl.when(block + d < blocks)
        def _():
            for copy in copies(d):
                copy.wait_send()


def attend(q, k, v, seg_rows, reach, blocks, cid):
    tokens = q.shape[0]
    wide = jax.ShapeDtypeStruct((tokens, D), f32)
    far = jax.ShapeDtypeStruct((reach, tokens, D), bf16)
    whole = pl.BlockSpec(memory_space=pltpu.VMEM)
    return pl.pallas_call(
        functools.partial(attend_kernel, reach, blocks),
        out_shape=(wide, wide, far, far),
        in_specs=[whole] * 4,
        out_specs=(whole,) * 4,
        scratch_shapes=[
            pltpu.SemaphoreType.DMA((reach, 2)),
            pltpu.SemaphoreType.DMA((reach, 2)),
        ],
        compiler_params=pltpu.CompilerParams(
            collective_id=cid, has_side_effects=True, vmem_limit_bytes=VMEM_MAX
        ),
        name="attend",
    )(q, k, v, seg_rows)


def attend_back_kernel(reach, blocks, q_ref, k_ref, v_ref, kr_ref, vr_ref, tot_ref, acc_ref, ga_ref,
                       seg_ref, dq_ref, dk_ref, dv_ref, gw, gt, far_k, far_v, got_k, got_v,
                       send_sem, recv_sem):
    shard = lax.axis_size("shard")
    mine = (lax.axis_index("blk") * shard + lax.axis_index("shard")) * 2 + lax.axis_index("section")
    block = mine % blocks
    tokens = q_ref.shape[0]
    meet(reach, block, blocks, mine, shard, -1)
    scale = HEAD_DIM ** (-0.5)
    left = half_masks(tokens)
    zero = jnp.zeros((tokens, 2 * HEAD_DIM), bf16)

    @pl.loop(0, HEADS // 2)
    def _(pair):
        lanes = pl.ds(pl.multiple_of(pair * 128, 128), 128)
        inverse = 1.0 / tot_ref[:, lanes]
        grad = ga_ref[:, lanes]
        gw[:, lanes] = (grad * inverse).astype(bf16)
        product = grad * acc_ref[:, lanes]
        first = jnp.sum(jnp.where(left, product, 0.0), axis=1, keepdims=True)
        second = jnp.sum(jnp.where(left, 0.0, product), axis=1, keepdims=True)
        gt[:, lanes] = -jnp.where(left, first, second) * inverse * inverse
        dq_ref[:, lanes] = jnp.zeros((tokens, 128), f32)

    def visit(d, keys, values, out_k, out_v):
        allowed = allowed_mask(d, seg_ref, tokens)

        @pl.loop(0, HEADS // 2)
        def _(pair):
            lanes = pl.ds(pl.multiple_of(pair * 128, 128), 128)
            q_pair, k_pair, v_pair, w_pair = q_ref[:, lanes], keys[:, lanes], values[:, lanes], gw[:, lanes]
            gt_pair = gt[:, lanes]
            dq, dk, dv = [], [], []
            for i, side in enumerate((left, ~left)):
                scores = lax.dot_general(
                    jnp.where(side, q_pair, zero),
                    k_pair,
                    (((1,), (1,)), ((), ())),
                    preferred_element_type=f32,
                )
                expo = jnp.where(allowed, jnp.exp(scores * scale), 0.0)
                probs = lax.dot_general(
                    jnp.where(side, w_pair, zero),
                    v_pair,
                    (((1,), (1,)), ((), ())),
                    preferred_element_type=f32,
                )
                part = (expo * (probs + gt_pair[:, i * HEAD_DIM : i * HEAD_DIM + 1])).astype(bf16)
                dq.append(jnp.dot(part, k_pair, preferred_element_type=f32))
                dk.append(
                    lax.dot_general(part, q_pair, (((0,), (0,)), ((), ())), preferred_element_type=f32)
                )
                dv.append(
                    lax.dot_general(
                        expo.astype(bf16), w_pair, (((0,), (0,)), ((), ())), preferred_element_type=f32
                    )
                )
            dq_ref[:, lanes] += jnp.where(left, dq[0], dq[1]) * scale
            out_k[:, lanes] = (jnp.where(left, dk[0], dk[1]) * scale).astype(out_k.dtype)
            out_v[:, lanes] = jnp.where(left, dv[0], dv[1]).astype(out_v.dtype)

    def copies(d):
        target = place_of(mine - d, shard)
        return [
            pltpu.make_async_remote_copy(
                src_ref=source.at[d - 1],
                dst_ref=target_ref.at[d - 1],
                send_sem=send_sem.at[d - 1, i],
                recv_sem=recv_sem.at[d - 1, i],
                device_id=target,
                device_id_type=MESH,
            )
            for i, (source, target_ref) in enumerate(((far_k, got_k), (far_v, got_v)))
        ]

    for d in range(reach, 0, -1):

        @pl.when(block >= d)
        def _():
            visit(d, kr_ref.at[d - 1], vr_ref.at[d - 1], far_k.at[d - 1], far_v.at[d - 1])
            for copy in copies(d):
                copy.start()

    visit(0, k_ref, v_ref, dk_ref, dv_ref)
    for d in range(reach, 0, -1):

        @pl.when(block + d < blocks)
        def _():
            for copy in copies(d):
                copy.wait_recv()
            dk_ref[...] += got_k[d - 1].astype(f32)
            dv_ref[...] += got_v[d - 1].astype(f32)

    for d in range(1, reach + 1):

        @pl.when(block >= d)
        def _():
            for copy in copies(d):
                copy.wait_send()


def attend_back(q, k, v, far_k, far_v, total, accum, grad, seg_rows, reach, blocks, cid):
    tokens = q.shape[0]
    wide = jax.ShapeDtypeStruct((tokens, D), f32)
    whole = pl.BlockSpec(memory_space=pltpu.VMEM)
    return pl.pallas_call(
        functools.partial(attend_back_kernel, reach, blocks),
        out_shape=(wide, wide, wide),
        in_specs=[whole] * 9,
        out_specs=(whole,) * 3,
        scratch_shapes=[pltpu.VMEM((tokens, D), bf16), pltpu.VMEM((tokens, D), f32)]
        + [pltpu.VMEM((reach, tokens, D), bf16)] * 4
        + [pltpu.SemaphoreType.DMA((reach, 2)), pltpu.SemaphoreType.DMA((reach, 2))],
        compiler_params=pltpu.CompilerParams(
            collective_id=cid, has_side_effects=True, vmem_limit_bytes=VMEM_MAX
        ),
        name="attend_back",
    )(q, k, v, far_k, far_v, total, accum, grad, seg_rows)


def matrix_layout():
    return ((D, 3 * D), (D, D), (D, 2 * FF), (FF, D))


def blocks_to_rows(blocks):
    count = blocks.shape[0]
    if count % 4:
        return blocks.reshape(-1, QUAD)
    quads = blocks.reshape(count // 4, 4, BS, BS).transpose(0, 2, 1, 3)
    return quads.reshape(-1, QUAD)


def rows_to_blocks(rows):
    count = rows.shape[0] * QUAD // (BS * BS)
    if count % 4:
        return rows.reshape(count, BS, BS)
    return rows.reshape(count // 4, BS, 4, BS).transpose(0, 2, 1, 3).reshape(count, BS, BS)


def rows_to_quads(rows, count):
    if count % 4:
        rows = rows.reshape(-1, 4, BS, BS).transpose(0, 2, 1, 3)
    return rows.reshape(-1, BS, QUAD)


def quads_to_rows(quads, count):
    if count % 4:
        quads = quads.reshape(-1, BS, 4, BS).transpose(0, 2, 1, 3)
    return quads.reshape(-1, count * BS * BS // QUAD, QUAD)


def quads_to_matrices(quads):
    matrices, offset = [], 0
    for rows, cols in matrix_layout():
        r, c = rows // BS, cols // QUAD
        part = quads[offset : offset + r * c].reshape(r, c, BS, QUAD)
        matrices.append(part.transpose(0, 2, 1, 3).reshape(rows, cols))
        offset += r * c
    return matrices


def matrices_to_quads(matrices):
    parts = []
    for matrix, (rows, cols) in zip(matrices, matrix_layout()):
        r, c = rows // BS, cols // QUAD
        parts.append(
            matrix.reshape(r, BS, c, QUAD).transpose(0, 2, 1, 3).reshape(r * c, BS, QUAD)
        )
    return jnp.concatenate(parts, axis=0)


def rms_scale(states, gain_row):
    return (
        states * lax.rsqrt(jnp.mean(states * states, axis=-1, keepdims=True) + norm_eps) * gain_row
    )


def rms_back(states, gain_row, grad_out):
    inverse = lax.rsqrt(jnp.mean(states * states, axis=-1, keepdims=True) + norm_eps)
    weighted = grad_out * gain_row
    grad_in = inverse * weighted - states * inverse * inverse * inverse * jnp.mean(
        weighted * states, axis=-1, keepdims=True
    )
    return (grad_in, jnp.sum(grad_out * states * inverse, axis=0))


def rope_tables(positions):
    half_dim = HEAD_DIM // 2
    frequency = rope_base ** (-jnp.arange(half_dim, dtype=f32) * 2.0 / HEAD_DIM)
    angles = positions.astype(f32)[:, None] * frequency[None, :]
    cosine, sine = jnp.cos(angles), jnp.sin(angles)
    return (
        jnp.concatenate([cosine, cosine], axis=-1)[:, None, :],
        jnp.concatenate([sine, sine], axis=-1)[:, None, :],
    )


def rotate(values, cosine, sine):
    half_dim = HEAD_DIM // 2
    turned = jnp.concatenate([-values[..., half_dim:], values[..., :half_dim]], axis=-1)
    return values * cosine + turned * sine


def rotate_back(grads, cosine, sine):
    half_dim = HEAD_DIM // 2
    scaled = grads * sine
    turned = jnp.concatenate([scaled[..., half_dim:], -scaled[..., :half_dim]], axis=-1)
    return grads * cosine + turned


def layer_forward(states, weights, gain_first, gain_second, tables, seg_rows, reach, blocks, cid):
    w_qkv, w_out, w_gate_up, w_down = weights
    rows = states.shape[0]
    normed = rms_scale(states, gain_first).astype(bf16)
    projected = jnp.dot(normed, w_qkv, preferred_element_type=f32)

    def turned(part):
        return rotate(part.reshape(rows, HEADS, HEAD_DIM), *tables).astype(bf16).reshape(rows, D)

    q = turned(projected[:, :D])
    k = turned(projected[:, D : 2 * D])
    v = projected[:, 2 * D :].astype(bf16)
    total, accum, far_k, far_v = attend(q, k, v, seg_rows, reach, blocks, cid)
    attended = (accum / total).astype(bf16)
    mixed = states + jnp.dot(attended, w_out, preferred_element_type=f32)
    normed_mid = rms_scale(mixed, gain_second).astype(bf16)
    gate_up = jnp.dot(normed_mid, w_gate_up, preferred_element_type=f32)
    gate, upper = gate_up[:, :FF], gate_up[:, FF:]
    hidden = (jax.nn.silu(gate) * upper).astype(bf16)
    output = mixed + jnp.dot(hidden, w_down, preferred_element_type=f32)
    return output, (
        states, normed, q, k, v, far_k, far_v, total, accum, attended, mixed, normed_mid, gate,
        upper, hidden,
    )


def layer_backward(cache, grad_out, weights, gain_first, gain_second, tables, seg_rows, reach, blocks, cid):
    (
        states, normed, q, k, v, far_k, far_v, total, accum, attended, mixed, normed_mid, gate,
        upper, hidden,
    ) = cache
    w_qkv, w_out, w_gate_up, w_down = weights
    rows = states.shape[0]

    def outer(left_side, right_side):
        return jnp.einsum(
            "rd,rf->df", left_side, right_side, preferred_element_type=f32
        ).astype(bf16)

    def through(grad, weight):
        return jnp.einsum("rf,df->rd", grad, weight, preferred_element_type=f32)

    grad_low = grad_out.astype(bf16)
    grad_w_down = outer(hidden, grad_low)
    grad_hidden = through(grad_low, w_down)
    sig = jax.nn.sigmoid(gate)
    grad_gate = grad_hidden * upper * sig * (1.0 + gate * (1.0 - sig))
    grad_up = grad_hidden * gate * sig
    grad_gate_up = jnp.concatenate([grad_gate, grad_up], axis=-1).astype(bf16)
    grad_w_gate_up = outer(normed_mid, grad_gate_up)
    grad_mid_norm, grad_gain_second = rms_back(mixed, gain_second, through(grad_gate_up, w_gate_up))
    grad_mixed = grad_out + grad_mid_norm
    grad_att = grad_mixed.astype(bf16)
    grad_w_out = outer(attended, grad_att)
    grad_attended = through(grad_att, w_out)
    grad_q, grad_k, grad_v = attend_back(
        q, k, v, far_k, far_v, total, accum, grad_attended, seg_rows, reach, blocks, cid
    )

    def unturned(part):
        return rotate_back(part.reshape(rows, HEADS, HEAD_DIM), *tables).reshape(rows, D)

    grad_qkv = jnp.concatenate([unturned(grad_q), unturned(grad_k), grad_v], axis=-1).astype(bf16)
    grad_w_qkv = outer(normed, grad_qkv)
    grad_in_norm, grad_gain_first = rms_back(states, gain_first, through(grad_qkv, w_qkv))
    return (
        grad_mixed + grad_in_norm,
        (grad_w_qkv, grad_w_out, grad_w_gate_up, grad_w_down),
        grad_gain_first,
        grad_gain_second,
    )


def adam_step(weight, first, second, grad_in, decay):
    first_new = beta_first * first + (1.0 - beta_first) * grad_in
    second_new = beta_second * second + (1.0 - beta_second) * grad_in * grad_in
    weight_new = weight - adam_rate * (
        first_new / (jnp.sqrt(second_new) + adam_eps) + decay * weight
    )
    return (weight_new, first_new, second_new)


def on_device(ids, targets, segments, table, table_m, table_v, blocks, left_stats, right_stats,
              left_root, right_root, gains, gains_m, gains_v):
    blk, shard = lax.axis_size("blk"), lax.axis_size("shard")
    section = lax.axis_index("section")
    blk_index, shard_index = lax.axis_index("blk"), lax.axis_index("shard")
    devices = 2 * blk * shard
    micro, _, tok_rows = ids.shape
    seq_len = segments.shape[2]
    all_tokens = micro * shard * seq_len
    tokens = all_tokens // devices
    seq_blocks = seq_len // tokens
    reach = pl.cdiv(seq_len // 2 - 1, tokens)
    vocab = table.shape[0]
    padded = pl.cdiv(vocab, 128) * 128
    own_blocks = blocks.shape[1]

    mine = my_place()
    seg_own = lax.dynamic_slice_in_dim(segments[:, 0, :], blk_index * tok_rows, tok_rows, axis=1)
    packed = jnp.stack(
        [ids[:, 0, :], targets[:, 0, :, 0], targets[:, 0, :, 1], seg_own], axis=0
    ).reshape(4 * micro, tok_rows)
    shared = lax.all_gather(packed, ("blk", "shard")).reshape(blk, shard, 4, micro, tok_rows)
    shared = shared.transpose(2, 3, 1, 0, 4).reshape(4, devices, tokens)
    first_row = ((section * blk + blk_index) * shard + shard_index) * vocab
    local_ids, local_first, local_second = (shared[i] - first_row for i in range(3))

    def mark(values):
        return jnp.where((values >= 0) & (values < vocab), values, -1)

    local_ids, local_first, local_second = mark(local_ids), mark(local_first), mark(local_second)
    seg_index = jnp.maximum(mine - jnp.arange(reach + 1), 0)
    seg_rows = jnp.take(shared[3], seg_index, axis=0).astype(f32)[:, None, :]

    rows_low = blocks_to_rows(blocks[0].astype(bf16))
    gathered = gather_all(rows_low, 0, by_section=True)
    gathered = gathered.reshape(2, blk * shard * rows_low.shape[0], QUAD)
    table_low = jnp.pad(table.astype(bf16), ((0, padded - vocab), (0, 0)))
    looked = lookup(local_ids, table_low)
    states = scatter_all(looked, 1).astype(f32)

    weights = [quads_to_matrices(rows_to_quads(gathered[l], own_blocks)) for l in range(2)]
    positions = (mine % seq_blocks) * tokens + jnp.arange(tokens, dtype=jnp.int32)
    tables = rope_tables(positions)
    caches = []
    for l in range(2):
        states, cache = layer_forward(
            states, weights[l], gains[2 * l], gains[2 * l + 1], tables, seg_rows, reach, seq_blocks, 2
        )
        caches.append(cache)
    final_gain = gains[gains.shape[0] - 1]
    normed_own = rms_scale(states, final_gain).astype(bf16)
    normed = gather_all(normed_own, 3)
    top, spread_sum = vocab_stats(normed, table_low, vocab)
    stats = gather_all(jnp.concatenate([top[:, 0], spread_sum[:, 0]], axis=0), 4)
    tops, sums = stats[:, :devices], stats[:, devices:]
    largest = jnp.max(tops, axis=0)
    log_total = largest + jnp.log(jnp.sum(sums * jnp.exp(tops - largest), axis=0))
    inv_count = 1.0 / all_tokens
    grad_rows, head_term, picks = vocab_grads(
        normed, table_low, log_total, local_first, local_second, vocab, inv_count
    )
    own_log = lax.dynamic_index_in_dim(log_total, mine, 0, keepdims=False)
    loss_part = (1.0 + second_weight) * jnp.sum(own_log) - jnp.sum(picks)
    grad_final = scatter_all(grad_rows, 1).astype(f32)
    grad_states, grad_gain_final = rms_back(states, final_gain, grad_final)
    gain_grads = [None] * 5
    gain_grads[4] = grad_gain_final
    quads = [None, None]
    for l in (1, 0):
        grad_states, grads, gain_grads[2 * l], gain_grads[2 * l + 1] = layer_backward(
            caches[l], grad_states, weights[l], gains[2 * l], gains[2 * l + 1], tables, seg_rows,
            reach, seq_blocks, 5
        )
        quads[l] = quads_to_rows(matrices_to_quads(grads), own_blocks)
    block_rows = scatter_all(jnp.concatenate(quads, axis=0), 6, by_section=True).astype(f32)
    grad_embed = gather_all(grad_states.astype(bf16), 3)
    table_own = spread(local_ids, grad_embed, head_term)[:vocab]
    block_own = rows_to_blocks(block_rows)
    square_sum = jnp.sum(table_own * table_own) + jnp.sum(block_rows * block_rows)
    small = jnp.stack(
        gain_grads
        + [jnp.full((D,), square_sum), jnp.full((D,), loss_part), jnp.zeros((D,), f32)]
    )
    summed = jnp.sum(gather_all(small, 7), axis=0)
    gain_grad = summed[:5]
    clip_norm = jnp.sqrt(summed[5, 0] + jnp.sum(gain_grad * gain_grad))
    factor = clip_bound / jnp.maximum(clip_norm, clip_bound)
    loss = summed[6, 0] * inv_count
    grad_blocks = block_own * factor
    left_new = stat_decay * left_stats[0] + (1.0 - stat_decay) * jnp.einsum(
        "bij,bkj->bik", grad_blocks, grad_blocks, precision=highest
    )
    right_new = stat_decay * right_stats[0] + (1.0 - stat_decay) * jnp.einsum(
        "bji,bjk->bik", grad_blocks, grad_blocks, precision=highest
    )
    direction = jnp.einsum(
        "bij,bjk->bik",
        left_root[0],
        jnp.einsum("bij,bjk->bik", grad_blocks, right_root[0], precision=highest),
        precision=highest,
    )
    blocks_new = blocks[0] - shampoo_rate * direction
    table_new, table_m_new, table_v_new = adam_step(
        table, table_m, table_v, table_own * factor, weight_decay
    )
    gains_new, gains_m_new, gains_v_new = adam_step(
        gains, gains_m, gains_v, gain_grad * factor, 0.0
    )
    return (
        loss, clip_norm, table_new, table_m_new, table_v_new, table_new.astype(bf16),
        blocks_new[None], blocks_new[None].astype(bf16), left_new[None], right_new[None],
        gains_new, gains_m_new, gains_v_new,
    )


def solution(mesh):
    rows = P(("section", "blk", "shard"), None)
    square = P("section", ("blk", "shard"), None, None)
    return jax.shard_map(
        on_device,
        mesh=mesh,
        in_specs=(
            P(None, "shard", "blk"),
            P(None, "shard", "blk", None),
            P(None, "shard", None),
            rows, rows, rows,
            square, square, square, square, square,
            P(), P(), P(),
        ),
        out_specs=(
            P(), P(),
            rows, rows, rows, rows,
            square, square, square, square,
            P(), P(), P(),
        ),
        check_vma=False,
    )
```

time: 3480 us -> 1500 us (0.43)
  waiting for transfers between devices: 2290 us -> 0 us
  Pallas kernels: 0 us -> 974 us
  local copies, waits for them, and re-layouts: 490 us -> 267 us
  matrix products: 291 us -> 83.3 us
  other arithmetic: 224 us -> 109 us
  starting transfers between devices: 94.1 us -> 0 us
    unnamed x12 -> x0, waiting for transfers between devices: 1340 us -> none
    pallas_call x0 -> x16, Pallas kernels: none -> 974 us  [the longest x3 378 us: reduce_scatter32(): pl.pallas_call(functools.partial(rs_kernel, B, H, parts, by_section, ((0,...]
    all_gather x8 -> x0, waiting for transfers between devices: 675 us -> none  [the longest x1 282 us: on_device(): lax.all_gather(blocks[0].astype(jnp.bfloat16), ('blk', 'shard'), axis=0,...]
    ppermute x50 -> x0, waiting for transfers between devices: 283 us -> none  [the longest x42 277 us: shifted_2(): return lax.ppermute(value, axis, pairs)]
    dot_general x60 -> x24, matrix products: 261 us -> 45.3 us  [the longest x8 15.9 us: through(): return jnp.einsum('rf,df->rd', grad, weight, preferred_element_type=f32)]
    reshape x17 -> x11, local copies, waits for them, and re-layouts: 208 us -> 33.5 us  [the longest x6 25.9 us: matrices_to_quads(): matrix.reshape(r, BS, c, QUAD).transpose(0, 2, 1, 3)]
    ppermute x50 -> x0, starting transfers between devices: 92.9 us -> none  [the longest x42 77.8 us: shifted_2(): return lax.ppermute(value, axis, pairs)]
    convert_element_type x63 -> x13, other arithmetic: 86.3 us -> 25 us  [the longest x1 8.66 us: on_device(): table_new.astype(bf16)]
  transfers between devices with their start and end apart: 60 -> 0, of which waited for: 49 -> 0; matrix products, arithmetic and copies ran while one was open for 14% -> 0% of each run, Pallas kernels for 0% -> 0%
where the time goes in v1:
time: 1500 us; the launch traced here: 1490 us
  Pallas kernels  974 us (65%)
  local copies, waits for them, and re-layouts  267 us (18%)
  other arithmetic  109 us (7%)
  matrix products  83.3 us (6%)
  blocking collectives  43.1 us (3%)
    pallas_call x3, Pallas kernels, reduce_scatter32(): pl.pallas_call(functools.partial(rs_kernel, B, H, parts, by_section, ((0,...  378 us
    pallas_call x5, Pallas kernels, all_gather32(): pl.pallas_call(functools.partial(ag_kernel, B, H, parts, by_section), out...  296 us
    pallas_call x1, Pallas kernels, vocab_grads(): pl.pallas_call(functools.partial(vocab_kernel, vocab, scale), grid=(count...  84.9 us
    unnamed x234, local copies, waits for them, and re-layouts  79.1 us
    pallas_call x2, Pallas kernels, attend_back(): pl.pallas_call(functools.partial(attend_back_kernel, reach, blocks), out_...  67.1 us
    pallas_call x2, Pallas kernels, attend(): pl.pallas_call(functools.partial(attend_kernel, reach, blocks), out_shape...  59.5 us
    all_gather x1, blocking collectives, on_device(): lax.all_gather(packed, ('blk', 'shard'))  43.1 us
    pallas_call x1, Pallas kernels, spread(): pl.pallas_call(spread_kernel, grid=(count,), out_shape=jax.ShapeDtypeStru...  31.9 us

profile of v1, /device:TPU:0, one launch (start us, length us, event | category | flops | bytes accessed | tf_op | source)
XLA Modules:
  0.0 1485.8 jit_solution(9062716647714255412)
XLA Ops:
  2.8 43.1 %all_gather.3 = s32[16,8,256]{2,1,0:T(8,128)S(1)} all-gather(s32[1,8,256]{2,1,0:T(8,128)S(1)} %all_gather_reshape.3), channel_id=1, replica_groups=mesh['section'=2,'blk'=4,'shard'=4] {'blk','shard'}, dimensions={0}, use_global_device_ids=true | all-gather | bytes 139264 | tf_op jit(solution)/shard_map/all_gather | solution.py:894
  50.7 24.4 %lookup.1.refs_0_ = bf16[32,256,768]{2,1,0:T(8,128)(2,1)} custom-call(s32[32,1,256]{2,1,0:T(1,128)} %and_select_fusion.2.ids_ref, bf16[1024,768]{1,0:T(8,128)(2,1)} %pad.4.tab_ref), custom_call_target="tpu_custom_call" | custom-call | tf_op jit(solution)/shard_map/lookup/pallas_call | solution.py:320
  75.1 90.0 %scatter_256.2 = bf16[256,768]{1,0:T(8,128)(2,1)} custom-call(bf16[32,256,768]{2,1,0:T(8,128)(2,1)} %lookup.1.refs_0_), custom_call_target="tpu_custom_call" | custom-call | tf_op jit(solution)/shard_map/scatter_256/pallas_call | solution.py:284
  175.2 114.7 %gather_1728.1 = bf16[32,1728,256]{2,1,0:T(8,128)(2,1)} custom-call(bf16[1728,256]{1,0:T(8,128)(2,1)} %reshape.426.x_ref), custom_call_target="tpu_custom_call" | custom-call | tf_op jit(solution)/shard_map/gather_1728/pallas_call | solution.py:137
  290.0 5.4 fusion.61
  322.8 21.4 %attend.2 = (f32[256,768]{1,0:T(8,128)}, f32[256,768]{1,0:T(8,128)}, bf16[2,256,768]{2,1,0:T(8,128)(2,1)}, bf16[2,256,768]{2,1,0:T(8,128)(2,1)}) custom-call(bf16[256,768]{1,0:T(8,128)(2,1)} %get-tuple-element.149.q_ref, bf16[256,768]{1,0:T(8,128)(2,1)} %get-tuple-element.148.k_ref, bf16[256,768]{1,0:T(8,128)(2,1)} %slice.320.v_ref, f32[3,1,256]{2,1,0:T(1,128)} %fusion.44.seg_ref), custom_call_target="tpu_custom_call" | custom-call | tf_op jit(solution)/shard_map/attend/pallas_call | solution.py:565
  344.2 16.7 %fusion.62 = (bf16[16,1728,256]{2,1,0:T(8,128)(2,1)}, bf16[16,1728,256]{2,1,0:T(8,128)(2,1)S(1)}) fusion(bf16[32,1728,256]{2,1,0:T(8,128)(2,1)} %gather_1728.1), kind=kLoop, calls=%fused_computation.200 | loop fusion | bytes 56623104 | tf_op jit(solution)/shard_map/slice | solution.py:913
  367.2 9.6 copy.236
  376.8 9.6 copy.301
  430.2 38.1 %attend.3 = (f32[256,768]{1,0:T(8,128)}, f32[256,768]{1,0:T(8,128)}, bf16[2,256,768]{2,1,0:T(8,128)(2,1)}, bf16[2,256,768]{2,1,0:T(8,128)(2,1)}) custom-call(bf16[256,768]{1,0:T(8,128)(2,1)} %get-tuple-element.147.q_ref, bf16[256,768]{1,0:T(8,128)(2,1)} %get-tuple-element.146.k_ref, bf16[256,768]{1,0:T(8,128)(2,1)} %slice.319.v_ref, f32[3,1,256]{2,1,0:T(1,128)} %fusion.44.seg_ref), custom_call_target="tpu_custom_call" | custom-call | tf_op jit(solution)/shard_map/attend/pallas_call | solution.py:565
  499.2 71.9 %gather_256.2.nf_ref = bf16[32,256,768]{2,1,0:T(8,128)(2,1)} custom-call(bf16[256,768]{1,0:T(8,128)(2,1)} %multiply_convert_fusion.6.x_ref), custom_call_target="tpu_custom_call" | custom-call | tf_op jit(solution)/shard_map/gather_256/pallas_call | solution.py:137
  571.1 31.5 %vocab_stats.1 = (f32[32,1,256]{2,1,0:T(1,128)}, f32[32,1,256]{2,1,0:T(1,128)}) custom-call(bf16[32,256,768]{2,1,0:T(8,128)(2,1)} %gather_256.2.nf_ref, bf16[1024,768]{1,0:T(8,128)(2,1)} %pad.4.tab_ref), custom_call_target="tpu_custom_call" | custom-call | tf_op jit(solution)/shard_map/vocab_stats/pallas_call | solution.py:376
  604.8 24.6 %gather_64.1 = f32[32,64,256]{2,1,0:T(8,128)} custom-call(f32[64,256]{1,0:T(8,128)} %pad_maximum_fusion.21.x_ref), custom_call_target="tpu_custom_call" | custom-call | tf_op jit(solution)/shard_map/gather_64/pallas_call | solution.py:137
  634.5 84.9 %vocab_grads.1 = (bf16[32,256,768]{2,1,0:T(8,128)(2,1)}, f32[1024,768]{1,0:T(8,128)}, f32[1,256]{1,0:T(1,128)}) custom-call(bf16[32,256,768]{2,1,0:T(8,128)(2,1)} %gather_256.2.nf_ref, bf16[1024,768]{1,0:T(8,128)(2,1)} %pad.4.tab_ref, f32[32,1,256]{2,1,0:T(1,128)} %add.234.lse_ref, s32[32,1,256]{2,1,0:T(1,128)} %get-tuple-element.209.t0_ref, ...), custom_call_target="tpu_custom_call" | custom-call | tf_op jit(solution)/shard_map/vocab_grads/pallas_call | solution.py:417
  719.4 92.9 %scatter_256.3 = bf16[256,768]{1,0:T(8,128)(2,1)} custom-call(bf16[32,256,768]{2,1,0:T(8,128)(2,1)} %get-tuple-element.40.refs_0_), custom_call_target="tpu_custom_call" | custom-call | tf_op jit(solution)/shard_map/scatter_256/pallas_call | solution.py:284
  824.7 29.2 %attend_back.2 = (f32[256,768]{1,0:T(8,128)}, f32[256,768]{1,0:T(8,128)}, f32[256,768]{1,0:T(8,128)}) custom-call(bf16[256,768]{1,0:T(8,128)(2,1)} %get-tuple-element.147.q_ref, bf16[256,768]{1,0:T(8,128)(2,1)} %get-tuple-element.146.k_ref, bf16[256,768]{1,0:T(8,128)(2,1)} %slice.319.v_ref, bf16[2,256,768]{2,1,0:T(8,128)(2,1)} %get-tuple-element.41.kr_ref, ...), custom_call_target="tpu_custom_call" | custom-call | tf_op jit(solution)/shard_map/attend_back/pallas_call | solution.py:686
  881.5 37.9 %attend_back.3 = (f32[256,768]{1,0:T(8,128)}, f32[256,768]{1,0:T(8,128)}, f32[256,768]{1,0:T(8,128)}) custom-call(bf16[256,768]{1,0:T(8,128)(2,1)} %get-tuple-element.149.q_ref, bf16[256,768]{1,0:T(8,128)(2,1)} %get-tuple-element.148.k_ref, bf16[256,768]{1,0:T(8,128)(2,1)} %slice.320.v_ref, bf16[2,256,768]{2,1,0:T(8,128)(2,1)} %get-tuple-element.32.kr_ref, ...), custom_call_target="tpu_custom_call" | custom-call | tf_op jit(solution)/shard_map/attend_back/pallas_call | solution.py:686
  943.3 64.9 %gather_256.3.g_ref = bf16[32,256,768]{2,1,0:T(8,128)(2,1)} custom-call(bf16[256,768]{1,0:T(8,128)(2,1)} %fusion.17.x_ref), custom_call_target="tpu_custom_call" | custom-call | tf_op jit(solution)/shard_map/gather_256/pallas_call | solution.py:137
  1008.2 31.9 %spread.1 = f32[1024,768]{1,0:T(8,128)} custom-call(s32[32,1,256]{2,1,0:T(1,128)} %and_select_fusion.2.ids_ref, bf16[32,256,768]{2,1,0:T(8,128)(2,1)} %gather_256.3.g_ref, f32[1024,768]{1,0:T(8,128)} %get-tuple-element.49.base_ref), custom_call_target="tpu_custom_call" | custom-call | tf_op jit(solution)/shard_map/spread/pallas_call | solution.py:347
  1069.3 8.2 reshape.460
  1082.5 6.9 pad_maximum_fusion.2
  1114.9 8.2 reshape.451
  1128.1 7.3 pad_maximum_fusion.1
  1135.4 19.6 %pad_maximum_fusion.refs_0_ = bf16[32,1728,256]{2,1,0:T(8,128)(2,1)} fusion(bf16[16,1728,256]{2,1,0:T(8,128)(2,1)} %bitcast.190, bf16[16,1728,256]{2,1,0:T(8,128)(2,1)} %bitcast.191), kind=kLoop, calls=%fused_computation.1 | loop fusion | flops 14155776 | bytes 56623104 | tf_op jit(solution)/shard_map/concatenate | solution.py:947
  1155.0 195.0 %scatter_1728.1 = bf16[1728,256]{1,0:T(8,128)(2,1)} custom-call(bf16[32,1728,256]{2,1,0:T(8,128)(2,1)} %pad_maximum_fusion.refs_0_), custom_call_target="tpu_custom_call" | custom-call | tf_op jit(solution)/shard_map/scatter_1728/pallas_call | solution.py:284
  1357.5 20.3 %gather_8.1 = f32[32,8,768]{2,1,0:T(8,128)} custom-call(f32[8,768]{1,0:T(8,128)} %stack.31.x_ref), custom_call_target="tpu_custom_call" | custom-call | tf_op jit(solution)/shard_map/gather_8/pallas_call | solution.py:137
  1382.3 8.7 fusion.59
  1407.0 8.8 fusion.70
  1415.7 5.2 copy.273
  1421.0 11.6 bitcast_subtract_fusion
  1451.0 9.1 fusion.3
  1469.6 8.6 fusion.1
  (407 shorter events, 316.3 us)
Async XLA Ops:
  75.1 90.0 %copy-start.80 = (f32[5,768]{1,0:T(8,128)S(1)}, f32[5,768]{1,0:T(8,128)}, u32[]{:S(2)}) copy-start(f32[5,768]{1,0:T(8,128)} %param.25) | copy-start | bytes 46084
  165.7 134.9 %copy-start.82 = (f32[768]{0:T(1024)}, f32[768]{0:T(1024)S(1)}, u32[]{:S(2)}) copy-start(f32[768]{0:T(1024)S(1)} %get-tuple-element.130) | copy-start | bytes 9220
  392.1 8.1 copy-start.34
  401.5 7.4 copy-start.40
  408.9 462.9 %copy-start.96 = (f32[256]{0:T(256)}, f32[256]{0:T(256)S(1)}, u32[]{:S(2)}) copy-start(f32[256]{0:T(256)S(1)} %add_rsqrt_fusion.2) | copy-start | bytes 3076
  473.2 22.8 %copy-start.9 = (f32[256,768]{1,0:T(8,128)}, f32[256,768]{1,0:T(8,128)S(1)}, u32[]{:S(2)}) copy-start(f32[256,768]{1,0:T(8,128)S(1)} %get-tuple-element.197) | copy-start | bytes 2359300
  487.9 7.5 copy-start.5
  602.6 31.1 %copy-start.78 = (s32[1,2,4,4,256]{4,3,2,1,0:T(4,128)S(1)}, s32[1,2,4,4,256]{4,3,2,1,0:T(4,128)}, u32[]{:S(2)}) copy-start(s32[1,2,4,4,256]{4,3,2,1,0:T(4,128)} %get-tuple-element.174) | copy-start | bytes 98308
  602.6 31.1 %copy-start.77 = (s32[1,2,4,4,256]{4,3,2,1,0:T(4,128)S(1)}, s32[1,2,4,4,256]{4,3,2,1,0:T(4,128)}, u32[]{:S(2)}) copy-start(s32[1,2,4,4,256]{4,3,2,1,0:T(4,128)} %get-tuple-element.175) | copy-start | bytes 98308
  812.3 7.7 slice-start.2
  813.9 6.1 slice-start.3
  813.9 6.1 copy-start.10
  822.6 49.3 %copy-start.22 = (f32[256,768]{1,0:T(8,128)}, f32[256,768]{1,0:T(8,128)S(1)}, u32[]{:S(2)}) copy-start(f32[256,768]{1,0:T(8,128)S(1)} %subtract_add_fusion.2) | copy-start | bytes 2359300
  870.5 6.3 slice-start
  880.1 62.1 %copy-start.24 = (f32[256,768]{1,0:T(8,128)}, f32[256,768]{1,0:T(8,128)S(1)}, u32[]{:S(2)}) copy-start(f32[256,768]{1,0:T(8,128)S(1)} %subtract_add_fusion) | copy-start | bytes 2359300
  928.3 6.9 copy-start.55
  1058.3 5.2 copy-start.23
  1058.3 5.2 copy-start.51
  1069.3 12.6 slice-start.4
  1082.5 7.0 copy-start.35
  1082.5 7.0 copy-start.45
  1104.0 5.2 copy-start.25
  1104.0 5.2 copy-start.49
  1114.9 12.6 slice-start.6
  1155.0 200.6 %copy-start.98 = (f32[1,256]{1,0:T(1,128)S(1)}, f32[1,256]{1,0:T(1,128)}, u32[]{:S(2)}) copy-start(f32[1,256]{1,0:T(1,128)} %get-tuple-element.50) | copy-start | bytes 3076
  1155.0 201.8 %copy-start.89 = (f32[1,768]{1,0:T(1,128)S(1)}, f32[1,768]{1,0:T(1,128)}, u32[]{:S(2)}) copy-start(f32[1,768]{1,0:T(1,128)} %stack.26) | copy-start | bytes 9220
  1155.0 201.8 %copy-start.90 = (f32[1,768]{1,0:T(1,128)S(1)}, f32[1,768]{1,0:T(1,128)}, u32[]{:S(2)}) copy-start(f32[1,768]{1,0:T(1,128)} %stack.27) | copy-start | bytes 9220
  1155.0 201.8 %copy-start.91 = (f32[1,768]{1,0:T(1,128)S(1)}, f32[1,768]{1,0:T(1,128)}, u32[]{:S(2)}) copy-start(f32[1,768]{1,0:T(1,128)} %stack.28) | copy-start | bytes 9220
  1155.0 201.8 %copy-start.92 = (f32[1,768]{1,0:T(1,128)S(1)}, f32[1,768]{1,0:T(1,128)}, u32[]{:S(2)}) copy-start(f32[1,768]{1,0:T(1,128)} %stack.29) | copy-start | bytes 9220
  1155.0 201.8 %copy-start.93 = (f32[1,768]{1,0:T(1,128)S(1)}, f32[1,768]{1,0:T(1,128)}, u32[]{:S(2)}) copy-start(f32[1,768]{1,0:T(1,128)} %stack.30) | copy-start | bytes 9220
  1382.3 8.7 copy-start.36
  1469.6 13.7 copy-start.1
  (75 other events, 213.2 us)

commit v2 on v1

--- a/solution.py
+++ b/solution.py
@@ -141,10 +141,8 @@
         scratch_shapes=[pltpu.SemaphoreType.DMA((nsend,)),pltpu.SemaphoreType.DMA((len(parts),n)),pltpu.SemaphoreType.DMA((1,))],
         compiler_params=pltpu.CompilerParams(collective_id=cid,has_side_effects=True),name=f"gather_{R}")(x)
 
-def rs_kernel(B,H,parts,by_section,ranges,*refs):
-    n_in=len(ranges)
-    p_refs=refs[:n_in]; o_ref=refs[n_in]
-    q,r1,ya,xa,za,xb,zb,yb,lsem,psem_s,psem_r,ssem,ya_s,xa_s,za_s,xb_s,zb_s,yb_s=refs[n_in+1:]
+def rs_kernel(B,H,parts,by_section,p_ref,o_ref,*refs):
+    q,r1,ya,xa,za,xb,zb,yb,lsem,psem_s,psem_r,ssem,ya_s,xa_s,za_s,xb_s,zb_s,yb_s=refs
     s=lax.axis_index("section"); b=lax.axis_index("blk"); h=lax.axis_index("shard")
     x=h&1; y=h>>1
     part=(1-s,b,h); xn=(s,b,h^1); yn=(s,b,h^2); lf=(s,b-1,h); rt=(s,b+1,h)
@@ -157,25 +155,28 @@
     @pl.when(has_r)
     def _(): pl.semaphore_signal(bar,inc=1,device_id=rt,device_id_type=MESH)
     (a0,an),(b0,bn)=parts
+    R=an+bn
+    A=pl.ds(a0,an); Bp=pl.ds(b0,bn)
     def slot(bb,hh,ss):
         return (ss*B+bb)*H+hh if by_section else (bb*H+hh)*2+ss
+    low=b<B//2
+    order=[]
+    for i in range(B-1):
+        down=B-1-i
+        order.append(jnp.where(low,down-(down<=b).astype(jnp.int32),i+(i>=b).astype(jnp.int32)))
+    order.append(b)
     hs=[h^3,h^2,h^1,h]
-    order=[(d,sg,k) for k in range(4) for d in range(B-1,-1,-1) for sg in ((1,-1) if d else (1,))]
-    N=B*H
-    def src(bb,hh,ss):
-        return p_refs[0].at[slot(bb,hh,ss)]
-    seq=[(bb,k) for k in range(4) for bb in range(B)]
-    loads=[]
-    for i,(bb,k) in enumerate(seq):
-        hh=hs[k]
-        cp=pltpu.make_async_copy(src(bb,hh,s),q.at[bb*H+hh],lsem.at[i]); cp.start()
-        loads.append(cp)
+    loads={}
+    for i,t in enumerate(order):
+        for k in range(4):
+            cp=pltpu.make_async_copy(p_ref.at[slot(t,hs[k],s)],q.at[t*H+hs[k]],lsem.at[i*4+k]); cp.start()
+            loads[i,k]=cp
     pl.semaphore_wait(bar,3+has_l.astype(jnp.int32)+has_r.astype(jnp.int32))
-    psend=[]
-    for i,(bb,k) in enumerate(seq):
-        hh=hs[k]
-        cp=remote(src(bb,hh,1-s),r1.at[bb*H+hh],psem_s.at[i],psem_r.at[i],part); cp.start()
-        psend.append(cp)
+    psend={}
+    for i,t in enumerate(order):
+        for k in range(4):
+            cp=remote(p_ref.at[slot(t,hs[k],1-s)],r1.at[t*H+hs[k]],psem_s.at[i*4+k],psem_r.at[i*4+k],part); cp.start()
+            psend[i,k]=cp
     pend=[]; late=[]
     def flush():
         while late:
@@ -191,83 +192,75 @@
         def _(i):
             r=pl.ds(pl.multiple_of(i*step,step),step)
             dst[r,:]=dst[r,:]+a[r,:]
-    A=pl.ds(a0,an); Bp=pl.ds(b0,bn)
     def got(dst,sem):
         remote(dst,dst,ssem.at[0],sem,part).wait_recv()
-    R=an+bn
-    for i,(bb,k) in enumerate(seq):
-        hh=hs[k]
-        loads[i].wait(); got(r1.at[bb*H+hh],psem_r.at[i])
-        add(q.at[bb*H+hh],r1.at[bb*H+hh],R)
+    def first(i):
+        t=order[i]
+        for k in range(4):
+            hh=hs[k]
+            loads[i,k].wait(); psend[i,k].wait_recv()
+            add(q.at[t*H+hh],r1.at[t*H+hh],R)
+            flush()
+            if k in (0,1):
+                xx=(x^1) if k==0 else x
+                queue(None,q.at[t*H+hh,A],ya.at[t*2+xx],ya_s.at[t*2+xx],yn)
+            if k in (0,2):
+                yy=(y^1) if k==0 else y
+                queue(None,q.at[t*H+hh,Bp],xb.at[t*2+yy],xb_s.at[t*2+yy],xn)
+    def second(i):
+        t=order[i]
+        xx=x^1
+        got(ya.at[t*2+xx],ya_s.at[t*2+xx])
+        add(q.at[t*H+hs[2],A],ya.at[t*2+xx],an)
         flush()
-        if k in (0,1):
-            xx=(x^1) if k==0 else x
-            queue(None,q.at[bb*H+hh,A],ya.at[bb*2+xx],ya_s.at[bb*2+xx],yn)
-        if k in (0,2):
-            yy=(y^1) if k==0 else y
-            queue(None,q.at[bb*H+hh,Bp],xb.at[bb*2+yy],xb_s.at[bb*2+yy],xn)
-    flush()
-    for bb in range(B):
-        for kk in range(2):
-            xx=(x^1) if kk==0 else x
-            hA=(h^1) if kk==0 else h
-            yy=(y^1) if kk==0 else y
-            hB=(h^2) if kk==0 else h
-            if kk==0:
-                got(ya.at[bb*2+xx],ya_s.at[bb*2+xx])
-                add(q.at[bb*H+hA,A],ya.at[bb*2+xx],an)
-                flush()
-                queue(None,q.at[bb*H+hA,A],xa.at[bb],xa_s.at[bb],xn)
-            got(xb.at[bb*2+yy],xb_s.at[bb*2+yy])
-            add(q.at[bb*H+hB,Bp],xb.at[bb*2+yy],bn)
+        queue(None,q.at[t*H+hs[2],A],xa.at[t],xa_s.at[t],xn)
+        got(xb.at[t*2+(y^1)],xb_s.at[t*2+(y^1)])
+        add(q.at[t*H+hs[1],Bp],xb.at[t*2+(y^1)],bn)
+        flush()
+        got(ya.at[t*2+x],ya_s.at[t*2+x])
+        add(q.at[t*H+h,A],ya.at[t*2+x],an)
+        got(xb.at[t*2+y],xb_s.at[t*2+y])
+        add(q.at[t*H+h,Bp],xb.at[t*2+y],bn)
+    lines=[(hs[1],Bp,bn,lambda d,t: zb.at[(d*B+t)*2+(y^1)],lambda d,t: zb_s.at[(d*B+t)*2+(y^1)]),
+           (h,Bp,bn,lambda d,t: zb.at[(d*B+t)*2+y],lambda d,t: zb_s.at[(d*B+t)*2+y]),
+           (h,A,an,lambda d,t: za.at[d*B+t],lambda d,t: za_s.at[d*B+t])]
+    def third(i):
+        t=order[i]
+        for j,(hh,rows,n,zr,zs) in enumerate(lines):
+            if j==2:
+                got(xa.at[t],xa_s.at[t])
+                add(q.at[t*H+h,A],xa.at[t],an)
+            for d,c,hin,dev in ((0,t>b,has_l,rt),(1,t<b,has_r,lf)):
+                @pl.when(jnp.logical_and(c,hin))
+                def _():
+                    got(zr(d,t),zs(d,t))
+                    add(q.at[t*H+hh,rows],zr(d,t),n)
             flush()
-    for bb in range(B):
-        got(ya.at[bb*2+x],ya_s.at[bb*2+x])
-        add(q.at[bb*H+h,A],ya.at[bb*2+x],an)
-    def line_step(qref_of,zref_of,zsem_of,nn,d,sg,pre=None):
-        t=b+sg*d
-        c=(t<B) if sg>0 else (t>=0)
-        hin=has_l if sg>0 else has_r
-        dn=0 if sg>0 else 1
-        dev=rt if sg>0 else lf
-        def run():
-            if pre is not None: pre(t)
+            for d,c,hin,dev in ((0,t>b,has_l,rt),(1,t<b,has_r,lf)):
+                queue(c,q.at[t*H+hh,rows],zr(d,t),zs(d,t),dev)
+    def last(j):
+        hh,rows,n,zr,zs=lines[j]
+        for d,hin in ((0,has_l),(1,has_r)):
             @pl.when(hin)
             def _():
-                got(zref_of(dn,t),zsem_of(dn,t))
-                add(qref_of(t),zref_of(dn,t),nn)
-        pl.when(c)(run)
-        flush()
-        queue(c,qref_of(t),zref_of(dn,t),zsem_of(dn,t),dev)
-    def final(qref_of,zref_of,zsem_of,nn):
-        for dn,hin in ((0,has_l),(1,has_r)):
-            @pl.when(hin)
-            def _():
-                got(zref_of(dn,b),zsem_of(dn,b))
-                add(qref_of(b),zref_of(dn,b),nn)
-    def pre_a(t):
-        got(xa.at[t],xa_s.at[t])
-        add(q.at[t*H+h,A],xa.at[t],an)
-    fB=[]
-    for yy,hh in ((y^1,h^2),(y,h)):
-        fB.append((lambda t,hh=hh: q.at[t*H+hh,Bp], lambda dn,t,yy=yy: zb.at[(dn*B+t)*2+yy], lambda dn,t,yy=yy: zb_s.at[(dn*B+t)*2+yy], bn))
-    fA=(lambda t: q.at[t*H+h,A], lambda dn,t: za.at[dn*B+t], lambda dn,t: za_s.at[dn*B+t], an)
-    for d in range(B-1,0,-1):
-        for sg in (1,-1):
-            line_step(*fB[0],d,sg)
-            line_step(*fB[1],d,sg)
-            line_step(*fA,d,sg,pre_a)
+                got(zr(d,b),zs(d,b))
+                add(q.at[b*H+hh,rows],zr(d,b),n)
+    for i in range(B+2):
+        if i<B: first(i)
+        if 1<=i<B+1: second(i-1)
+        if 2<=i<B+1: third(i-2)
     flush()
-    pre_a(b)
-    final(*fB[0])
-    queue(None,q.at[b*H+(h^2),Bp],yb,yb_s.at[0],yn)
-    final(*fA)
+    last(0)
+    queue(None,q.at[b*H+hs[1],Bp],yb,yb_s.at[0],yn)
+    got(xa.at[b],xa_s.at[b])
+    add(q.at[b*H+h,A],xa.at[b],an)
     flush()
-    final(*fB[1])
+    last(1)
+    last(2)
     got(yb,yb_s.at[0])
     add(q.at[b*H+h,Bp],yb,bn)
     o_ref[...]=q[b*H+h]
-    for cp in psend: cp.wait_send()
+    for cp in psend.values(): cp.wait_send()
     for c,cp in pend:
         if c is None: cp.wait_send()
         else: pl.when(c)(cp.wait_send)
@@ -280,14 +273,73 @@
     D=lambda *s: pltpu.SemaphoreType.DMA(s)
     N=B*H
     an,bn=a,R-a
-    nsend=8*B+B+6*(B-1)+8
-    return pl.pallas_call(functools.partial(rs_kernel,B,H,parts,by_section,((0,n),)),
+    nsend=4*B+B+6*(B-1)+2
+    return pl.pallas_call(functools.partial(rs_kernel,B,H,parts,by_section),
         out_shape=jax.ShapeDtypeStruct((R,C),p.dtype),
         in_specs=[pl.BlockSpec(memory_space=pl.ANY)],
         out_specs=pl.BlockSpec(memory_space=pltpu.VMEM),
         scratch_shapes=[V(N,R,C),V(N,R,C),V(2*B,an,C),V(B,an,C),V(2*B,an,C),V(2*B,bn,C),V(4*B,bn,C),V(bn,C),
            D(N),D(N),D(N),D(nsend),D(2*B),D(B),D(2*B),D(2*B),D(4*B),D(1)],
         compiler_params=pltpu.CompilerParams(collective_id=cid,has_side_effects=True,vmem_limit_bytes=63*1024*1024),name=f"scatter_{R}")(p)
+
+def swap_kernel(n,join,x_ref,o_ref,got,total,ssem,rsem,ssem2,rsem2):
+    B,H=lax.axis_size("blk"),lax.axis_size("shard")
+    me=(lax.axis_index("blk")*H+lax.axis_index("shard"))*2+lax.axis_index("section")
+    bar=pltpu.get_barrier_semaphore()
+    def place(k):
+        t=(me+k)%n
+        return t,(t%2,t//(2*H),(t//2)%H)
+    @pl.loop(1,n)
+    def _(k):
+        pl.semaphore_signal(bar,inc=1,device_id=place(k)[1],device_id_type=MESH)
+    pl.semaphore_wait(bar,n-1)
+    if join is None:
+        def copy(k):
+            return remote(x_ref,o_ref.at[me],ssem.at[k],rsem.at[k],place(k)[1])
+        @pl.loop(1,n)
+        def _(k): copy(k).start()
+        o_ref[me]=x_ref[...]
+        @pl.loop(1,n)
+        def _(k): copy(k).wait()
+        return
+    def piece(k):
+        t,dev=place(k)
+        return remote(x_ref.at[t],got.at[me],ssem.at[k],rsem.at[k],dev)
+    def spread(k):
+        return remote(total,o_ref.at[me],ssem2.at[k],rsem2.at[k],place(k)[1])
+    @pl.loop(1,n)
+    def _(k): piece(k).start()
+    got[me]=x_ref[me]
+    @pl.loop(1,n)
+    def _(k): piece(k).wait()
+    total[...]=join(got)
+    o_ref[me]=total[...]
+    @pl.loop(1,n)
+    def _(k): spread(k).start()
+    @pl.loop(1,n)
+    def _(k): spread(k).wait()
+
+def swap_all(x,n,cid,join=None,out_rows=None,name="swap"):
+    whole=pl.BlockSpec(memory_space=pltpu.VMEM)
+    D=pltpu.SemaphoreType.DMA
+    C=x.shape[-1]
+    R=x.shape[-2]
+    out=(n,R,C) if join is None else (n,out_rows,C)
+    small=(8,128) if join is None else (out_rows,C)
+    return pl.pallas_call(functools.partial(swap_kernel,n,join),
+        out_shape=jax.ShapeDtypeStruct(out,x.dtype),in_specs=[whole],out_specs=whole,
+        scratch_shapes=[pltpu.VMEM((8,128) if join is None else (n,R,C),x.dtype),pltpu.VMEM(small,x.dtype),D((n,)),D((n,)),D((n,)),D((n,))],
+        compiler_params=pltpu.CompilerParams(collective_id=cid,has_side_effects=True),name=name)(x)
+
+
+def join_stats(got):
+    tops=got[:,0:1,:]
+    largest=jnp.max(tops,axis=0)
+    return largest+jnp.log(jnp.sum(got[:,1:2,:]*jnp.exp(tops-largest),axis=0))
+
+
+def join_sum(got):
+    return jnp.sum(got[...],axis=0)
 
 
 def gather_all(value, cid, by_section=False):
@@ -729,136 +781,414 @@
     return quads.reshape(-1, count * BS * BS // QUAD, QUAD)
 
 
-def quads_to_matrices(quads):
-    matrices, offset = [], 0
-    for rows, cols in matrix_layout():
-        r, c = rows // BS, cols // QUAD
-        part = quads[offset : offset + r * c].reshape(r, c, BS, QUAD)
-        matrices.append(part.transpose(0, 2, 1, 3).reshape(rows, cols))
-        offset += r * c
-    return matrices
-
-
-def matrices_to_quads(matrices):
-    parts = []
-    for matrix, (rows, cols) in zip(matrices, matrix_layout()):
-        r, c = rows // BS, cols // QUAD
-        parts.append(
-            matrix.reshape(r, BS, c, QUAD).transpose(0, 2, 1, 3).reshape(r * c, BS, QUAD)
-        )
-    return jnp.concatenate(parts, axis=0)
-
-
-def rms_scale(states, gain_row):
-    return (
-        states * lax.rsqrt(jnp.mean(states * states, axis=-1, keepdims=True) + norm_eps) * gain_row
-    )
-
-
-def rms_back(states, gain_row, grad_out):
-    inverse = lax.rsqrt(jnp.mean(states * states, axis=-1, keepdims=True) + norm_eps)
-    weighted = grad_out * gain_row
-    grad_in = inverse * weighted - states * inverse * inverse * inverse * jnp.mean(
-        weighted * states, axis=-1, keepdims=True
-    )
-    return (grad_in, jnp.sum(grad_out * states * inverse, axis=0))
-
-
 def rope_tables(positions):
     half_dim = HEAD_DIM // 2
     frequency = rope_base ** (-jnp.arange(half_dim, dtype=f32) * 2.0 / HEAD_DIM)
     angles = positions.astype(f32)[:, None] * frequency[None, :]
     cosine, sine = jnp.cos(angles), jnp.sin(angles)
     return (
-        jnp.concatenate([cosine, cosine], axis=-1)[:, None, :],
-        jnp.concatenate([sine, sine], axis=-1)[:, None, :],
-    )
-
-
-def rotate(values, cosine, sine):
-    half_dim = HEAD_DIM // 2
-    turned = jnp.concatenate([-values[..., half_dim:], values[..., :half_dim]], axis=-1)
-    return values * cosine + turned * sine
-
-
-def rotate_back(grads, cosine, sine):
-    half_dim = HEAD_DIM // 2
-    scaled = grads * sine
-    turned = jnp.concatenate([scaled[..., half_dim:], -scaled[..., :half_dim]], axis=-1)
-    return grads * cosine + turned
-
-
-def layer_forward(states, weights, gain_first, gain_second, tables, seg_rows, reach, blocks, cid):
-    w_qkv, w_out, w_gate_up, w_down = weights
-    rows = states.shape[0]
-    normed = rms_scale(states, gain_first).astype(bf16)
-    projected = jnp.dot(normed, w_qkv, preferred_element_type=f32)
-
-    def turned(part):
-        return rotate(part.reshape(rows, HEADS, HEAD_DIM), *tables).astype(bf16).reshape(rows, D)
-
-    q = turned(projected[:, :D])
-    k = turned(projected[:, D : 2 * D])
-    v = projected[:, 2 * D :].astype(bf16)
-    total, accum, far_k, far_v = attend(q, k, v, seg_rows, reach, blocks, cid)
-    attended = (accum / total).astype(bf16)
-    mixed = states + jnp.dot(attended, w_out, preferred_element_type=f32)
-    normed_mid = rms_scale(mixed, gain_second).astype(bf16)
-    gate_up = jnp.dot(normed_mid, w_gate_up, preferred_element_type=f32)
-    gate, upper = gate_up[:, :FF], gate_up[:, FF:]
-    hidden = (jax.nn.silu(gate) * upper).astype(bf16)
-    output = mixed + jnp.dot(hidden, w_down, preferred_element_type=f32)
-    return output, (
-        states, normed, q, k, v, far_k, far_v, total, accum, attended, mixed, normed_mid, gate,
-        upper, hidden,
-    )
-
-
-def layer_backward(cache, grad_out, weights, gain_first, gain_second, tables, seg_rows, reach, blocks, cid):
-    (
-        states, normed, q, k, v, far_k, far_v, total, accum, attended, mixed, normed_mid, gate,
-        upper, hidden,
-    ) = cache
-    w_qkv, w_out, w_gate_up, w_down = weights
-    rows = states.shape[0]
-
-    def outer(left_side, right_side):
-        return jnp.einsum(
-            "rd,rf->df", left_side, right_side, preferred_element_type=f32
-        ).astype(bf16)
-
-    def through(grad, weight):
-        return jnp.einsum("rf,df->rd", grad, weight, preferred_element_type=f32)
-
-    grad_low = grad_out.astype(bf16)
-    grad_w_down = outer(hidden, grad_low)
-    grad_hidden = through(grad_low, w_down)
-    sig = jax.nn.sigmoid(gate)
-    grad_gate = grad_hidden * upper * sig * (1.0 + gate * (1.0 - sig))
-    grad_up = grad_hidden * gate * sig
-    grad_gate_up = jnp.concatenate([grad_gate, grad_up], axis=-1).astype(bf16)
-    grad_w_gate_up = outer(normed_mid, grad_gate_up)
-    grad_mid_norm, grad_gain_second = rms_back(mixed, gain_second, through(grad_gate_up, w_gate_up))
-    grad_mixed = grad_out + grad_mid_norm
-    grad_att = grad_mixed.astype(bf16)
-    grad_w_out = outer(attended, grad_att)
-    grad_attended = through(grad_att, w_out)
-    grad_q, grad_k, grad_v = attend_back(
-        q, k, v, far_k, far_v, total, accum, grad_attended, seg_rows, reach, blocks, cid
-    )
-
-    def unturned(part):
-        return rotate_back(part.reshape(rows, HEADS, HEAD_DIM), *tables).reshape(rows, D)
-
-    grad_qkv = jnp.concatenate([unturned(grad_q), unturned(grad_k), grad_v], axis=-1).astype(bf16)
-    grad_w_qkv = outer(normed, grad_qkv)
-    grad_in_norm, grad_gain_first = rms_back(states, gain_first, through(grad_qkv, w_qkv))
-    return (
-        grad_mixed + grad_in_norm,
-        (grad_w_qkv, grad_w_out, grad_w_gate_up, grad_w_down),
-        grad_gain_first,
-        grad_gain_second,
-    )
+        jnp.concatenate([cosine, cosine] * 4, axis=-1),
+        jnp.concatenate([-sine, sine] * 4, axis=-1),
+    )
+
+
+QKV, OUT, GATE, DOWN = (0, 12, 9), (108, 12, 3), (144, 12, 16), (336, 32, 3)
+QUADS = 432
+WHOLE = pl.BlockSpec(memory_space=pltpu.VMEM)
+LEFT = pl.BlockSpec(memory_space=pl.ANY)
+
+
+def struct(shape, dtype=f32):
+    return jax.ShapeDtypeStruct(shape, dtype)
+
+
+def column(buf, kind, c, base=0):
+    offset, rows, cols = kind
+    return jnp.concatenate([buf[offset - base + r * cols + c] for r in range(rows)], axis=0)
+
+
+def band(buf, kind, r, base=0):
+    offset, _, cols = kind
+    return jnp.concatenate(
+        [
+            jnp.concatenate([buf[offset - base + (4 * r + i) * cols + c] for c in range(cols)], axis=1)
+            for i in range(4)
+        ],
+        axis=0,
+    )
+
+
+def lanes_of(c):
+    return pl.ds(pl.multiple_of(c * QUAD, QUAD), QUAD)
+
+
+def dot(left_side, right_side):
+    return jnp.dot(left_side, right_side, preferred_element_type=f32)
+
+
+def dot_nt(left_side, right_side):
+    return lax.dot_general(
+        left_side, right_side, (((1,), (1,)), ((), ())), preferred_element_type=f32
+    )
+
+
+def norm_of(x):
+    return lax.rsqrt(jnp.mean(x * x, axis=-1, keepdims=True) + norm_eps)
+
+
+def norm_back(x, gain, grad):
+    inverse = norm_of(x)
+    weighted = grad * gain
+    grad_in = inverse * weighted - x * (inverse * inverse * inverse) * jnp.mean(
+        weighted * x, axis=-1, keepdims=True
+    )
+    return grad_in, jnp.sum(grad * x * inverse, axis=0, keepdims=True)
+
+
+def swapped(u):
+    lane = lax.broadcasted_iota(jnp.int32, u.shape, 1)
+    half = HEAD_DIM // 2
+    return jnp.where(
+        lane % HEAD_DIM < half, pltpu.roll(u, u.shape[1] - half, 1), pltpu.roll(u, half, 1)
+    )
+
+
+def load_quads(w_ref, layer, kinds, bufs, sem):
+    copies = []
+    for i, ((offset, rows, cols), buf) in enumerate(zip(kinds, bufs)):
+        copy = pltpu.make_async_copy(w_ref.at[layer, pl.ds(offset, rows * cols)], buf, sem.at[i])
+        copy.start()
+        copies.append(copy)
+    return copies
+
+
+def quad_buffers(kinds):
+    return [pltpu.VMEM((rows * cols, BS, QUAD), bf16) for _, rows, cols in kinds] + [
+        pltpu.SemaphoreType.DMA((len(kinds),))
+    ]
+
+
+def big(**extra):
+    return pltpu.CompilerParams(vmem_limit_bytes=VMEM_MAX, **extra)
+
+
+def qkv_kernel(layer, x_ref, gain_ref, cos_ref, sin_ref, w_ref, a_ref, q_ref, k_ref, v_ref, wq, sem):
+    (copy,) = load_quads(w_ref, layer, (QKV,), (wq,), sem)
+    x = x_ref[...]
+    a_ref[...] = (x * norm_of(x) * gain_ref[...]).astype(bf16)
+    copy.wait()
+    for i, out in enumerate((q_ref, k_ref, v_ref)):
+
+        @pl.loop(0, 3)
+        def _(c):
+            part = dot(a_ref[...], column(wq, QKV, 3 * i + c, QKV[0]))
+            if i < 2:
+                part = part * cos_ref[...] + swapped(part) * sin_ref[...]
+            out[:, lanes_of(c)] = part.astype(bf16)
+
+
+def qkv_forward(layer, x, gain, cosine, sine, quads):
+    tokens = x.shape[0]
+    low = struct((tokens, D), bf16)
+    return pl.pallas_call(
+        functools.partial(qkv_kernel, layer),
+        out_shape=(low,) * 4,
+        in_specs=[WHOLE] * 4 + [LEFT],
+        out_specs=(WHOLE,) * 4,
+        scratch_shapes=quad_buffers((QKV,)),
+        compiler_params=big(),
+        name="qkv",
+    )(x, gain, cosine, sine, quads)
+
+
+def mlp_kernel(layer, last, x_ref, acc_ref, tot_ref, gain_ref, final_ref, w_ref, out_ref, att_ref,
+               mixed_ref, nm_ref, gate_ref, up_ref, hid_ref, nf_ref, wo, wg, wd, sem):
+    copies = load_quads(w_ref, layer, (OUT, GATE, DOWN), (wo, wg, wd), sem)
+    att_ref[...] = (acc_ref[...] / tot_ref[...]).astype(bf16)
+    copies[0].wait()
+
+    @pl.loop(0, 3)
+    def _(c):
+        lanes = lanes_of(c)
+        mixed_ref[:, lanes] = x_ref[:, lanes] + dot(att_ref[...], column(wo, OUT, c, OUT[0]))
+
+    mixed = mixed_ref[...]
+    nm_ref[...] = (mixed * norm_of(mixed) * gain_ref[...]).astype(bf16)
+    copies[1].wait()
+
+    @pl.loop(0, FF // QUAD)
+    def _(c):
+        lanes = lanes_of(c)
+        gate = dot(nm_ref[...], column(wg, GATE, c, GATE[0]))
+        upper = dot(nm_ref[...], column(wg, GATE, c + FF // QUAD, GATE[0]))
+        gate_ref[:, lanes] = gate
+        up_ref[:, lanes] = upper
+        hid_ref[:, lanes] = (gate / (1.0 + jnp.exp(-gate)) * upper).astype(bf16)
+
+    copies[2].wait()
+
+    @pl.loop(0, 3)
+    def _(c):
+        lanes = lanes_of(c)
+        out_ref[:, lanes] = mixed_ref[:, lanes] + dot(hid_ref[...], column(wd, DOWN, c, DOWN[0]))
+
+    if last:
+        out = out_ref[...]
+        nf_ref[...] = (out * norm_of(out) * final_ref[...]).astype(bf16)
+    else:
+        nf_ref[...] = jnp.zeros_like(nf_ref)
+
+
+def mlp_forward(layer, last, x, accum, total, gain, final_gain, quads):
+    tokens = x.shape[0]
+    wide, low = struct((tokens, D)), struct((tokens, D), bf16)
+    return pl.pallas_call(
+        functools.partial(mlp_kernel, layer, last),
+        out_shape=(
+            wide, low, wide, low, struct((tokens, FF)), struct((tokens, FF)),
+            struct((tokens, FF), bf16), low,
+        ),
+        in_specs=[WHOLE] * 5 + [LEFT],
+        out_specs=(WHOLE,) * 8,
+        scratch_shapes=quad_buffers((OUT, GATE, DOWN)),
+        compiler_params=big(),
+        name="mlp",
+    )(x, accum, total, gain, final_gain, quads)
+
+
+def put_quads(buf, kind, c, value, base):
+    offset, rows, cols = kind
+    for r in range(rows):
+        buf[offset - base + r * cols + c] = value[r * BS : (r + 1) * BS].astype(bf16)
+
+
+def mlp_back_kernel(layer, last, first_call, *refs):
+    (gy_ref, h_ref, mixed_ref, nm_ref, gate_ref, up_ref, hid_ref, att_ref, gain_ref, final_ref,
+     w_ref) = refs[:11]
+    (p_ref, gm_ref, gatt_ref, gg_ref, gf_ref, wo, wg, wd, sem, grads, gl, ggu, turned, gin,
+     out_sem) = refs[11 + (not first_call):]
+    copies = load_quads(w_ref, layer, (DOWN, GATE, OUT), (wd, wg, wo), sem)
+    base = OUT[0]
+    if last:
+        grad, gain_row = norm_back(h_ref[...], final_ref[...], gy_ref[...].astype(f32))
+        gf_ref[...] = gain_row
+    else:
+        grad = gy_ref[...]
+        gf_ref[...] = jnp.zeros_like(gf_ref)
+    gin[...] = grad
+    gl[...] = grad.astype(bf16)
+    copies[0].wait()
+
+    @pl.loop(0, FF // QUAD)
+    def _(r):
+        lanes = lanes_of(r)
+        grad_down = dot(jnp.transpose(hid_ref[:, lanes]), gl[...])
+        for i in range(4):
+            for c in range(3):
+                grads[DOWN[0] - base + (4 * r + i) * 3 + c] = grad_down[
+                    i * BS : (i + 1) * BS, c * QUAD : (c + 1) * QUAD
+                ].astype(bf16)
+        grad_hidden = dot_nt(gl[...], band(wd, DOWN, r, DOWN[0]))
+        gate, upper = gate_ref[:, lanes], up_ref[:, lanes]
+        sig = 1.0 / (1.0 + jnp.exp(-gate))
+        ggu[:, lanes] = (grad_hidden * upper * sig * (1.0 + gate * (1.0 - sig))).astype(bf16)
+        ggu[:, lanes_of(r + FF // QUAD)] = (grad_hidden * gate * sig).astype(bf16)
+
+    def send(i, kind):
+        offset, rows, cols = kind
+        copy = pltpu.make_async_copy(
+            grads.at[pl.ds(offset - base, rows * cols)],
+            p_ref.at[layer, pl.ds(offset, rows * cols)],
+            out_sem.at[i],
+        )
+        copy.start()
+        return copy
+
+    sent = [send(0, DOWN)]
+    turned[...] = jnp.transpose(nm_ref[...])
+    gatt_ref[...] = jnp.zeros_like(gatt_ref)
+    copies[1].wait()
+
+    @pl.loop(0, 2 * FF // QUAD)
+    def _(c):
+        part = ggu[:, lanes_of(c)]
+        put_quads(grads, GATE, c, dot(turned[...], part), base)
+        gatt_ref[...] += dot_nt(part, column(wg, GATE, c, GATE[0]))
+
+    sent.append(send(1, GATE))
+    grad_norm, gain_row = norm_back(mixed_ref[...], gain_ref[...], gatt_ref[...])
+    gg_ref[...] = gain_row
+    grad_mixed = gin[...] + grad_norm
+    gm_ref[...] = grad_mixed
+    gl[...] = grad_mixed.astype(bf16)
+    turned[...] = jnp.transpose(att_ref[...])
+    gatt_ref[...] = jnp.zeros_like(gatt_ref)
+    copies[2].wait()
+
+    @pl.loop(0, 3)
+    def _(c):
+        part = gl[:, lanes_of(c)]
+        put_quads(grads, OUT, c, dot(turned[...], part), base)
+        gatt_ref[...] += dot_nt(part, column(wo, OUT, c, OUT[0]))
+
+    sent.append(send(2, OUT))
+    for copy in sent:
+        copy.wait()
+
+
+def mlp_backward(layer, last, grad, states, cache, gain, final_gain, quads, store):
+    mixed, nm, gate, upper, hidden, att = cache
+    tokens = mixed.shape[0]
+    wide, row = struct((tokens, D)), struct((1, D))
+    kinds = (DOWN, GATE, OUT)
+    buffers = quad_buffers((OUT, GATE, DOWN))
+    operands = [grad, states, mixed, nm, gate, upper, hidden, att, gain, final_gain, quads]
+    aliases = {}
+    if store is not None:
+        operands.append(store)
+        aliases = {11: 0}
+    return pl.pallas_call(
+        functools.partial(mlp_back_kernel, layer, last, store is None),
+        out_shape=(struct((2, QUADS, BS, QUAD), bf16), wide, wide, row, row),
+        in_specs=[WHOLE] * 10 + [LEFT] * (len(operands) - 10),
+        out_specs=(LEFT,) + (WHOLE,) * 4,
+        scratch_shapes=buffers
+        + [
+            pltpu.VMEM((QUADS - OUT[0], BS, QUAD), bf16),
+            pltpu.VMEM((tokens, D), bf16),
+            pltpu.VMEM((tokens, 2 * FF), bf16),
+            pltpu.VMEM((D, tokens), bf16),
+            pltpu.VMEM((tokens, D), f32),
+            pltpu.SemaphoreType.DMA((3,)),
+        ],
+        input_output_aliases=aliases,
+        compiler_params=big(),
+        name="mlp_back",
+    )(*operands)
+
+
+def qkv_back_kernel(layer, dq_ref, dk_ref, dv_ref, a_ref, x_ref, gm_ref, gain_ref, cos_ref, sin_ref,
+                    w_ref, store_ref, p_ref, gx_ref, low_ref, gg_ref, wq, sem, grads, turned, out_sem):
+    (copy,) = load_quads(w_ref, layer, (QKV,), (wq,), sem)
+    turned[...] = jnp.transpose(a_ref[...])
+    gx_ref[...] = jnp.zeros_like(gx_ref)
+    copy.wait()
+    for i, ref in enumerate((dq_ref, dk_ref, dv_ref)):
+
+        @pl.loop(0, 3)
+        def _(c):
+            part = ref[:, lanes_of(c)]
+            if i < 2:
+                part = part * cos_ref[...] - swapped(part) * sin_ref[...]
+            part = part.astype(bf16)
+            put_quads(grads, QKV, 3 * i + c, dot(turned[...], part), QKV[0])
+            gx_ref[...] += dot_nt(part, column(wq, QKV, 3 * i + c, QKV[0]))
+
+    out = pltpu.make_async_copy(
+        grads, p_ref.at[layer, pl.ds(QKV[0], QKV[1] * QKV[2])], out_sem.at[0]
+    )
+    out.start()
+    grad_norm, gain_row = norm_back(x_ref[...], gain_ref[...], gx_ref[...])
+    gg_ref[...] = gain_row
+    grad = gm_ref[...] + grad_norm
+    gx_ref[...] = grad
+    low_ref[...] = grad.astype(bf16)
+    out.wait()
+
+
+def qkv_backward(layer, dq, dk, dv, a, x, grad_mixed, gain, cosine, sine, quads, store):
+    tokens = x.shape[0]
+    return pl.pallas_call(
+        functools.partial(qkv_back_kernel, layer),
+        out_shape=(
+            struct((2, QUADS, BS, QUAD), bf16), struct((tokens, D)), struct((tokens, D), bf16),
+            struct((1, D)),
+        ),
+        in_specs=[WHOLE] * 9 + [LEFT] * 2,
+        out_specs=(LEFT,) + (WHOLE,) * 3,
+        scratch_shapes=quad_buffers((QKV,))
+        + [
+            pltpu.VMEM((QKV[1] * QKV[2], BS, QUAD), bf16),
+            pltpu.VMEM((D, tokens), bf16),
+            pltpu.SemaphoreType.DMA((1,)),
+        ],
+        input_output_aliases={10: 0},
+        compiler_params=big(),
+        name="qkv_back",
+    )(dq, dk, dv, a, x, grad_mixed, gain, cosine, sine, quads, store)
+
+
+def shampoo_kernel(scale_ref, g_ref, w_ref, ls_ref, rs_ref, lr_ref, rr_ref, wn_ref, wl_ref, ln_ref,
+                   rn_ref):
+    factor = scale_ref[0, 0]
+    row = lax.broadcasted_iota(jnp.int32, (QUAD, QUAD), 0)
+    col = lax.broadcasted_iota(jnp.int32, (QUAD, QUAD), 1)
+    same = (row // BS) == (col // BS)
+
+    def diagonal(wide):
+        return jnp.where(same, jnp.concatenate([wide] * 4, axis=0), jnp.zeros((), wide.dtype))
+
+    for j in range(g_ref.shape[0]):
+
+        def side(ref):
+            return jnp.concatenate([ref[4 * j + i] for i in range(4)], axis=1).astype(bf16)
+
+        g = g_ref[j]
+        left = dot_nt(g, diagonal(g)) * (factor * factor * (1.0 - stat_decay))
+        right = lax.dot_general(g, g, (((0,), (0,)), ((), ())), preferred_element_type=f32)
+        right = right * (factor * factor * (1.0 - stat_decay))
+        inner = dot(g, diagonal(side(rr_ref))) * factor
+        step = dot(side(lr_ref), diagonal(inner.astype(bf16)))
+        for i in range(4):
+            cut = slice(i * BS, (i + 1) * BS)
+            n = 4 * j + i
+            ln_ref[n] = stat_decay * ls_ref[n] + left[:, cut]
+            rn_ref[n] = stat_decay * rs_ref[n] + right[cut, cut]
+            new = w_ref[n] - shampoo_rate * step[:, cut]
+            wn_ref[n] = new
+            wl_ref[n] = new.astype(bf16)
+
+
+def shampoo(factor, rows, weights, left_stats, right_stats, left_root, right_root):
+    count = weights.shape[0]
+    quads = 3
+    square = pl.BlockSpec((4 * quads, BS, BS), lambda i: (i, 0, 0))
+    return pl.pallas_call(
+        shampoo_kernel,
+        grid=(count // (4 * quads),),
+        out_shape=(
+            struct((count, BS, BS)), struct((count, BS, BS), bf16), struct((count, BS, BS)),
+            struct((count, BS, BS)),
+        ),
+        in_specs=[
+            pl.BlockSpec(memory_space=pltpu.SMEM),
+            pl.BlockSpec((quads, BS, QUAD), lambda i: (i, 0, 0)),
+        ]
+        + [square] * 5,
+        out_specs=(square,) * 4,
+        name="shampoo",
+    )(
+        factor.reshape(1, 1), rows.reshape(-1, BS, QUAD), weights, left_stats, right_stats,
+        left_root, right_root,
+    )
+
+
+def shampoo_plain(factor, rows, weights, left_stats, right_stats, left_root, right_root):
+    grads = rows_to_blocks(rows.astype(f32)) * factor
+    left_new = stat_decay * left_stats + (1.0 - stat_decay) * jnp.einsum(
+        "bij,bkj->bik", grads, grads, precision=highest
+    )
+    right_new = stat_decay * right_stats + (1.0 - stat_decay) * jnp.einsum(
+        "bji,bjk->bik", grads, grads, precision=highest
+    )
+    direction = jnp.einsum(
+        "bij,bjk->bik",
+        left_root,
+        jnp.einsum("bij,bjk->bik", grads, right_root, precision=highest),
+        precision=highest,
+    )
+    new = weights - shampoo_rate * direction
+    return new, new.astype(bf16), left_new, right_new
 
 
 def adam_step(weight, first, second, grad_in, decay):
@@ -868,6 +1198,35 @@
         first_new / (jnp.sqrt(second_new) + adam_eps) + decay * weight
     )
     return (weight_new, first_new, second_new)
+
+
+def share_ids(packed, cid):
+    blk, shard = lax.axis_size("blk"), lax.axis_size("shard")
+    if blk * shard <= 16:
+        every = swap_all(packed, 2 * blk * shard, cid, name="swap_ids")
+        return every.reshape(blk, shard, 2, *packed.shape)[:, :, 0]
+    return lax.all_gather(packed, ("blk", "shard")).reshape(blk, shard, *packed.shape)
+
+
+def share_stats(top, total, cid):
+    blk, shard = lax.axis_size("blk"), lax.axis_size("shard")
+    devices = 2 * blk * shard
+    if blk * shard <= 16:
+        pair = jnp.concatenate([top, total], axis=1)
+        return swap_all(pair, devices, cid, join_stats, 1, name="swap_stats")[:, 0]
+    largest = lax.pmax(top[:, 0], ORDER)
+    return largest + jnp.log(lax.psum(total[:, 0] * jnp.exp(top[:, 0] - largest), ORDER))
+
+
+def share_sum(small, cid):
+    blk, shard = lax.axis_size("blk"), lax.axis_size("shard")
+    devices = 2 * blk * shard
+    if blk * shard <= 16:
+        lanes = pl.cdiv(small.size, devices * 128) * 128
+        flat = jnp.pad(small.reshape(-1), (0, devices * lanes - small.size))
+        every = swap_all(flat.reshape(devices, 1, lanes), devices, cid, join_sum, 1, name="swap_sum")
+        return every.reshape(-1)[: small.size].reshape(small.shape)
+    return lax.psum(small, ORDER)
 
 
 def on_device(ids, targets, segments, table, table_m, table_v, blocks, left_stats, right_stats,
@@ -891,7 +1250,7 @@
     packed = jnp.stack(
         [ids[:, 0, :], targets[:, 0, :, 0], targets[:, 0, :, 1], seg_own], axis=0
     ).reshape(4 * micro, tok_rows)
-    shared = lax.all_gather(packed, ("blk", "shard")).reshape(blk, shard, 4, micro, tok_rows)
+    shared = share_ids(packed, 8).reshape(blk, shard, 4, micro, tok_rows)
     shared = shared.transpose(2, 3, 1, 0, 4).reshape(4, devices, tokens)
     first_row = ((section * blk + blk_index) * shard + shard_index) * vocab
     local_ids, local_first, local_second = (shared[i] - first_row for i in range(3))
@@ -905,73 +1264,74 @@
 
     rows_low = blocks_to_rows(blocks[0].astype(bf16))
     gathered = gather_all(rows_low, 0, by_section=True)
-    gathered = gathered.reshape(2, blk * shard * rows_low.shape[0], QUAD)
+    weights = jnp.stack([rows_to_quads(part, own_blocks) for part in gathered.reshape(
+        2, blk * shard * rows_low.shape[0], QUAD)]) if own_blocks % 4 else gathered.reshape(
+        2, QUADS, BS, QUAD)
     table_low = jnp.pad(table.astype(bf16), ((0, padded - vocab), (0, 0)))
     looked = lookup(local_ids, table_low)
     states = scatter_all(looked, 1).astype(f32)
 
-    weights = [quads_to_matrices(rows_to_quads(gathered[l], own_blocks)) for l in range(2)]
     positions = (mine % seq_blocks) * tokens + jnp.arange(tokens, dtype=jnp.int32)
-    tables = rope_tables(positions)
+    cosine, sine = rope_tables(positions)
+    rows_of_gain = [gains[i : i + 1] for i in range(5)]
     caches = []
     for l in range(2):
-        states, cache = layer_forward(
-            states, weights[l], gains[2 * l], gains[2 * l + 1], tables, seg_rows, reach, seq_blocks, 2
+        a, q, k, v = qkv_forward(l, states, rows_of_gain[2 * l], cosine, sine, weights)
+        total, accum, far_k, far_v = attend(q, k, v, seg_rows, reach, seq_blocks, 2)
+        out, att, mixed, nm, gate, upper, hidden, normed_own = mlp_forward(
+            l, l == 1, states, accum, total, rows_of_gain[2 * l + 1], rows_of_gain[4], weights
         )
-        caches.append(cache)
-    final_gain = gains[gains.shape[0] - 1]
-    normed_own = rms_scale(states, final_gain).astype(bf16)
+        caches.append(
+            (states, a, q, k, v, far_k, far_v, total, accum, (mixed, nm, gate, upper, hidden, att))
+        )
+        states = out
     normed = gather_all(normed_own, 3)
     top, spread_sum = vocab_stats(normed, table_low, vocab)
-    stats = gather_all(jnp.concatenate([top[:, 0], spread_sum[:, 0]], axis=0), 4)
-    tops, sums = stats[:, :devices], stats[:, devices:]
-    largest = jnp.max(tops, axis=0)
-    log_total = largest + jnp.log(jnp.sum(sums * jnp.exp(tops - largest), axis=0))
+    log_total = share_stats(top, spread_sum, 4)
     inv_count = 1.0 / all_tokens
     grad_rows, head_term, picks = vocab_grads(
         normed, table_low, log_total, local_first, local_second, vocab, inv_count
     )
     own_log = lax.dynamic_index_in_dim(log_total, mine, 0, keepdims=False)
     loss_part = (1.0 + second_weight) * jnp.sum(own_log) - jnp.sum(picks)
-    grad_final = scatter_all(grad_rows, 1).astype(f32)
-    grad_states, grad_gain_final = rms_back(states, final_gain, grad_final)
+    grad = scatter_all(grad_rows, 1)
     gain_grads = [None] * 5
-    gain_grads[4] = grad_gain_final
-    quads = [None, None]
+    store = None
     for l in (1, 0):
-        grad_states, grads, gain_grads[2 * l], gain_grads[2 * l + 1] = layer_backward(
-            caches[l], grad_states, weights[l], gains[2 * l], gains[2 * l + 1], tables, seg_rows,
-            reach, seq_blocks, 5
+        before, a, q, k, v, far_k, far_v, total, accum, cache = caches[l]
+        store, grad_mixed, grad_att, gain_grads[2 * l + 1], final_row = mlp_backward(
+            l, l == 1, grad, states, cache, rows_of_gain[2 * l + 1], rows_of_gain[4], weights, store
         )
-        quads[l] = quads_to_rows(matrices_to_quads(grads), own_blocks)
-    block_rows = scatter_all(jnp.concatenate(quads, axis=0), 6, by_section=True).astype(f32)
-    grad_embed = gather_all(grad_states.astype(bf16), 3)
+        if l == 1:
+            gain_grads[4] = final_row
+        dq, dk, dv = attend_back(
+            q, k, v, far_k, far_v, total, accum, grad_att, seg_rows, reach, seq_blocks, 5
+        )
+        store, grad, grad_low, gain_grads[2 * l] = qkv_backward(
+            l, dq, dk, dv, a, before, grad_mixed, rows_of_gain[2 * l], cosine, sine, weights, store
+        )
+    sends = store
+    if own_blocks % 4:
+        sends = jnp.stack([quads_to_rows(store[l], own_blocks) for l in range(2)])
+    sends = sends.reshape(devices, rows_low.shape[0], QUAD)
+    block_rows = scatter_all(sends, 6, by_section=True)
+    grad_embed = gather_all(grad_low, 3)
     table_own = spread(local_ids, grad_embed, head_term)[:vocab]
-    block_own = rows_to_blocks(block_rows)
-    square_sum = jnp.sum(table_own * table_own) + jnp.sum(block_rows * block_rows)
-    small = jnp.stack(
+    square_rows = block_rows.astype(f32)
+    square_sum = jnp.sum(table_own * table_own) + jnp.sum(square_rows * square_rows)
+    small = jnp.concatenate(
         gain_grads
-        + [jnp.full((D,), square_sum), jnp.full((D,), loss_part), jnp.zeros((D,), f32)]
-    )
-    summed = jnp.sum(gather_all(small, 7), axis=0)
+        + [jnp.full((1, D), square_sum), jnp.full((1, D), loss_part), jnp.zeros((1, D), f32)]
+    )
+    summed = share_sum(small, 7)
     gain_grad = summed[:5]
     clip_norm = jnp.sqrt(summed[5, 0] + jnp.sum(gain_grad * gain_grad))
     factor = clip_bound / jnp.maximum(clip_norm, clip_bound)
     loss = summed[6, 0] * inv_count
-    grad_blocks = block_own * factor
-    left_new = stat_decay * left_stats[0] + (1.0 - stat_decay) * jnp.einsum(
-        "bij,bkj->bik", grad_blocks, grad_blocks, precision=highest
-    )
-    right_new = stat_decay * right_stats[0] + (1.0 - stat_decay) * jnp.einsum(
-        "bji,bjk->bik", grad_blocks, grad_blocks, precision=highest
-    )
-    direction = jnp.einsum(
-        "bij,bjk->bik",
-        left_root[0],
-        jnp.einsum("bij,bjk->bik", grad_blocks, right_root[0], precision=highest),
-        precision=highest,
-    )
-    blocks_new = blocks[0] - shampoo_rate * direction
+    update = shampoo if own_blocks % 12 == 0 else shampoo_plain
+    blocks_new, blocks_low, left_new, right_new = update(
+        factor, block_rows, blocks[0], left_stats[0], right_stats[0], left_root[0], right_root[0]
+    )
     table_new, table_m_new, table_v_new = adam_step(
         table, table_m, table_v, table_own * factor, weight_decay
     )
@@ -980,7 +1340,7 @@
     )
     return (
         loss, clip_norm, table_new, table_m_new, table_v_new, table_new.astype(bf16),
-        blocks_new[None], blocks_new[None].astype(bf16), left_new[None], right_new[None],
+        blocks_new[None], blocks_low[None], left_new[None], right_new[None],
         gains_new, gains_m_new, gains_v_new,
     )
 

time: 1500 us -> 1090 us (0.73)
  local copies, waits for them, and re-layouts: 267 us -> 54.3 us
  matrix products: 83.3 us -> 0 us
  other arithmetic: 109 us -> 29.2 us
  blocking collectives: 43.1 us -> 0 us
  Pallas kernels: 974 us -> 989 us
    dot_general x28 -> x0, matrix products: 83.3 us -> none  [the longest x8 15.9 us: through(): return jnp.einsum('rf,df->rd', grad, weight, preferred_element_type=f32)]
    pallas_call x3 -> x15, Pallas kernels: 378 us -> 438 us  [the longest x3 276 us: reduce_scatter32(): pl.pallas_call(functools.partial(rs_kernel, B, H, parts, by_section), out...]
    transpose x16 -> x0, local copies, waits for them, and re-layouts: 53.6 us -> none  [the longest x10 30 us: matrices_to_quads(): matrix.reshape(r, BS, c, QUAD).transpose(0, 2, 1, 3)]
    slice x17 -> x4, local copies, waits for them, and re-layouts: 49.5 us -> 2.34 us  [the longest x1 0.91 us: share_ids(): return every.reshape(blk, shard, 2, *packed.shape)[:, :, 0]]
    pallas_call x5 -> x3, Pallas kernels: 296 us -> 250 us  [all_gather32(): pl.pallas_call(functools.partial(ag_kernel, B, H, parts, by_section), out...]
    all_gather x1 -> x0, blocking collectives: 43.1 us -> none  [on_device(): lax.all_gather(packed, ('blk', 'shard'))]
    unnamed x234 -> x44, local copies, waits for them, and re-layouts: 79.1 us -> 38.8 us
    concatenate x9 -> x1, other arithmetic: 37.3 us -> 1.46 us  [share_stats(): pair = jnp.concatenate([top, total], axis=1)]
where the time goes in v2:
time: 1090 us; the launch traced here: 1080 us
  Pallas kernels  989 us (91%)
  local copies, waits for them, and re-layouts  54.3 us (5%)
  other arithmetic  29.2 us (3%)
    pallas_call x3, Pallas kernels, reduce_scatter32(): pl.pallas_call(functools.partial(rs_kernel, B, H, parts, by_section), out...  276 us
    pallas_call x3, Pallas kernels, all_gather32(): pl.pallas_call(functools.partial(ag_kernel, B, H, parts, by_section), out...  250 us
    pallas_call x1, Pallas kernels, vocab_grads(): pl.pallas_call(functools.partial(vocab_kernel, vocab, scale), grid=(count...  84.9 us
    pallas_call x2, Pallas kernels, attend_back(): pl.pallas_call(functools.partial(attend_back_kernel, reach, blocks), out_...  67.8 us
    pallas_call x2, Pallas kernels, attend(): pl.pallas_call(functools.partial(attend_kernel, reach, blocks), out_shape...  61.5 us
    pallas_call x3, Pallas kernels, swap_all(): pl.pallas_call(functools.partial(swap_kernel, n, join), out_shape=jax.Sha...  43.9 us
    unnamed x44, local copies, waits for them, and re-layouts  38.8 us
    pallas_call x2, Pallas kernels, mlp_backward(): pl.pallas_call(functools.partial(mlp_back_kernel, layer, last, store is N...  38.5 us

profile of v2, /device:TPU:0, one launch (start us, length us, event | category | flops | bytes accessed | tf_op | source)
XLA Modules:
  0.0 1081.5 jit_solution(11964865753912170188)
XLA Ops:
  3.4 14.3 %swap_ids.1 = s32[32,8,256]{2,1,0:T(8,128)} custom-call(s32[8,256]{1,0:T(8,128)} %reshape.204.x_ref), custom_call_target="tpu_custom_call" | custom-call | tf_op jit(solution)/shard_map/swap_ids/pallas_call | solution.py:329
  23.4 24.3 %lookup.1.p_ref = bf16[32,256,768]{2,1,0:T(8,128)(2,1)} custom-call(s32[32,1,256]{2,1,0:T(1,128)} %and_select_fusion.2.ids_ref, bf16[1024,768]{1,0:T(8,128)(2,1)} %pad.8.tab_ref), custom_call_target="tpu_custom_call" | custom-call | tf_op jit(solution)/shard_map/lookup/pallas_call | solution.py:372
  47.7 69.3 %scatter_256.2 = bf16[256,768]{1,0:T(8,128)(2,1)} custom-call(bf16[32,256,768]{2,1,0:T(8,128)(2,1)} %lookup.1.p_ref), custom_call_target="tpu_custom_call" | custom-call | tf_op jit(solution)/shard_map/scatter_256/pallas_call | solution.py:277
  122.1 4.4 copy.65
  133.7 112.9 %gather_1728.1 = bf16[32,1728,256]{2,1,0:T(8,128)(2,1)} custom-call(bf16[1728,256]{1,0:T(8,128)(2,1)} %reshape.206.x_ref), custom_call_target="tpu_custom_call" | custom-call | tf_op jit(solution)/shard_map/gather_1728/pallas_call | solution.py:137
  246.6 7.6 qkv.2
  255.6 23.2 %attend.2 = (f32[256,768]{1,0:T(8,128)}, f32[256,768]{1,0:T(8,128)}, bf16[2,256,768]{2,1,0:T(8,128)(2,1)}, bf16[2,256,768]{2,1,0:T(8,128)(2,1)}) custom-call(bf16[256,768]{1,0:T(8,128)(2,1)} %get-tuple-element.74.q_ref, bf16[256,768]{1,0:T(8,128)(2,1)} %get-tuple-element.75.k_ref, bf16[256,768]{1,0:T(8,128)(2,1)} %get-tuple-element.76.v_ref, ...), custom_call_target="tpu_custom_call" | custom-call | tf_op jit(solution)/shard_map/attend/pallas_call | solution.py:617
  278.7 12.1 %mlp.2 = (f32[256,768]{1,0:T(8,128)}, bf16[256,768]{1,0:T(8,128)(2,1)}, f32[256,768]{1,0:T(8,128)}, bf16[256,768]{1,0:T(8,128)(2,1)}, f32[256,2048]{1,0:T(8,128)...) custom-call(f32[256,768]{1,0:T(8,128)} %convert_element_type.41.x_ref, ...), custom_call_target="tpu_custom_call" | custom-call | tf_op jit(solution)/shard_map/mlp/pallas_call | solution.py:945
  290.8 7.6 qkv.3
  298.4 38.3 %attend.3 = (f32[256,768]{1,0:T(8,128)}, f32[256,768]{1,0:T(8,128)}, bf16[2,256,768]{2,1,0:T(8,128)(2,1)}, bf16[2,256,768]{2,1,0:T(8,128)(2,1)}) custom-call(bf16[256,768]{1,0:T(8,128)(2,1)} %get-tuple-element.82.q_ref, bf16[256,768]{1,0:T(8,128)(2,1)} %get-tuple-element.83.k_ref, bf16[256,768]{1,0:T(8,128)(2,1)} %get-tuple-element.84.v_ref, ...), custom_call_target="tpu_custom_call" | custom-call | tf_op jit(solution)/shard_map/attend/pallas_call | solution.py:617
  336.7 12.1 %mlp.3 = (f32[256,768]{1,0:T(8,128)}, bf16[256,768]{1,0:T(8,128)(2,1)}, f32[256,768]{1,0:T(8,128)}, bf16[256,768]{1,0:T(8,128)(2,1)}, f32[256,2048]{1,0:T(8,128)...) custom-call(f32[256,768]{1,0:T(8,128)} %get-tuple-element.81.x_ref, ...), custom_call_target="tpu_custom_call" | custom-call | tf_op jit(solution)/shard_map/mlp/pallas_call | solution.py:945
  348.8 72.3 %gather_256.2.nf_ref = bf16[32,256,768]{2,1,0:T(8,128)(2,1)} custom-call(bf16[256,768]{1,0:T(8,128)(2,1)} %get-tuple-element.89.x_ref), custom_call_target="tpu_custom_call" | custom-call | tf_op jit(solution)/shard_map/gather_256/pallas_call | solution.py:137
  421.0 31.6 %vocab_stats.1 = (f32[32,1,256]{2,1,0:T(1,128)}, f32[32,1,256]{2,1,0:T(1,128)}) custom-call(bf16[32,256,768]{2,1,0:T(8,128)(2,1)} %gather_256.2.nf_ref, bf16[1024,768]{1,0:T(8,128)(2,1)} %pad.8.tab_ref), custom_call_target="tpu_custom_call" | custom-call | tf_op jit(solution)/shard_map/vocab_stats/pallas_call | solution.py:428
  454.1 15.9 %swap_stats.1.lse_ref = f32[32,1,256]{2,1,0:T(1,128)} custom-call(f32[32,2,256]{2,1,0:T(2,128)} %pad_maximum_fusion.x_ref), custom_call_target="tpu_custom_call" | custom-call | tf_op jit(solution)/shard_map/swap_stats/pallas_call | solution.py:329
  470.8 84.9 %vocab_grads.1 = (bf16[32,256,768]{2,1,0:T(8,128)(2,1)}, f32[1024,768]{1,0:T(8,128)}, f32[1,256]{1,0:T(1,128)}) custom-call(bf16[32,256,768]{2,1,0:T(8,128)(2,1)} %gather_256.2.nf_ref, bf16[1024,768]{1,0:T(8,128)(2,1)} %pad.8.tab_ref, f32[32,1,256]{2,1,0:T(1,128)} %swap_stats.1.lse_ref, s32[32,1,256]{2,1,0:T(1,128)} %get-tuple-element.198.t0_ref, ...), custom_call_target="tpu_custom_call" | custom-call | tf_op jit(solution)/shard_map/vocab_grads/pallas_call | solution.py:469
  555.7 67.1 %scatter_256.3.refs_0_ = bf16[256,768]{1,0:T(8,128)(2,1)} custom-call(bf16[32,256,768]{2,1,0:T(8,128)(2,1)} %get-tuple-element.92.p_ref), custom_call_target="tpu_custom_call" | custom-call | tf_op jit(solution)/shard_map/scatter_256/pallas_call | solution.py:277
  622.8 19.2 %mlp_back.2 = (bf16[2,432,64,256]{3,2,1,0:T(8,128)(2,1)}, f32[256,768]{1,0:T(8,128)}, f32[256,768]{1,0:T(8,128)}, f32[1,768]{1,0:T(1,128)}, f32[1,768]{1,0:T(1,128)}) custom-call(bf16[256,768]{1,0:T(8,128)(2,1)} %scatter_256.3.refs_0_, f32[256,768]{1,0:T(8,128)} %get-tuple-element.93.refs_1_, f32[256,768]{1,0:T(8,128)} %get-tuple-element.94.refs_2_, ...), custom_call_target="tpu_custom_call" | custom-call | tf_op jit(solution)/shard_map/mlp_back/pallas_call | solution.py:1050
  642.0 29.9 %attend_back.2 = (f32[256,768]{1,0:T(8,128)}, f32[256,768]{1,0:T(8,128)}, f32[256,768]{1,0:T(8,128)}) custom-call(bf16[256,768]{1,0:T(8,128)(2,1)} %get-tuple-element.82.q_ref, bf16[256,768]{1,0:T(8,128)(2,1)} %get-tuple-element.83.k_ref, bf16[256,768]{1,0:T(8,128)(2,1)} %get-tuple-element.84.v_ref, bf16[2,256,768]{2,1,0:T(8,128)(2,1)} %get-tuple-element.85.kr_ref, ...), custom_call_target="tpu_custom_call" | custom-call | tf_op jit(solution)/shard_map/attend_back/pallas_call | solution.py:738
  671.9 11.7 %qkv_back.2 = (bf16[2,432,64,256]{3,2,1,0:T(8,128)(2,1)}, f32[256,768]{1,0:T(8,128)}, bf16[256,768]{1,0:T(8,128)(2,1)}, f32[1,768]{1,0:T(1,128)}) custom-call(f32[256,768]{1,0:T(8,128)} %get-tuple-element.101.dq_ref, f32[256,768]{1,0:T(8,128)} %get-tuple-element.102.dk_ref, f32[256,768]{1,0:T(8,128)} %get-tuple-element.103.dv_ref, ...), custom_call_target="tpu_custom_call", output_to_operand_aliasing={{0}: (10, {})} | custom-call | tf_op jit(solution)/shard_map/qkv_back/pallas_call | solution.py:1101
  683.6 19.3 %mlp_back.3 = (bf16[2,432,64,256]{3,2,1,0:T(8,128)(2,1)}, f32[256,768]{1,0:T(8,128)}, f32[256,768]{1,0:T(8,128)}, f32[1,768]{1,0:T(1,128)}, f32[1,768]{1,0:T(1,128)}) custom-call(f32[256,768]{1,0:T(8,128)} %get-tuple-element.107.refs_0_, f32[256,768]{1,0:T(8,128)} %get-tuple-element.93.refs_1_, ...), custom_call_target="tpu_custom_call", output_to_operand_aliasing={{0}: (11, {})} | custom-call | tf_op jit(solution)/shard_map/mlp_back/pallas_call | solution.py:1050
  702.9 37.9 %attend_back.3 = (f32[256,768]{1,0:T(8,128)}, f32[256,768]{1,0:T(8,128)}, f32[256,768]{1,0:T(8,128)}) custom-call(bf16[256,768]{1,0:T(8,128)(2,1)} %get-tuple-element.74.q_ref, bf16[256,768]{1,0:T(8,128)(2,1)} %get-tuple-element.75.k_ref, bf16[256,768]{1,0:T(8,128)(2,1)} %get-tuple-element.76.v_ref, bf16[2,256,768]{2,1,0:T(8,128)(2,1)} %get-tuple-element.77.kr_ref, ...), custom_call_target="tpu_custom_call" | custom-call | tf_op jit(solution)/shard_map/attend_back/pallas_call | solution.py:738
  740.9 11.8 %qkv_back.3 = (bf16[2,432,64,256]{3,2,1,0:T(8,128)(2,1)}, f32[256,768]{1,0:T(8,128)}, bf16[256,768]{1,0:T(8,128)(2,1)}, f32[1,768]{1,0:T(1,128)}) custom-call(f32[256,768]{1,0:T(8,128)} %get-tuple-element.116.dq_ref, f32[256,768]{1,0:T(8,128)} %get-tuple-element.117.dk_ref, f32[256,768]{1,0:T(8,128)} %get-tuple-element.118.dv_ref, ...), custom_call_target="tpu_custom_call", output_to_operand_aliasing={{0}: (10, {})} | custom-call | tf_op jit(solution)/shard_map/qkv_back/pallas_call | solution.py:1101
  752.7 64.8 %gather_256.3.g_ref = bf16[32,256,768]{2,1,0:T(8,128)(2,1)} custom-call(bf16[256,768]{1,0:T(8,128)(2,1)} %get-tuple-element.127.x_ref), custom_call_target="tpu_custom_call" | custom-call | tf_op jit(solution)/shard_map/gather_256/pallas_call | solution.py:137
  817.4 31.4 %spread.1 = f32[1024,768]{1,0:T(8,128)} custom-call(s32[32,1,256]{2,1,0:T(1,128)} %and_select_fusion.2.ids_ref, bf16[32,256,768]{2,1,0:T(8,128)(2,1)} %gather_256.3.g_ref, f32[1024,768]{1,0:T(8,128)} %get-tuple-element.128.base_ref), custom_call_target="tpu_custom_call" | custom-call | tf_op jit(solution)/shard_map/spread/pallas_call | solution.py:399
  852.2 139.5 %scatter_1728.1 = bf16[1728,256]{1,0:T(8,128)(2,1)} custom-call(bf16[32,1728,256]{2,1,0:T(8,128)(2,1)} %bitcast.48), custom_call_target="tpu_custom_call" | custom-call | tf_op jit(solution)/shard_map/scatter_1728/pallas_call | solution.py:277
  999.1 13.7 %swap_sum.1 = f32[32,1,256]{2,1,0:T(1,128)} custom-call(f32[32,1,256]{2,1,0:T(1,128)} %bitcast.62), custom_call_target="tpu_custom_call" | custom-call | tf_op jit(solution)/shard_map/swap_sum/pallas_call | solution.py:329
  1017.5 8.7 fusion.5
  1030.2 5.3 copy.72
  1039.6 5.1 copy.74
  1044.7 16.9 %shampoo.1 = (f32[108,64,64]{2,1,0:T(8,128)}, bf16[108,64,64]{2,1,0:T(8,128)(2,1)}, f32[108,64,64]{2,1,0:T(8,128)}, f32[108,64,64]{2,1,0:T(8,128)}) custom-call(f32[1,1]{1,0:T(1,128)} %bitcast.19.scale_ref, bf16[27,64,256]{2,1,0:T(8,128)(2,1)} %bitcast.54, f32[108,64,64]{2,1,0:T(8,128)} %bitcast.49, f32[108,64,64]{2,1,0:T(8,128)} %bitcast.50, ...), custom_call_target="tpu_custom_call" | custom-call | tf_op jit(solution)/shard_map/shampoo/pallas_call | solution.py:1156
  1061.5 4.6 copy.75
  1068.8 4.6 copy.77
  (88 shorter events, 51.0 us)
Async XLA Ops:
  0.6 0.7 copy-start
  47.7 71.3 %copy-start.10 = (f32[5,768]{1,0:T(8,128)S(1)}, f32[5,768]{1,0:T(8,128)}, u32[]{:S(2)}) copy-start(f32[5,768]{1,0:T(8,128)} %param.25) | copy-start | bytes 46084
  126.6 3.2 copy-start.2
  246.6 7.6 copy-start.9
  421.0 48.9 %copy-start.8 = (s32[1,2,4,4,256]{4,2,1,0,3:T(4,128)S(1)}, s32[1,2,4,4,256]{4,2,1,0,3:T(4,128)}, u32[]{:S(2)}) copy-start(s32[1,2,4,4,256]{4,2,1,0,3:T(4,128)} %get-tuple-element.181) | copy-start | bytes 98308
  421.0 49.0 %copy-start.7 = (s32[1,2,4,4,256]{4,2,1,0,3:T(4,128)S(1)}, s32[1,2,4,4,256]{4,2,1,0,3:T(4,128)}, u32[]{:S(2)}) copy-start(s32[1,2,4,4,256]{4,2,1,0,3:T(4,128)} %get-tuple-element.182) | copy-start | bytes 98308
  852.1 144.9 %copy-start.16 = (f32[1,256]{1,0:T(1,128)S(1)}, f32[1,256]{1,0:T(1,128)}, u32[]{:S(2)}) copy-start(f32[1,256]{1,0:T(1,128)} %get-tuple-element.130) | copy-start | bytes 3076
  852.1 146.2 %copy-start.11 = (f32[1,768]{1,0:T(1,128)S(1)}, f32[1,768]{1,0:T(1,128)}, u32[]{:S(2)}) copy-start(f32[1,768]{1,0:T(1,128)} %get-tuple-element.125) | copy-start | bytes 9220
  852.1 146.2 %copy-start.12 = (f32[1,768]{1,0:T(1,128)S(1)}, f32[1,768]{1,0:T(1,128)}, u32[]{:S(2)}) copy-start(f32[1,768]{1,0:T(1,128)} %get-tuple-element.126) | copy-start | bytes 9220
  852.1 146.2 %copy-start.13 = (f32[1,768]{1,0:T(1,128)S(1)}, f32[1,768]{1,0:T(1,128)}, u32[]{:S(2)}) copy-start(f32[1,768]{1,0:T(1,128)} %get-tuple-element.124) | copy-start | bytes 9220
  852.2 146.2 %copy-start.14 = (f32[1,768]{1,0:T(1,128)S(1)}, f32[1,768]{1,0:T(1,128)}, u32[]{:S(2)}) copy-start(f32[1,768]{1,0:T(1,128)} %get-tuple-element.123) | copy-start | bytes 9220
  852.2 146.2 %copy-start.15 = (f32[1,768]{1,0:T(1,128)S(1)}, f32[1,768]{1,0:T(1,128)}, u32[]{:S(2)}) copy-start(f32[1,768]{1,0:T(1,128)} %get-tuple-element.122) | copy-start | bytes 9220
  1017.5 8.7 copy-start.4
  1030.2 5.3 copy-start.5
  1061.5 4.6 copy-start.6
  1068.8 4.6 copy-start.3
  1068.8 9.9 copy-start.1

commit v3 on v2

--- a/solution.py
+++ b/solution.py
@@ -40,7 +40,13 @@
     a=int(round(R*frac/step))*step
     return min(max(a,0),R)
 
-def ag_kernel(B,H,parts,by_section,x_ref,o_ref,ssem,rsem,lsem):
+def ag_kernel(B,H,parts,by_section,side,counts,*refs):
+    ni,no=counts
+    x_ref,o_ref=refs[0],refs[1+ni]
+    ssem,rsem,lsem=refs[2+ni+no:5+ni+no]
+    todo=[]
+    if side is not None:
+        todo=side(*refs[1:1+ni],*refs[2+ni:2+ni+no],*refs[5+ni+no:])
     s=lax.axis_index("section"); b=lax.axis_index("blk"); h=lax.axis_index("shard")
     x1=h^1; y1=h^2; xy=h^3
     part=(1-s,b,h)
@@ -93,6 +99,8 @@
         for c,cp in cps:
             cc=cond if c is None else (c if cond is None else jnp.logical_and(cond,c))
             pend.append((cc,cp))
+    def work():
+        if todo: todo.pop(0)()
     two=len(parts)>1
     group(None,[],[(0,b,h,rt,has_r,True),(0,b,h,lf,has_l,True),(0,b,h,xn,None,True),(0,b,h,yn,None,True)])
     if two:
@@ -100,7 +108,9 @@
     group(None,[],[(p,b,h,part,None,True) for p in range(len(parts))])
     if two:
         group(None,[(1,b,y1)],[(1,b,y1,rt,has_r,False),(1,b,y1,lf,has_l,False),(1,b,y1,xn,None,False),(1,b,y1,part,None,False)])
+    work()
     group(None,[(0,b,x1)],[(0,b,x1,yn,None,False),(0,b,x1,part,None,False)])
+    work()
     for d in range(1,B):
         cl=b>=d; cr=b+d<B
         group(cl,[(0,b-d,h)],[(0,b-d,h,rt,has_r,False),(0,b-d,h,xn,None,False),(0,b-d,h,yn,None,False),(0,b-d,h,part,None,False)])
@@ -109,8 +119,11 @@
             for hh in (h,y1):
                 group(cl,[(1,b-d,hh)],[(1,b-d,hh,rt,has_r,False),(1,b-d,hh,xn,None,False),(1,b-d,hh,part,None,False)])
                 group(cr,[(1,b+d,hh)],[(1,b+d,hh,lf,has_l,False),(1,b+d,hh,xn,None,False),(1,b+d,hh,part,None,False)])
+        work()
         group(cl,[(0,b-d,x1)],[(0,b-d,x1,yn,None,False),(0,b-d,x1,part,None,False)])
         group(cr,[(0,b+d,x1)],[(0,b+d,x1,yn,None,False),(0,b+d,x1,part,None,False)])
+        work()
+    while todo: work()
     for d in range(B):
         for sg in ((1,-1) if d else (1,)):
             c=None if d==0 else (b+d<B if sg>0 else b>=d)
@@ -127,22 +140,31 @@
         if c is None: cp.wait_send()
         else: pl.when(c)(cp.wait_send)
 
-def all_gather32(x,B,H,cid,by_section=False,frac=0.636,vmem_out=False):
+def all_gather32(x,B,H,cid,by_section=False,frac=0.636,side=None,side_in=(),side_out=(),side_scratch=()):
     R,C=x.shape
     step=16 if x.dtype==jnp.bfloat16 else 8
     a=split_rows(R,step,frac) if R>=4*step else R
     parts=[(0,a)]+([(a,R-a)] if a<R else [])
     n=2*B*H
     nsend=4+4+2+4+2+(B-1)*(8+4*4*1+4)+ (2*B-1)*4+16
-    return pl.pallas_call(functools.partial(ag_kernel,B,H,parts,by_section),
-        out_shape=jax.ShapeDtypeStruct((n,R,C),x.dtype),
-        in_specs=[pl.BlockSpec(memory_space=pltpu.VMEM)],
-        out_specs=pl.BlockSpec(memory_space=pl.ANY),
-        scratch_shapes=[pltpu.SemaphoreType.DMA((nsend,)),pltpu.SemaphoreType.DMA((len(parts),n)),pltpu.SemaphoreType.DMA((1,))],
-        compiler_params=pltpu.CompilerParams(collective_id=cid,has_side_effects=True),name=f"gather_{R}")(x)
-
-def rs_kernel(B,H,parts,by_section,p_ref,o_ref,*refs):
-    q,r1,ya,xa,za,xb,zb,yb,lsem,psem_s,psem_r,ssem,ya_s,xa_s,za_s,xb_s,zb_s,yb_s=refs
+    specs=[pl.BlockSpec(memory_space=pltpu.VMEM)]+[sp for _,sp in side_in]
+    out=pl.pallas_call(functools.partial(ag_kernel,B,H,parts,by_section,side,(len(side_in),len(side_out))),
+        out_shape=(jax.ShapeDtypeStruct((n,R,C),x.dtype),)+tuple(sh for sh,_ in side_out),
+        in_specs=specs,
+        out_specs=(pl.BlockSpec(memory_space=pl.ANY),)+tuple(sp for _,sp in side_out),
+        scratch_shapes=[pltpu.SemaphoreType.DMA((nsend,)),pltpu.SemaphoreType.DMA((len(parts),n)),pltpu.SemaphoreType.DMA((1,))]+list(side_scratch),
+        compiler_params=pltpu.CompilerParams(collective_id=cid,has_side_effects=True,vmem_limit_bytes=VMEM_MAX),name=f"gather_{R}_{cid}")(x,*[v for v,_ in side_in])
+    return out if side is not None else out[0]
+
+def rs_kernel(B,H,parts,by_section,side,counts,*refs):
+    ni,no=counts
+    p_ref,o_ref=refs[0],refs[1+ni]
+    q,r1,ya,xa,za,xb,zb,yb,lsem,psem_s,psem_r,ssem,ya_s,xa_s,za_s,xb_s,zb_s,yb_s=refs[2+ni+no:20+ni+no]
+    todo=[]
+    if side is not None:
+        todo=side(*refs[1:1+ni],*refs[2+ni:2+ni+no],*refs[20+ni+no:])
+    def work():
+        if todo: todo.pop(0)()
     s=lax.axis_index("section"); b=lax.axis_index("blk"); h=lax.axis_index("shard")
     x=h&1; y=h>>1
     part=(1-s,b,h); xn=(s,b,h^1); yn=(s,b,h^2); lf=(s,b-1,h); rt=(s,b+1,h)
@@ -247,9 +269,13 @@
                 add(q.at[b*H+hh,rows],zr(d,b),n)
     for i in range(B+2):
         if i<B: first(i)
+        work()
         if 1<=i<B+1: second(i-1)
+        work()
         if 2<=i<B+1: third(i-2)
-    flush()
+        flush()
+        work()
+    while todo: work()
     last(0)
     queue(None,q.at[b*H+hs[1],Bp],yb,yb_s.at[0],yn)
     got(xa.at[b],xa_s.at[b])
@@ -265,7 +291,7 @@
         if c is None: cp.wait_send()
         else: pl.when(c)(cp.wait_send)
 
-def reduce_scatter32(p,B,H,cid,by_section=False,frac=0.636):
+def reduce_scatter32(p,B,H,cid,by_section=False,frac=0.636,side=None,side_in=(),side_out=(),side_scratch=()):
     n,R,C=p.shape
     a=split_rows(R,16,frac)
     parts=((0,a),(a,R-a))
@@ -274,13 +300,14 @@
     N=B*H
     an,bn=a,R-a
     nsend=4*B+B+6*(B-1)+2
-    return pl.pallas_call(functools.partial(rs_kernel,B,H,parts,by_section),
-        out_shape=jax.ShapeDtypeStruct((R,C),p.dtype),
-        in_specs=[pl.BlockSpec(memory_space=pl.ANY)],
-        out_specs=pl.BlockSpec(memory_space=pltpu.VMEM),
+    out=pl.pallas_call(functools.partial(rs_kernel,B,H,parts,by_section,side,(len(side_in),len(side_out))),
+        out_shape=(jax.ShapeDtypeStruct((R,C),p.dtype),)+tuple(sh for sh,_ in side_out),
+        in_specs=[pl.BlockSpec(memory_space=pl.ANY)]+[sp for _,sp in side_in],
+        out_specs=(pl.BlockSpec(memory_space=pltpu.VMEM),)+tuple(sp for _,sp in side_out),
         scratch_shapes=[V(N,R,C),V(N,R,C),V(2*B,an,C),V(B,an,C),V(2*B,an,C),V(2*B,bn,C),V(4*B,bn,C),V(bn,C),
-           D(N),D(N),D(N),D(nsend),D(2*B),D(B),D(2*B),D(2*B),D(4*B),D(1)],
-        compiler_params=pltpu.CompilerParams(collective_id=cid,has_side_effects=True,vmem_limit_bytes=63*1024*1024),name=f"scatter_{R}")(p)
+           D(N),D(N),D(N),D(nsend),D(2*B),D(B),D(2*B),D(2*B),D(4*B),D(1)]+list(side_scratch),
+        compiler_params=pltpu.CompilerParams(collective_id=cid,has_side_effects=True,vmem_limit_bytes=VMEM_MAX),name=f"scatter_{R}_{cid}")(p,*[v for v,_ in side_in])
+    return out if side is not None else out[0]
 
 def swap_kernel(n,join,x_ref,o_ref,got,total,ssem,rsem,ssem2,rsem2):
     B,H=lax.axis_size("blk"),lax.axis_size("shard")
@@ -344,7 +371,7 @@
 
 def gather_all(value, cid, by_section=False):
     blk, shard = lax.axis_size("blk"), lax.axis_size("shard")
-    if blk * shard <= 16 and shard == 4:
+    if kernels_fit():
         return all_gather32(value, blk, shard, cid, by_section)
     names = ("section", "blk", "shard") if by_section else ORDER
     return lax.all_gather(value, names)
@@ -352,10 +379,15 @@
 
 def scatter_all(value, cid, by_section=False):
     blk, shard = lax.axis_size("blk"), lax.axis_size("shard")
-    if blk * shard <= 16 and shard == 4:
+    if kernels_fit():
         return reduce_scatter32(value, blk, shard, cid, by_section)
     names = ("section", "blk", "shard") if by_section else ORDER
     return lax.psum_scatter(value, names, scatter_dimension=0)
+
+
+def kernels_fit():
+    blk, shard = lax.axis_size("blk"), lax.axis_size("shard")
+    return blk * shard <= 16 and shard == 4
 
 
 def lookup_kernel(ids_ref, tab_ref, o_ref):
@@ -410,73 +442,188 @@
     )(local_ids[:, None, :], grads, base)
 
 
-def stats_kernel(vocab, nf_ref, tab_ref, top_ref, sum_ref):
+GROUP = 4
+
+
+def lookup_work(ids_ref, tab_ref, o_ref, out_buf, out_sem):
+    count = ids_ref.shape[0]
+
+    def put(n):
+        return pltpu.make_async_copy(out_buf.at[n % GROUP], o_ref.at[n], out_sem.at[n % GROUP])
+
+    def step(first):
+        @pl.loop(0, GROUP)
+        def _(i):
+            n = first + i
+            if first:
+                put(n - GROUP).wait()
+            rows = lax.broadcasted_iota(jnp.int32, (tab_ref.shape[0], ids_ref.shape[-1]), 0)
+            hot = jnp.where(rows == ids_ref[n], 1.0, 0.0).astype(bf16)
+            out_buf[n % GROUP] = lax.dot_general(
+                hot, tab_ref[...], (((0,), (0,)), ((), ())), preferred_element_type=f32
+            ).astype(bf16)
+            put(n).start()
+
+    def finish():
+        for n in range(count - GROUP, count):
+            put(n).wait()
+
+    return [functools.partial(step, n) for n in range(0, count, GROUP)] + [finish]
+
+
+def gather_and_lookup(value, cid, local_ids, table_low):
+    if not kernels_fit():
+        return gather_all(value, cid, True), lookup(local_ids, table_low)
+    count, tokens = local_ids.shape
+    inside = pl.BlockSpec(memory_space=pltpu.VMEM)
+    return all_gather32(
+        value, lax.axis_size("blk"), lax.axis_size("shard"), cid, True,
+        side=lookup_work,
+        side_in=((local_ids[:, None, :], inside), (table_low, inside)),
+        side_out=(
+            (jax.ShapeDtypeStruct((count, tokens, D), bf16), pl.BlockSpec(memory_space=pl.ANY)),
+        ),
+        side_scratch=(
+            pltpu.VMEM((GROUP, tokens, D), bf16),
+            pltpu.SemaphoreType.DMA((GROUP,)),
+        ),
+    )
+
+
+def spread_work(ids_ref, g_ref, base_ref, o_ref, buf, sem):
+    count = ids_ref.shape[0]
+
+    def load(first, i):
+        side = (first // GROUP) % 2
+        return pltpu.make_async_copy(g_ref.at[first + i], buf.at[side, i], sem.at[side, i])
+
+    def start(first):
+        for i in range(GROUP):
+            load(first, i).start()
+
+    def step(first):
+        if first == 0:
+            start(0)
+            o_ref[...] = base_ref[...]
+        if first + GROUP < count:
+            start(first + GROUP)
+        for i in range(GROUP):
+            load(first, i).wait()
+
+        @pl.loop(0, GROUP)
+        def _(i):
+            rows = lax.broadcasted_iota(jnp.int32, (o_ref.shape[0], ids_ref.shape[-1]), 0)
+            hot = jnp.where(rows == ids_ref[first + i], 1.0, 0.0).astype(bf16)
+            o_ref[...] += jnp.dot(
+                hot, buf[(first // GROUP) % 2, i], preferred_element_type=f32
+            )
+
+    return [functools.partial(step, n) for n in range(0, count, GROUP)]
+
+
+def scatter_and_spread(value, cid, local_ids, grads, base):
+    if not kernels_fit():
+        return scatter_all(value, cid, True), spread(local_ids, grads, base)
+    tokens = local_ids.shape[1]
+    inside = pl.BlockSpec(memory_space=pltpu.VMEM)
+    return reduce_scatter32(
+        value, lax.axis_size("blk"), lax.axis_size("shard"), cid, True,
+        side=spread_work,
+        side_in=(
+            (local_ids[:, None, :], inside),
+            (grads, pl.BlockSpec(memory_space=pl.ANY)),
+            (base, inside),
+        ),
+        side_out=((jax.ShapeDtypeStruct(base.shape, f32), inside),),
+        side_scratch=(
+            pltpu.VMEM((2, GROUP, tokens, D), bf16),
+            pltpu.SemaphoreType.DMA((2, GROUP)),
+        ),
+    )
+
+
+def stats_kernel(vocab, nf_ref, tab_ref, t0_ref, t1_ref, top_ref, sum_ref, exp_ref, pick_ref):
     logits = lax.dot_general(
         tab_ref[...], nf_ref[0], (((1,), (1,)), ((), ())), preferred_element_type=f32
     )
     rows = lax.broadcasted_iota(jnp.int32, logits.shape, 0)
+    hits = jnp.where(rows == t0_ref[0], 1.0, 0.0) + jnp.where(rows == t1_ref[0], second_weight, 0.0)
+
+    @pl.when(pl.program_id(0) == 0)
+    def _():
+        pick_ref[...] = jnp.zeros_like(pick_ref)
+
+    pick_ref[...] += jnp.sum(hits * logits, axis=0, keepdims=True)
     logits = jnp.where(rows < vocab, logits, -1e30)
     top = jnp.max(logits, axis=0, keepdims=True)
+    expo = jnp.exp(logits - top)
     top_ref[0] = top
-    sum_ref[0] = jnp.sum(jnp.exp(logits - top), axis=0, keepdims=True)
-
-
-def vocab_stats(normed, table_low, vocab):
+    sum_ref[0] = jnp.sum(expo, axis=0, keepdims=True)
+    exp_ref[0] = expo.astype(bf16)
+
+
+def vocab_stats(normed, table_low, first, second, vocab):
     count, tokens, _ = normed.shape
     padded = table_low.shape[0]
     row = jax.ShapeDtypeStruct((count, 1, tokens), f32)
+    row_spec = pl.BlockSpec((1, 1, tokens), lambda i: (i, 0, 0))
     return pl.pallas_call(
         functools.partial(stats_kernel, vocab),
         grid=(count,),
-        out_shape=(row, row),
-        in_specs=[
-            pl.BlockSpec((1, tokens, D), lambda i: (i, 0, 0)),
-            pl.BlockSpec((padded, D), lambda i: (0, 0)),
-        ],
-        out_specs=(
-            pl.BlockSpec((1, 1, tokens), lambda i: (i, 0, 0)),
-            pl.BlockSpec((1, 1, tokens), lambda i: (i, 0, 0)),
-        ),
-        name="vocab_stats",
-    )(normed, table_low)
-
-
-def vocab_kernel(vocab, scale, nf_ref, tab_ref, lse_ref, t0_ref, t1_ref, g_ref, acc_ref, pick_ref):
-    logits = lax.dot_general(
-        tab_ref[...], nf_ref[0], (((1,), (1,)), ((), ())), preferred_element_type=f32
-    )
-    rows = lax.broadcasted_iota(jnp.int32, logits.shape, 0)
-    hits = jnp.where(rows == t0_ref[0], 1.0, 0.0) + jnp.where(rows == t1_ref[0], second_weight, 0.0)
-    soft = jnp.exp(logits - lse_ref[0]) * (1.0 + second_weight)
-    grad = jnp.where(rows < vocab, (soft - hits) * scale, 0.0).astype(bf16)
-
-    @pl.when(pl.program_id(0) == 0)
-    def _():
-        acc_ref[...] = jnp.zeros_like(acc_ref)
-        pick_ref[...] = jnp.zeros_like(pick_ref)
-
-    pick_ref[...] += jnp.sum(hits * logits, axis=0, keepdims=True)
-    g_ref[0] = lax.dot_general(
-        grad, tab_ref[...], (((0,), (0,)), ((), ())), preferred_element_type=f32
-    ).astype(bf16)
-    acc_ref[...] += jnp.dot(grad, nf_ref[0], preferred_element_type=f32)
-
-
-def vocab_grads(normed, table_low, log_total, first, second, vocab, scale):
-    count, tokens, _ = normed.shape
-    padded = table_low.shape[0]
-    row = pl.BlockSpec((1, 1, tokens), lambda i: (i, 0, 0))
-    return pl.pallas_call(
-        functools.partial(vocab_kernel, vocab, scale),
-        grid=(count,),
         out_shape=(
-            jax.ShapeDtypeStruct((count, tokens, D), bf16),
-            jax.ShapeDtypeStruct((padded, D), f32),
+            row, row, jax.ShapeDtypeStruct((count, padded, tokens), bf16),
             jax.ShapeDtypeStruct((1, tokens), f32),
         ),
         in_specs=[
             pl.BlockSpec((1, tokens, D), lambda i: (i, 0, 0)),
             pl.BlockSpec((padded, D), lambda i: (0, 0)),
+            row_spec,
+            row_spec,
+        ],
+        out_specs=(
+            row_spec,
+            row_spec,
+            pl.BlockSpec((1, padded, tokens), lambda i: (i, 0, 0)),
+            pl.BlockSpec((1, tokens), lambda i: (0, 0)),
+        ),
+        name="vocab_stats",
+    )(normed, table_low, first[:, None, :], second[:, None, :])
+
+
+def vocab_kernel(scale, exp_ref, nf_ref, tab_ref, top_ref, lse_ref, t0_ref, t1_ref, g_ref, acc_ref):
+    rows = lax.broadcasted_iota(jnp.int32, exp_ref.shape[1:], 0)
+    hits = jnp.where(rows == t0_ref[0], scale, 0.0) + jnp.where(
+        rows == t1_ref[0], second_weight * scale, 0.0
+    )
+    weight = jnp.exp(top_ref[0] - lse_ref[0]) * ((1.0 + second_weight) * scale)
+    grad = (exp_ref[0].astype(f32) * weight - hits).astype(bf16)
+
+    @pl.when(pl.program_id(0) == 0)
+    def _():
+        acc_ref[...] = jnp.zeros_like(acc_ref)
+
+    g_ref[0] = lax.dot_general(
+        grad, tab_ref[...], (((0,), (0,)), ((), ())), preferred_element_type=f32
+    ).astype(bf16)
+    acc_ref[...] += jnp.dot(grad, nf_ref[0], preferred_element_type=f32)
+
+
+def vocab_grads(expo, normed, table_low, top, log_total, first, second, scale):
+    count, tokens, _ = normed.shape
+    padded = table_low.shape[0]
+    row = pl.BlockSpec((1, 1, tokens), lambda i: (i, 0, 0))
+    return pl.pallas_call(
+        functools.partial(vocab_kernel, scale),
+        grid=(count,),
+        out_shape=(
+            jax.ShapeDtypeStruct((count, tokens, D), bf16),
+            jax.ShapeDtypeStruct((padded, D), f32),
+        ),
+        in_specs=[
+            pl.BlockSpec((1, padded, tokens), lambda i: (i, 0, 0)),
+            pl.BlockSpec((1, tokens, D), lambda i: (i, 0, 0)),
+            pl.BlockSpec((padded, D), lambda i: (0, 0)),
+            row,
             row,
             row,
             row,
@@ -484,19 +631,25 @@
         out_specs=(
             pl.BlockSpec((1, tokens, D), lambda i: (i, 0, 0)),
             pl.BlockSpec((padded, D), lambda i: (0, 0)),
-            pl.BlockSpec((1, tokens), lambda i: (0, 0)),
         ),
         name="vocab_grads",
-    )(normed, table_low, log_total[:, None, :], first[:, None, :], second[:, None, :])
+    )(expo, normed, table_low, top, log_total[:, None, :], first[:, None, :], second[:, None, :])
+
+
+CORNER = (0, 3, 1, 2)
 
 
 def place_of(index, shard):
-    return (index % 2, index // (2 * shard), (index // 2) % shard)
-
-
-def my_place():
+    turn, group = index % 4, index // 4
+    side = ((turn + 1) // 2) % 2
+    return (turn // 2, group // (shard // 2), 2 * (group % (shard // 2)) + side)
+
+
+def my_block():
     shard = lax.axis_size("shard")
-    return (lax.axis_index("blk") * shard + lax.axis_index("shard")) * 2 + lax.axis_index("section")
+    section, h = lax.axis_index("section"), lax.axis_index("shard")
+    side = h % 2
+    return (lax.axis_index("blk") * (shard // 2) + h // 2) * 4 + side + section * (3 - 2 * side)
 
 
 def meet(reach, block, blocks, mine, shard, sign):
@@ -535,7 +688,7 @@
 def attend_kernel(reach, blocks, q_ref, k_ref, v_ref, seg_ref, tot_ref, acc_ref, kr_ref, vr_ref,
                   send_sem, recv_sem):
     shard = lax.axis_size("shard")
-    mine = (lax.axis_index("blk") * shard + lax.axis_index("shard")) * 2 + lax.axis_index("section")
+    mine = my_block()
     block = mine % blocks
     tokens = q_ref.shape[0]
     meet(reach, block, blocks, mine, shard, 1)
@@ -634,7 +787,7 @@
                        seg_ref, dq_ref, dk_ref, dv_ref, gw, gt, far_k, far_v, got_k, got_v,
                        send_sem, recv_sem):
     shard = lax.axis_size("shard")
-    mine = (lax.axis_index("blk") * shard + lax.axis_index("shard")) * 2 + lax.axis_index("section")
+    mine = my_block()
     block = mine % blocks
     tokens = q_ref.shape[0]
     meet(reach, block, blocks, mine, shard, -1)
@@ -1202,7 +1355,7 @@
 
 def share_ids(packed, cid):
     blk, shard = lax.axis_size("blk"), lax.axis_size("shard")
-    if blk * shard <= 16:
+    if kernels_fit():
         every = swap_all(packed, 2 * blk * shard, cid, name="swap_ids")
         return every.reshape(blk, shard, 2, *packed.shape)[:, :, 0]
     return lax.all_gather(packed, ("blk", "shard")).reshape(blk, shard, *packed.shape)
@@ -1211,7 +1364,7 @@
 def share_stats(top, total, cid):
     blk, shard = lax.axis_size("blk"), lax.axis_size("shard")
     devices = 2 * blk * shard
-    if blk * shard <= 16:
+    if kernels_fit():
         pair = jnp.concatenate([top, total], axis=1)
         return swap_all(pair, devices, cid, join_stats, 1, name="swap_stats")[:, 0]
     largest = lax.pmax(top[:, 0], ORDER)
@@ -1221,7 +1374,7 @@
 def share_sum(small, cid):
     blk, shard = lax.axis_size("blk"), lax.axis_size("shard")
     devices = 2 * blk * shard
-    if blk * shard <= 16:
+    if kernels_fit():
         lanes = pl.cdiv(small.size, devices * 128) * 128
         flat = jnp.pad(small.reshape(-1), (0, devices * lanes - small.size))
         every = swap_all(flat.reshape(devices, 1, lanes), devices, cid, join_sum, 1, name="swap_sum")
@@ -1245,7 +1398,8 @@
     padded = pl.cdiv(vocab, 128) * 128
     own_blocks = blocks.shape[1]
 
-    mine = my_place()
+    mine = my_block()
+    slot = (blk_index * shard + shard_index) * 2 + section
     seg_own = lax.dynamic_slice_in_dim(segments[:, 0, :], blk_index * tok_rows, tok_rows, axis=1)
     packed = jnp.stack(
         [ids[:, 0, :], targets[:, 0, :, 0], targets[:, 0, :, 1], seg_own], axis=0
@@ -1253,7 +1407,9 @@
     shared = share_ids(packed, 8).reshape(blk, shard, 4, micro, tok_rows)
     shared = shared.transpose(2, 3, 1, 0, 4).reshape(4, devices, tokens)
     first_row = ((section * blk + blk_index) * shard + shard_index) * vocab
-    local_ids, local_first, local_second = (shared[i] - first_row for i in range(3))
+    placed = jnp.stack([shared.reshape(4, devices // 4, 4, tokens)[:3, :, i] for i in CORNER], axis=2)
+    placed = placed.reshape(3, devices, tokens)
+    local_ids, local_first, local_second = (placed[i] - first_row for i in range(3))
 
     def mark(values):
         return jnp.where((values >= 0) & (values < vocab), values, -1)
@@ -1263,12 +1419,11 @@
     seg_rows = jnp.take(shared[3], seg_index, axis=0).astype(f32)[:, None, :]
 
     rows_low = blocks_to_rows(blocks[0].astype(bf16))
-    gathered = gather_all(rows_low, 0, by_section=True)
+    table_low = jnp.pad(table.astype(bf16), ((0, padded - vocab), (0, 0)))
+    gathered, looked = gather_and_lookup(rows_low, 0, local_ids, table_low)
     weights = jnp.stack([rows_to_quads(part, own_blocks) for part in gathered.reshape(
         2, blk * shard * rows_low.shape[0], QUAD)]) if own_blocks % 4 else gathered.reshape(
         2, QUADS, BS, QUAD)
-    table_low = jnp.pad(table.astype(bf16), ((0, padded - vocab), (0, 0)))
-    looked = lookup(local_ids, table_low)
     states = scatter_all(looked, 1).astype(f32)
 
     positions = (mine % seq_blocks) * tokens + jnp.arange(tokens, dtype=jnp.int32)
@@ -1286,13 +1441,15 @@
         )
         states = out
     normed = gather_all(normed_own, 3)
-    top, spread_sum = vocab_stats(normed, table_low, vocab)
+    top, spread_sum, expo, picks = vocab_stats(
+        normed, table_low, local_first, local_second, vocab
+    )
     log_total = share_stats(top, spread_sum, 4)
     inv_count = 1.0 / all_tokens
-    grad_rows, head_term, picks = vocab_grads(
-        normed, table_low, log_total, local_first, local_second, vocab, inv_count
-    )
-    own_log = lax.dynamic_index_in_dim(log_total, mine, 0, keepdims=False)
+    grad_rows, head_term = vocab_grads(
+        expo, normed, table_low, top, log_total, local_first, local_second, inv_count
+    )
+    own_log = lax.dynamic_index_in_dim(log_total, slot, 0, keepdims=False)
     loss_part = (1.0 + second_weight) * jnp.sum(own_log) - jnp.sum(picks)
     grad = scatter_all(grad_rows, 1)
     gain_grads = [None] * 5
@@ -1314,9 +1471,9 @@
     if own_blocks % 4:
         sends = jnp.stack([quads_to_rows(store[l], own_blocks) for l in range(2)])
     sends = sends.reshape(devices, rows_low.shape[0], QUAD)
-    block_rows = scatter_all(sends, 6, by_section=True)
     grad_embed = gather_all(grad_low, 3)
-    table_own = spread(local_ids, grad_embed, head_term)[:vocab]
+    block_rows, table_own = scatter_and_spread(sends, 6, local_ids, grad_embed, head_term)
+    table_own = table_own[:vocab]
     square_rows = block_rows.astype(f32)
     square_sum = jnp.sum(table_own * table_own) + jnp.sum(square_rows * square_rows)
     small = jnp.concatenate(

time: 1090 us -> 987 us (0.906)
  Pallas kernels: 989 us -> 889 us
    pallas_call x9 -> x7, Pallas kernels: 667 us -> 573 us  [the longest x3 281 us: reduce_scatter32(): pl.pallas_call(functools.partial(rs_kernel, B, H, parts, by_section, side...]
    pallas_call x2, Pallas kernels: 61.5 us -> 48.4 us  [attend(): pl.pallas_call(functools.partial(attend_kernel, reach, blocks), out_shape...]
    pallas_call x1, Pallas kernels: 31.6 us -> 43 us  [vocab_stats(): pl.pallas_call(functools.partial(stats_kernel, vocab), grid=(count,), out...]
    unnamed x44 -> x43, local copies, waits for them, and re-layouts: 38.8 us -> 38.2 us
where the time goes in v3:
time: 987 us; the launch traced here: 977 us
  Pallas kernels  889 us (90%)
  local copies, waits for them, and re-layouts  53 us (5%)
  other arithmetic  26.6 us (3%)
    pallas_call x3, Pallas kernels, reduce_scatter32(): pl.pallas_call(functools.partial(rs_kernel, B, H, parts, by_section, side...  281 us
    pallas_call x3, Pallas kernels, all_gather32(): pl.pallas_call(functools.partial(ag_kernel, B, H, parts, by_section, side...  234 us
    pallas_call x2, Pallas kernels, attend_back(): pl.pallas_call(functools.partial(attend_back_kernel, reach, blocks), out_...  60.1 us
    pallas_call x1, Pallas kernels, vocab_grads(): pl.pallas_call(functools.partial(vocab_kernel, scale), grid=(count,), out...  57.6 us
    pallas_call x2, Pallas kernels, attend(): pl.pallas_call(functools.partial(attend_kernel, reach, blocks), out_shape...  48.4 us
    pallas_call x3, Pallas kernels, swap_all(): pl.pallas_call(functools.partial(swap_kernel, n, join), out_shape=jax.Sha...  46.1 us
    pallas_call x1, Pallas kernels, vocab_stats(): pl.pallas_call(functools.partial(stats_kernel, vocab), grid=(count,), out...  43 us
    pallas_call x2, Pallas kernels, mlp_backward(): pl.pallas_call(functools.partial(mlp_back_kernel, layer, last, store is N...  38.5 us

profile of v3, /device:TPU:0, one launch (start us, length us, event | category | flops | bytes accessed | tf_op | source)
XLA Modules:
  0.0 977.0 jit_solution(3510423285440706705)
XLA Ops:
  0.7 4.4 copy.59
  12.9 14.3 %swap_ids.1 = s32[32,8,256]{2,1,0:T(8,128)} custom-call(s32[8,256]{1,0:T(8,128)} %reshape.206.x_ref), custom_call_target="tpu_custom_call" | custom-call | tf_op jit(solution)/shard_map/swap_ids/pallas_call | solution.py:356
  32.4 118.4 %gather_1728_0.1 = (bf16[32,1728,256]{2,1,0:T(8,128)(2,1)}, bf16[32,256,768]{2,1,0:T(8,128)(2,1)}) custom-call(bf16[1728,256]{1,0:T(8,128)(2,1)} %reshape.205.refs_0_, s32[32,1,256]{2,1,0:T(1,128)} %and_select_fusion.2.refs_1_, bf16[1024,768]{1,0:T(8,128)(2,1)} %pad.8.refs_2_.tab_ref), custom_call_target="tpu_custom_call" | custom-call | tf_op jit(solution)/shard_map/gather_1728_0/pallas_call | solution.py:151
  150.8 69.2 %scatter_256_1.2 = bf16[256,768]{1,0:T(8,128)(2,1)} custom-call(bf16[32,256,768]{2,1,0:T(8,128)(2,1)} %get-tuple-element.79.refs_0_), custom_call_target="tpu_custom_call" | custom-call | tf_op jit(solution)/shard_map/scatter_256_1/pallas_call | solution.py:303
  225.1 7.5 qkv.2
  233.9 21.5 %attend.2 = (f32[256,768]{1,0:T(8,128)}, f32[256,768]{1,0:T(8,128)}, bf16[2,256,768]{2,1,0:T(8,128)(2,1)}, bf16[2,256,768]{2,1,0:T(8,128)(2,1)}) custom-call(bf16[256,768]{1,0:T(8,128)(2,1)} %get-tuple-element.81.q_ref, bf16[256,768]{1,0:T(8,128)(2,1)} %get-tuple-element.82.k_ref, bf16[256,768]{1,0:T(8,128)(2,1)} %get-tuple-element.83.v_ref, ...), custom_call_target="tpu_custom_call" | custom-call | tf_op jit(solution)/shard_map/attend/pallas_call | solution.py:770
  255.4 12.1 %mlp.2 = (f32[256,768]{1,0:T(8,128)}, bf16[256,768]{1,0:T(8,128)(2,1)}, f32[256,768]{1,0:T(8,128)}, bf16[256,768]{1,0:T(8,128)(2,1)}, f32[256,2048]{1,0:T(8,128)...) custom-call(f32[256,768]{1,0:T(8,128)} %convert_element_type.43.x_ref, ...), custom_call_target="tpu_custom_call" | custom-call | tf_op jit(solution)/shard_map/mlp/pallas_call | solution.py:1098
  267.5 7.5 qkv.3
  275.1 26.8 %attend.3 = (f32[256,768]{1,0:T(8,128)}, f32[256,768]{1,0:T(8,128)}, bf16[2,256,768]{2,1,0:T(8,128)(2,1)}, bf16[2,256,768]{2,1,0:T(8,128)(2,1)}) custom-call(bf16[256,768]{1,0:T(8,128)(2,1)} %get-tuple-element.89.q_ref, bf16[256,768]{1,0:T(8,128)(2,1)} %get-tuple-element.90.k_ref, bf16[256,768]{1,0:T(8,128)(2,1)} %get-tuple-element.91.v_ref, ...), custom_call_target="tpu_custom_call" | custom-call | tf_op jit(solution)/shard_map/attend/pallas_call | solution.py:770
  301.9 12.1 %mlp.3 = (f32[256,768]{1,0:T(8,128)}, bf16[256,768]{1,0:T(8,128)(2,1)}, f32[256,768]{1,0:T(8,128)}, bf16[256,768]{1,0:T(8,128)(2,1)}, f32[256,2048]{1,0:T(8,128)...) custom-call(f32[256,768]{1,0:T(8,128)} %get-tuple-element.88.x_ref, ...), custom_call_target="tpu_custom_call" | custom-call | tf_op jit(solution)/shard_map/mlp/pallas_call | solution.py:1098
  314.0 60.8 %gather_256_3.2.nf_ref = bf16[32,256,768]{2,1,0:T(8,128)(2,1)} custom-call(bf16[256,768]{1,0:T(8,128)(2,1)} %get-tuple-element.96.refs_0_), custom_call_target="tpu_custom_call" | custom-call | tf_op jit(solution)/shard_map/gather_256_3/pallas_call | solution.py:151
  375.6 43.0 %vocab_stats.1 = (f32[32,1,256]{2,1,0:T(1,128)}, f32[32,1,256]{2,1,0:T(1,128)}, bf16[32,1024,256]{2,1,0:T(8,128)(2,1)}, f32[1,256]{1,0:T(1,128)}) custom-call(bf16[32,256,768]{2,1,0:T(8,128)(2,1)} %gather_256_3.2.nf_ref, bf16[1024,768]{1,0:T(8,128)(2,1)} %pad.8.refs_2_.tab_ref, s32[32,1,256]{2,1,0:T(1,128)} %get-tuple-element.209.t0_ref, ...), custom_call_target="tpu_custom_call" | custom-call | tf_op jit(solution)/shard_map/vocab_stats/pallas_call | solution.py:570
  420.0 18.1 %swap_stats.1.lse_ref = f32[32,1,256]{2,1,0:T(1,128)} custom-call(f32[32,2,256]{2,1,0:T(2,128)} %pad_maximum_fusion.x_ref), custom_call_target="tpu_custom_call" | custom-call | tf_op jit(solution)/shard_map/swap_stats/pallas_call | solution.py:356
  438.1 57.6 %vocab_grads.1 = (bf16[32,256,768]{2,1,0:T(8,128)(2,1)}, f32[1024,768]{1,0:T(8,128)}) custom-call(bf16[32,1024,256]{2,1,0:T(8,128)(2,1)} %get-tuple-element.97.exp_ref, bf16[32,256,768]{2,1,0:T(8,128)(2,1)} %gather_256_3.2.nf_ref, bf16[1024,768]{1,0:T(8,128)(2,1)} %pad.8.refs_2_.tab_ref, f32[32,1,256]{2,1,0:T(1,128)} %get-tuple-element.98.top_ref, ...), custom_call_target="tpu_custom_call" | custom-call | tf_op jit(solution)/shard_map/vocab_grads/pallas_call | solution.py:615
  495.7 67.0 %scatter_256_1.3.refs_0_ = bf16[256,768]{1,0:T(8,128)(2,1)} custom-call(bf16[32,256,768]{2,1,0:T(8,128)(2,1)} %get-tuple-element.100.refs_0_), custom_call_target="tpu_custom_call" | custom-call | tf_op jit(solution)/shard_map/scatter_256_1/pallas_call | solution.py:303
  562.7 19.2 %mlp_back.2 = (bf16[2,432,64,256]{3,2,1,0:T(8,128)(2,1)}, f32[256,768]{1,0:T(8,128)}, f32[256,768]{1,0:T(8,128)}, f32[1,768]{1,0:T(1,128)}, f32[1,768]{1,0:T(1,128)}) custom-call(bf16[256,768]{1,0:T(8,128)(2,1)} %scatter_256_1.3.refs_0_, f32[256,768]{1,0:T(8,128)} %get-tuple-element.101.refs_1_, f32[256,768]{1,0:T(8,128)} %get-tuple-element.102.refs_2_, ...), custom_call_target="tpu_custom_call" | custom-call | tf_op jit(solution)/shard_map/mlp_back/pallas_call | solution.py:1203
  581.9 30.1 %attend_back.2 = (f32[256,768]{1,0:T(8,128)}, f32[256,768]{1,0:T(8,128)}, f32[256,768]{1,0:T(8,128)}) custom-call(bf16[256,768]{1,0:T(8,128)(2,1)} %get-tuple-element.89.q_ref, bf16[256,768]{1,0:T(8,128)(2,1)} %get-tuple-element.90.k_ref, bf16[256,768]{1,0:T(8,128)(2,1)} %get-tuple-element.91.v_ref, bf16[2,256,768]{2,1,0:T(8,128)(2,1)} %get-tuple-element.92.kr_ref, ...), custom_call_target="tpu_custom_call" | custom-call | tf_op jit(solution)/shard_map/attend_back/pallas_call | solution.py:891
  612.0 11.7 %qkv_back.2 = (bf16[2,432,64,256]{3,2,1,0:T(8,128)(2,1)}, f32[256,768]{1,0:T(8,128)}, bf16[256,768]{1,0:T(8,128)(2,1)}, f32[1,768]{1,0:T(1,128)}) custom-call(f32[256,768]{1,0:T(8,128)} %get-tuple-element.109.dq_ref, f32[256,768]{1,0:T(8,128)} %get-tuple-element.110.dk_ref, f32[256,768]{1,0:T(8,128)} %get-tuple-element.111.dv_ref, ...), custom_call_target="tpu_custom_call", output_to_operand_aliasing={{0}: (10, {})} | custom-call | tf_op jit(solution)/shard_map/qkv_back/pallas_call | solution.py:1254
  623.6 19.3 %mlp_back.3 = (bf16[2,432,64,256]{3,2,1,0:T(8,128)(2,1)}, f32[256,768]{1,0:T(8,128)}, f32[256,768]{1,0:T(8,128)}, f32[1,768]{1,0:T(1,128)}, f32[1,768]{1,0:T(1,128)}) custom-call(f32[256,768]{1,0:T(8,128)} %get-tuple-element.115.refs_0_, f32[256,768]{1,0:T(8,128)} %get-tuple-element.101.refs_1_, ...), custom_call_target="tpu_custom_call", output_to_operand_aliasing={{0}: (11, {})} | custom-call | tf_op jit(solution)/shard_map/mlp_back/pallas_call | solution.py:1203
  643.0 30.1 %attend_back.3 = (f32[256,768]{1,0:T(8,128)}, f32[256,768]{1,0:T(8,128)}, f32[256,768]{1,0:T(8,128)}) custom-call(bf16[256,768]{1,0:T(8,128)(2,1)} %get-tuple-element.81.q_ref, bf16[256,768]{1,0:T(8,128)(2,1)} %get-tuple-element.82.k_ref, bf16[256,768]{1,0:T(8,128)(2,1)} %get-tuple-element.83.v_ref, bf16[2,256,768]{2,1,0:T(8,128)(2,1)} %get-tuple-element.84.kr_ref, ...), custom_call_target="tpu_custom_call" | custom-call | tf_op jit(solution)/shard_map/attend_back/pallas_call | solution.py:891
  673.1 11.7 %qkv_back.3 = (bf16[2,432,64,256]{3,2,1,0:T(8,128)(2,1)}, f32[256,768]{1,0:T(8,128)}, bf16[256,768]{1,0:T(8,128)(2,1)}, f32[1,768]{1,0:T(1,128)}) custom-call(f32[256,768]{1,0:T(8,128)} %get-tuple-element.124.dq_ref, f32[256,768]{1,0:T(8,128)} %get-tuple-element.125.dk_ref, f32[256,768]{1,0:T(8,128)} %get-tuple-element.126.dv_ref, ...), custom_call_target="tpu_custom_call", output_to_operand_aliasing={{0}: (10, {})} | custom-call | tf_op jit(solution)/shard_map/qkv_back/pallas_call | solution.py:1254
  684.8 55.2 %gather_256_3.3.refs_2_ = bf16[32,256,768]{2,1,0:T(8,128)(2,1)} custom-call(bf16[256,768]{1,0:T(8,128)(2,1)} %get-tuple-element.136.refs_0_), custom_call_target="tpu_custom_call" | custom-call | tf_op jit(solution)/shard_map/gather_256_3/pallas_call | solution.py:151
  740.0 145.1 %scatter_1728_6.1 = (bf16[1728,256]{1,0:T(8,128)(2,1)}, f32[1024,768]{1,0:T(8,128)}) custom-call(bf16[32,1728,256]{2,1,0:T(8,128)(2,1)} %bitcast.49, s32[32,1,256]{2,1,0:T(1,128)} %and_select_fusion.2.refs_1_, bf16[32,256,768]{2,1,0:T(8,128)(2,1)} %gather_256_3.3.refs_2_, f32[1024,768]{1,0:T(8,128)} %get-tuple-element.137.refs_3_), custom_call_target="tpu_custom_call" | custom-call | tf_op jit(solution)/shard_map/scatter_1728_6/pallas_call | solution.py:303
  896.1 13.7 %swap_sum.1 = f32[32,1,256]{2,1,0:T(1,128)} custom-call(f32[32,1,256]{2,1,0:T(1,128)} %bitcast.66), custom_call_target="tpu_custom_call" | custom-call | tf_op jit(solution)/shard_map/swap_sum/pallas_call | solution.py:356
  914.6 7.0 fusion.6
  921.6 5.2 copy.67
  926.8 4.0 copy.68
  930.8 5.3 copy.69
  936.1 4.1 copy.70
  940.2 16.9 %shampoo.1 = (f32[108,64,64]{2,1,0:T(8,128)}, bf16[108,64,64]{2,1,0:T(8,128)(2,1)}, f32[108,64,64]{2,1,0:T(8,128)}, f32[108,64,64]{2,1,0:T(8,128)}) custom-call(f32[1,1]{1,0:T(1,128)} %bitcast.20.scale_ref, bf16[27,64,256]{2,1,0:T(8,128)(2,1)} %bitcast.59, f32[108,64,64]{2,1,0:T(8,128)} %bitcast.50, f32[108,64,64]{2,1,0:T(8,128)} %bitcast.51, ...), custom_call_target="tpu_custom_call" | custom-call | tf_op jit(solution)/shard_map/shampoo/pallas_call | solution.py:1309
  957.1 4.6 copy.71
  964.4 4.6 copy.73
  (86 shorter events, 40.4 us)
Async XLA Ops:
  0.6 11.6 %copy-start = (s32[2,1,1024]{2,1,0:T(1,128)S(1)}, s32[2,1,1024]{2,1,0:T(1,128)}, u32[]{:S(2)}) copy-start(s32[2,1,1024]{2,1,0:T(1,128)} %param.16) | copy-start | bytes 24580
  5.1 3.3 copy-start.2
  5.5 6.7 copy-start.9
  5.5 6.7 copy-start.15
  150.8 71.1 %copy-start.8 = (f32[5,768]{1,0:T(8,128)S(1)}, f32[5,768]{1,0:T(8,128)}, u32[]{:S(2)}) copy-start(f32[5,768]{1,0:T(8,128)} %param.25) | copy-start | bytes 46084
  885.1 9.0 copy-start.16
  885.1 10.2 %copy-start.10 = (f32[1,768]{1,0:T(1,128)S(1)}, f32[1,768]{1,0:T(1,128)}, u32[]{:S(2)}) copy-start(f32[1,768]{1,0:T(1,128)} %get-tuple-element.133) | copy-start | bytes 9220
  885.1 10.2 %copy-start.11 = (f32[1,768]{1,0:T(1,128)S(1)}, f32[1,768]{1,0:T(1,128)}, u32[]{:S(2)}) copy-start(f32[1,768]{1,0:T(1,128)} %get-tuple-element.134) | copy-start | bytes 9220
  885.1 10.2 %copy-start.12 = (f32[1,768]{1,0:T(1,128)S(1)}, f32[1,768]{1,0:T(1,128)}, u32[]{:S(2)}) copy-start(f32[1,768]{1,0:T(1,128)} %get-tuple-element.132) | copy-start | bytes 9220
  885.2 10.2 %copy-start.13 = (f32[1,768]{1,0:T(1,128)S(1)}, f32[1,768]{1,0:T(1,128)}, u32[]{:S(2)}) copy-start(f32[1,768]{1,0:T(1,128)} %get-tuple-element.131) | copy-start | bytes 9220
  885.2 10.2 %copy-start.14 = (f32[1,768]{1,0:T(1,128)S(1)}, f32[1,768]{1,0:T(1,128)}, u32[]{:S(2)}) copy-start(f32[1,768]{1,0:T(1,128)} %get-tuple-element.130) | copy-start | bytes 9220
  885.2 29.4 %copy-start.3 = (f32[1000,768]{1,0:T(8,128)S(1)}, f32[1000,768]{1,0:T(8,128)}, u32[]{:S(2)}) copy-start(f32[1000,768]{1,0:T(8,128)} %param.17) | copy-start | bytes 9216004
  921.6 5.2 copy-start.5
  930.8 5.3 copy-start.6
  957.1 4.6 copy-start.7
  964.4 4.6 copy-start.4
  964.4 9.9 %copy-start.1 = (s32[2,1,1024]{2,1,0:T(1,128)S(1)}, s32[2,1,1024]{2,1,0:T(1,128)}, u32[]{:S(2)}) copy-start(s32[2,1,1024]{2,1,0:T(1,128)} %param.16) | copy-start | bytes 24580
